TPU v7x, 128 devices: a whole 4x4x4 slice. The times are simulated.
128 devices in a mesh: expert: 32 (over z, y, core), dp: 4 (over x).
Axes of the slice: x: 4, y: 4, z: 4, core: 2. Of those that a mesh axis runs over, the one named last changes fastest.
Arguments:
- tokens: bfloat16 [2, 8192, 1024], P(None, ('expert', 'dp')), may hold values from -6 to 6
- routes: int32 [2, 8192, 6], P(None, ('expert', 'dp')), may hold values from 0 to 31, all different within a row; in each aligned block of 64 rows (0 to 63, 64 to 127, ..., all dimensions but the last counted through in order) at most 16 rows name the same one
- gate_weights: float32 [2, 8192, 6], P(None, ('expert', 'dp')), may hold values from 0.05 to 0.35
- cotangent: bfloat16 [2, 8192, 1024], P(None, ('expert', 'dp')), may hold values from -6 to 6
- expert_plan: int32 [32], replicated, may hold values from 0 to 31, each once
- weight_in: bfloat16 [32, 1024, 1536], P('expert', 'dp'), may hold values from -0.1875 to 0.1875
- weight_out: bfloat16 [32, 768, 1024], P('expert', 'dp'), may hold values from -0.21875 to 0.21875
- first_in: float32 [32, 1024, 1536], P('expert', 'dp'), may hold values from -6 to 6
- second_in: float32 [32, 1024, 1536], P('expert', 'dp'), may hold values from 0.5 to 20
- first_out: float32 [32, 768, 1024], P('expert', 'dp'), may hold values from -6 to 6
- second_out: float32 [32, 768, 1024], P('expert', 'dp'), may hold values from 0.5 to 20
Outputs:
- layer_output: bfloat16 [2, 8192, 1024], P(None, ('expert', 'dp'))
- token_gradient: bfloat16 [2, 8192, 1024], P(None, ('expert', 'dp'))
- weight_in_next: bfloat16 [32, 1024, 1536], P('expert', 'dp')
- weight_out_next: bfloat16 [32, 768, 1024], P('expert', 'dp')
- first_in_next: float32 [32, 1024, 1536], P('expert', 'dp')
- second_in_next: float32 [32, 1024, 1536], P('expert', 'dp')
- first_out_next: float32 [32, 768, 1024], P('expert', 'dp')
- second_out_next: float32 [32, 768, 1024], P('expert', 'dp')
Inputs may be any that keep to these rules, and one draw needn't show every extreme that they name: `routes`: each row names 6 different experts. In the 64 rows of one device in one micro-batch (an aligned block), no expert is named by more than 16 rows; in some blocks one expert is named by exactly 16 rows. A permutation. Before the migration, index d of the expert axis holds expert d; after it, expert expert_plan[d].
All inputs are finite; a program needn't handle non-finite values.
Results may differ from a plain program's by a relative error of at most 0.014.
Values may be sent and summed in bfloat16 or wider, within the bound.
No kernel may reach another device: no remote copies, remote signals or barrier semaphores. Data moves between devices by JAX's collectives and lax.ppermute only.
A program may use at most 128 MiB of HBM per device.

v0:
```python
import jax
import jax.numpy as jnp
from jax import lax
from jax.sharding import PartitionSpec as P

beta_one = 0.9
beta_two = 0.95
learn_rate = 0.00042
decay_rate = 0.1
epsilon = 1e-08
steps_done = 10


def side_by_side(arrays, axis, split_dim, concat_dim, along):
    ends, at = ([], 0)
    for a in arrays[:-1]:
        at += a.shape[along]
        ends.append(at)
    both = jnp.concatenate(arrays, axis=along)
    return tuple(
        jnp.split(
            lax.all_to_all(both, axis, split_axis=split_dim, concat_axis=concat_dim, tiled=True),
            ends,
            axis=along,
        )
    )


def as_sent(x):
    return jax.tree.map(lambda a: a.astype(jnp.bfloat16) if a.dtype == jnp.float32 else a, x)


def joined_along(parts, dim):
    parts = jnp.moveaxis(parts, 0, dim)
    lengths = parts.shape
    return parts.reshape(*lengths[:dim], lengths[dim] * lengths[dim + 1], *lengths[dim + 2 :])


def gather_packed(arrays, axis, dims):
    flat = jnp.concatenate([a.reshape(-1) for a in arrays])
    lines, at, done = (lax.all_gather(flat, axis), 0, [])
    for a, dim in zip(arrays, dims):
        parts = lines[:, at : at + a.size].reshape(-1, *a.shape)
        done.append(joined_along(parts, dim))
        at += a.size
    return tuple(done)


def adam_update(weight, gradient, first, second):
    first_new = beta_one * first + (1.0 - beta_one) * gradient
    second_new = beta_two * second + (1.0 - beta_two) * gradient * gradient
    ratio = (
        first_new
        / (1.0 - beta_one**steps_done)
        / (jnp.sqrt(second_new / (1.0 - beta_two**steps_done)) + epsilon)
    )
    master = weight.astype(jnp.float32)
    return (
        (master - learn_rate * (ratio + decay_rate * master)).astype(jnp.bfloat16),
        first_new,
        second_new,
    )


def relocate_weights(pair, expert_plan):
    count = expert_plan.shape[0]
    spread = side_by_side(
        (pair[0].reshape(count, -1), pair[1].reshape(count, -1)), "expert", 0, 0, 1
    )
    picked_first = jnp.take(spread[0], expert_plan, axis=0)
    picked_second = jnp.take(spread[1], expert_plan, axis=0)
    landed = side_by_side((picked_first, picked_second), "expert", 0, 0, 1)
    return (landed[0].reshape(pair[0].shape), landed[1].reshape(pair[1].shape))


def relocate_moments(group, expert_plan):
    count = expert_plan.shape[0]
    spread = tuple(
        (
            part.astype(jnp.float32)
            for part in side_by_side(
                (
                    group[0].reshape(count, -1).astype(jnp.bfloat16),
                    group[1].reshape(count, -1).astype(jnp.bfloat16),
                    group[2].reshape(count, -1).astype(jnp.bfloat16),
                    group[3].reshape(count, -1).astype(jnp.bfloat16),
                ),
                "expert",
                0,
                0,
                1,
            )
        )
    )
    picked = [jnp.take(member, expert_plan, axis=0) for member in spread]
    landed = (
        lax.all_to_all(as_sent(picked[0]), "expert", split_axis=0, concat_axis=0, tiled=True),
        lax.all_to_all(as_sent(picked[1]), "expert", split_axis=0, concat_axis=0, tiled=True),
        lax.all_to_all(as_sent(picked[2]), "expert", split_axis=0, concat_axis=0, tiled=True),
        lax.all_to_all(as_sent(picked[3]), "expert", split_axis=0, concat_axis=0, tiled=True),
    )
    return tuple((landed[place].reshape(group[place].shape) for place in range(4)))


def slot_layout(chosen, holders, capacity):
    count = holders.shape[0]
    hits = (chosen[:, :, None] == holders[None, None, :]).astype(jnp.int32)
    per_token = jnp.sum(hits, axis=1)
    before = jnp.cumsum(per_token, axis=0) - per_token
    ranks = jnp.sum(hits * before[:, None, :], axis=2)
    owners = jnp.sum(hits * jnp.arange(count, dtype=jnp.int32)[None, None, :], axis=2)
    return owners * capacity + ranks


def expert_forward(rows, weight_first, weight_second):
    hidden_width = weight_second.shape[0]
    pre = jnp.dot(rows, weight_first, preferred_element_type=jnp.float32)
    gate_part = pre[:, :hidden_width]
    up_part = pre[:, hidden_width:]
    sigma = jax.nn.sigmoid(gate_part)
    hidden = (gate_part * sigma * up_part).astype(jnp.bfloat16)
    output = jnp.dot(hidden, weight_second, preferred_element_type=jnp.float32).astype(jnp.bfloat16)
    return (output, gate_part, up_part, sigma, hidden)


def on_device(
    tokens,
    routes,
    gate_weights,
    cotangent,
    expert_plan,
    weight_in,
    weight_out,
    first_in,
    second_in,
    first_out,
    second_out,
):
    count = lax.axis_size("expert")
    micro_count = tokens.shape[0]
    token_count = tokens.shape[1]
    width = tokens.shape[2]
    top_count = routes.shape[2]
    capacity = token_count * top_count * 4 // (3 * count)
    total_slots = count * capacity
    weight_in, weight_out = relocate_weights((weight_in, weight_out), expert_plan)
    first_in, second_in, first_out, second_out = relocate_moments(
        (first_in, second_in, first_out, second_out), expert_plan
    )
    whole_in, whole_out = gather_packed((weight_in[0], weight_out[0]), "dp", (0, 0))
    hidden_width = whole_out.shape[0]
    grad_in = jnp.zeros((width, 2 * hidden_width), jnp.float32)
    grad_out = jnp.zeros((hidden_width, width), jnp.float32)
    blank = jnp.zeros((1, width), jnp.bfloat16)
    layer_parts = []
    token_parts = []
    for micro in range(micro_count):
        slots = slot_layout(routes[micro], expert_plan, capacity)
        flat_slots = slots.reshape(-1)
        marks = (flat_slots[:, None] == jnp.arange(total_slots, dtype=jnp.int32)[None, :]).astype(
            jnp.int32
        )
        pair_ids = jnp.arange(flat_slots.shape[0], dtype=jnp.int32) + 1
        anchor = jnp.sum(marks * pair_ids[:, None], axis=0)
        token_anchor = jnp.where(anchor > 0, (anchor - 1) // top_count + 1, 0)
        outgoing = jnp.take(jnp.concatenate([blank, tokens[micro]], axis=0), token_anchor, axis=0)
        arrived = lax.all_to_all(
            outgoing.reshape(count, capacity, width),
            "expert",
            split_axis=0,
            concat_axis=0,
            tiled=True,
        ).reshape(total_slots, width)
        output, gate_part, up_part, sigma, hidden = expert_forward(arrived, whole_in, whole_out)
        returned = lax.all_to_all(
            output.reshape(count, capacity, width),
            "expert",
            split_axis=0,
            concat_axis=0,
            tiled=True,
        ).reshape(total_slots, width)
        picked = jnp.take(returned, flat_slots, axis=0).reshape(token_count, top_count, width)
        gates = gate_weights[micro]
        layer_parts.append(
            jnp.sum(gates[:, :, None] * picked.astype(jnp.float32), axis=1).astype(jnp.bfloat16)
        )
        scaled = (gates[:, :, None] * cotangent[micro][:, None, :].astype(jnp.float32)).astype(
            jnp.bfloat16
        )
        outgoing_grad = jnp.take(
            jnp.concatenate([blank, scaled.reshape(-1, width)], axis=0), anchor, axis=0
        )
        arrived_grad = lax.all_to_all(
            outgoing_grad.reshape(count, capacity, width),
            "expert",
            split_axis=0,
            concat_axis=0,
            tiled=True,
        ).reshape(total_slots, width)
        hidden_grad = lax.dot_general(
            arrived_grad, whole_out, (((1,), (1,)), ((), ())), preferred_element_type=jnp.float32
        )
        pre_grad = jnp.concatenate(
            [
                hidden_grad * up_part * sigma * (1.0 + gate_part * (1.0 - sigma)),
                hidden_grad * gate_part * sigma,
            ],
            axis=1,
        ).astype(jnp.bfloat16)
        grad_in = grad_in + lax.dot_general(
            arrived, pre_grad, (((0,), (0,)), ((), ())), preferred_element_type=jnp.float32
        )
        grad_out = grad_out + lax.dot_general(
            hidden, arrived_grad, (((0,), (0,)), ((), ())), preferred_element_type=jnp.float32
        )
        token_part = lax.dot_general(
            pre_grad, whole_in, (((1,), (1,)), ((), ())), preferred_element_type=jnp.float32
        ).astype(jnp.bfloat16)
        returned_grad = lax.all_to_all(
            token_part.reshape(count, capacity, width),
            "expert",
            split_axis=0,
            concat_axis=0,
            tiled=True,
        ).reshape(total_slots, width)
        picked_grad = jnp.take(returned_grad, flat_slots, axis=0).reshape(
            token_count, top_count, width
        )
        token_parts.append(jnp.sum(picked_grad.astype(jnp.float32), axis=1).astype(jnp.bfloat16))
    rows_in = weight_in.shape[1]
    rows_out = weight_out.shape[1]
    summed = (
        lax.psum(grad_in.astype(jnp.bfloat16), "dp").astype(jnp.float32),
        lax.psum(grad_out.astype(jnp.bfloat16), "dp").astype(jnp.float32),
    )
    replica = lax.axis_index("dp")
    share_in = lax.dynamic_slice_in_dim(summed[0], replica * rows_in, rows_in, 0)
    share_out = lax.dynamic_slice_in_dim(summed[1], replica * rows_out, rows_out, 0)
    new_in, first_in_new, second_in_new = adam_update(
        weight_in, share_in[None], first_in, second_in
    )
    new_out, first_out_new, second_out_new = adam_update(
        weight_out, share_out[None], first_out, second_out
    )
    return (
        jnp.stack(layer_parts, axis=0),
        jnp.stack(token_parts, axis=0),
        new_in,
        new_out,
        first_in_new,
        second_in_new,
        first_out_new,
        second_out_new,
    )


def solution(mesh):
    placed = (
        P(None, ("expert", "dp"), None),
        P(None, ("expert", "dp"), None),
        P(None, ("expert", "dp"), None),
        P(None, ("expert", "dp"), None),
        P(),
        P("expert", "dp", None),
        P("expert", "dp", None),
        P("expert", "dp", None),
        P("expert", "dp", None),
        P("expert", "dp", None),
        P("expert", "dp", None),
    )
    return jax.shard_map(
        on_device,
        mesh=mesh,
        in_specs=placed,
        out_specs=(
            P(None, ("expert", "dp"), None),
            P(None, ("expert", "dp"), None),
            P("expert", "dp", None),
            P("expert", "dp", None),
            P("expert", "dp", None),
            P("expert", "dp", None),
            P("expert", "dp", None),
            P("expert", "dp", None),
        ),
        check_vma=False,
    )
```

profile of v0, /device:TPU:1, one launch (start us, length us, event | category | flops | bytes accessed | tf_op | source)
XLA Modules:
  0.0 466.1 jit_solution(17562823960519675966)
XLA Ops:
  13.8 9.7 %all-to-all-start.1 = ((bf16[32,2,9216]{2,1,0:T(2,128)(2,1)}), bf16[32,2,9216]{2,1,0:T(2,128)(2,1)S(1)}, u32[]{:S(2)}, u32[]{:S(2)}) async-start(bf16[32,2,9216]{2,1,0:T(2,128)(2,1)} %reshape.496), calls=%async_computation.1 | async-start | bytes 2359296 | tf_op jit(solution)/shard_map/all_to_all | solution.py:22
  31.8 3.1 reduce.10
  34.9 4.7 %reshape.500 = bf16[32,2,18432]{2,1,0:T(2,128)(2,1)} reshape(bf16[32,36864]{1,0:T(8,128)(2,1)} %reduce.10) | data formatting | bytes 4718592
  39.6 2.4 all-to-all-done.1
  43.0 5.0 %all-to-all-start.10 = ((bf16[32,2,18432]{2,1,0:T(2,128)(2,1)}), bf16[32,2,18432]{2,1,0:T(2,128)(2,1)S(1)}, u32[]{:S(2)}, u32[]{:S(2)}) async-start(bf16[32,2,18432]{2,1,0:T(2,128)(2,1)} %reshape.500), calls=%async_computation.10 | async-start | bytes 4718592 | tf_op jit(solution)/shard_map/all_to_all | solution.py:22
  48.3 5.8 %reshape.497 = bf16[32,1,18432]{2,1,0:T(2,128)(2,1)} reshape(bf16[32,2,9216]{2,1,0:T(2,128)(2,1)} %copy-done.4) | data formatting | bytes 2359296
  60.0 19.5 %all-to-all-done.10 = bf16[32,2,18432]{2,1,0:T(2,128)(2,1)S(1)} async-done(((bf16[32,2,18432]{2,1,0:T(2,128)(2,1)}), bf16[32,2,18432]{2,1,0:T(2,128)(2,1)S(1)}, u32[]{:S(2)}, u32[]{:S(2)}) %all-to-all-start.10) | async-done | bytes 2359328 | tf_op jit(solution)/shard_map/all_to_all | solution.py:22
  79.5 7.0 %reshape.501 = bf16[32,1,36864]{2,1,0:T(2,128)(2,1)} reshape(bf16[32,2,18432]{2,1,0:T(2,128)(2,1)S(1)} %all-to-all-done.10) | data formatting | bytes 4718592
  86.5 4.9 %copy.106 = bf16[32,1,36864]{2,0,1:T(8,128)(2,1)S(1)} copy(bf16[32,1,36864]{2,1,0:T(2,128)(2,1)} %reshape.501) | data formatting | bytes 4718592
  100.5 23.5 %all_to_all.112 = bf16[32,2,9216]{2,1,0:T(2,128)(2,1)S(1)} all-to-all(bf16[32,2,9216]{2,1,0:T(2,128)(2,1)S(1)} %reshape.498), channel_id=1, replica_groups=mesh['expert'=32,'dp'=4] {'expert'}, dimensions={0} | all-to-all | bytes 2359296 | tf_op jit(solution)/shard_map/all_to_all | solution.py:22
  135.5 4.5 all-to-all-start.4
  148.1 9.2 %all-to-all-done.4 = bf16[32,16,1024]{2,1,0:T(8,128)(2,1)S(1)} async-done(((bf16[32,16,1024]{2,1,0:T(8,128)(2,1)}), bf16[32,16,1024]{2,1,0:T(8,128)(2,1)S(1)}, u32[]{:S(2)}, u32[]{:S(2)}) %all-to-all-start.4) | async-done | bytes 1048608 | tf_op jit(solution)/shard_map/all_to_all | solution.py:167
  157.2 4.0 all-to-all-start.8
  166.5 11.9 %all-to-all-done.8 = bf16[32,16,1024]{2,1,0:T(8,128)(2,1)S(1)} async-done(((bf16[32,16,1024]{2,1,0:T(8,128)(2,1)}), bf16[32,16,1024]{2,1,0:T(8,128)(2,1)S(1)}, u32[]{:S(2)}, u32[]{:S(2)}) %all-to-all-start.8) | async-done | bytes 1048608 | tf_op jit(solution)/shard_map/all_to_all | solution.py:193
  178.4 4.6 all-to-all-start
  199.5 6.3 %reshape.453 = bf16[4,589824]{1,0:T(4,128)(2,1)} reshape(bf16[2359296]{0:T(1024)(128)(2,1)} %all-gather.3.cloned.1.call-done) | data formatting | bytes 9437184 | tf_op jit(solution)/shard_map/all_gather | solution.py:41
  210.6 4.6 reshape_reshape.6
  215.1 3.9 reshape_reshape.7
  219.1 7.9 %all-to-all-start.6 = ((bf16[32,16,1024]{2,1,0:T(8,128)(2,1)}), bf16[32,16,1024]{2,1,0:T(8,128)(2,1)S(1)}, u32[]{:S(2)}, u32[]{:S(2)}) async-start(bf16[32,16,1024]{2,1,0:T(8,128)(2,1)} %bitcast.19), calls=%async_computation.6 | async-start | bytes 2097152 | tf_op jit(solution)/shard_map/all_to_all | solution.py:193
  227.0 3.8 fusion.32
  230.9 3.0 multiply_convert_fusion.1
  233.9 10.1 %all-to-all-done.6 = bf16[32,16,1024]{2,1,0:T(8,128)(2,1)S(1)} async-done(((bf16[32,16,1024]{2,1,0:T(8,128)(2,1)}), bf16[32,16,1024]{2,1,0:T(8,128)(2,1)S(1)}, u32[]{:S(2)}, u32[]{:S(2)}) %all-to-all-start.6) | async-done | bytes 1048608 | tf_op jit(solution)/shard_map/all_to_all | solution.py:193
  243.9 3.9 all-to-all-start.14
  247.8 5.6 %fusion.31 = f32[512,1536]{1,0:T(8,128)} fusion(bf16[512,1024]{1,0:T(8,128)(2,1)} %bitcast.4, bf16[1024,1536]{1,0:T(8,128)(2,1)} %reshape_reshape.6), kind=kOutput, calls=%fused_computation.154 | convolution fusion | flops 1610612736 | bytes 7340032 | tf_op jit(solution)/shard_map/dot_general | solution.py:117
  253.5 4.6 all-to-all-done.14
  258.1 3.8 all-to-all-start.13
  261.9 5.3 %multiply_convert_fusion.4 = (bf16[512,768]{1,0:T(8,128)(2,1)}, bf16[512,768]{1,0:T(8,128)(2,1)}, bf16[512,768]{1,0:T(8,128)(2,1)}) fusion(f32[512,1536]{1,0:T(8,128)} %fusion.31, bf16[512,1024]{1,0:T(8,128)(2,1)S(1)} %bitcast.114, bf16[768,1024]{1,0:T(8,128)(2,1)} %reshape_reshape.7), kind=kOutput, calls=%fused_computation.35 | convolution fusion | flops 811597824 | bytes 8126464 | tf_op jit(solution)/shard_map/dot_general | solution.py:200
  267.2 4.9 %all-to-all-done.13 = bf16[32,2,3072]{2,1,0:T(2,128)(2,1)S(1)} async-done(((bf16[32,2,3072]{2,1,0:T(2,128)(2,1)}), bf16[32,2,3072]{2,1,0:T(2,128)(2,1)S(1)}, u32[]{:S(2)}, u32[]{:S(2)}) %all-to-all-start.13) | async-done | bytes 393248 | tf_op jit(solution)/shard_map/all_to_all | solution.py:99
  272.9 3.8 all-to-all-start.12
  276.8 6.3 %fusion.2 = f32[1024,1536]{1,0:T(8,128)} fusion(bf16[512,1024]{1,0:T(8,128)(2,1)} %bitcast.4, bf16[512,768]{1,0:T(8,128)(2,1)} %get-tuple-element.30, bf16[512,768]{1,0:T(8,128)(2,1)} %get-tuple-element.29), kind=kOutput, calls=%fused_computation.55 | convolution fusion | flops 1613758464 | bytes 8912896 | tf_op jit(solution)/shard_map/dot_general | solution.py:210
  283.1 2.8 convolution_convert_fusion.2
  285.9 5.2 %all-to-all-done.12 = bf16[32,2,6144]{2,1,0:T(2,128)(2,1)S(1)} async-done(((bf16[32,2,6144]{2,1,0:T(2,128)(2,1)}), bf16[32,2,6144]{2,1,0:T(2,128)(2,1)S(1)}, u32[]{:S(2)}, u32[]{:S(2)}) %all-to-all-start.12) | async-done | bytes 786464 | tf_op jit(solution)/shard_map/all_to_all | solution.py:98
  292.0 4.4 all-to-all-start.11
  296.5 3.9 fusion.33
  300.4 6.4 %add_convert_fusion = bf16[1024,1536]{1,0:T(8,128)(2,1)} fusion(f32[1024,1536]{1,0:T(8,128)} %fusion.2, bf16[512,1024]{1,0:T(8,128)(2,1)S(1)} %bitcast.119, bf16[512,768]{1,0:T(8,128)(2,1)S(1)} %copy-done.53, bf16[512,768]{1,0:T(8,128)(2,1)S(1)} %copy-done.51), kind=kOutput, calls=%fused_computation.14 | convolution fusion | flops 1616904192 | bytes 12058624 | tf_op jit(solution)/shard_map/dot_general | solution.py:210
  306.8 3.9 all-to-all-done.11
  310.7 4.1 all-to-all-start.9
  314.8 4.3 add_convert_fusion.1
  320.6 3.1 convolution_convert_fusion
  323.7 8.3 %all-to-all-done.9 = bf16[32,16,1024]{2,1,0:T(8,128)(2,1)S(1)} async-done(((bf16[32,16,1024]{2,1,0:T(8,128)(2,1)}), bf16[32,16,1024]{2,1,0:T(8,128)(2,1)S(1)}, u32[]{:S(2)}, u32[]{:S(2)}) %all-to-all-start.9) | async-done | bytes 1048608 | tf_op jit(solution)/shard_map/all_to_all | solution.py:219
  331.9 4.0 all-to-all-start.5
  336.6 5.2 %convolution_convert_fusion.3 = bf16[512,1024]{1,0:T(8,128)(2,1)} fusion(bf16[1024,1536]{1,0:T(8,128)(2,1)} %reshape_reshape.6, bf16[512,768]{1,0:T(8,128)(2,1)} %get-tuple-element.30, bf16[512,768]{1,0:T(8,128)(2,1)} %get-tuple-element.29), kind=kOutput, calls=%fused_computation.44 | convolution fusion | flops 1614282752 | bytes 5767168 | tf_op jit(solution)/shard_map/dot_general | solution.py:216
  341.7 11.4 %all-to-all-done.5 = bf16[32,16,1024]{2,1,0:T(8,128)(2,1)S(1)} async-done(((bf16[32,16,1024]{2,1,0:T(8,128)(2,1)}), bf16[32,16,1024]{2,1,0:T(8,128)(2,1)S(1)}, u32[]{:S(2)}, u32[]{:S(2)}) %all-to-all-start.5) | async-done | bytes 1048608 | tf_op jit(solution)/shard_map/all_to_all | solution.py:175
  353.1 4.3 all-to-all-start.7
  358.5 4.3 convert_reduce_fusion.2
  366.1 4.3 convert_reduce_fusion.3
  372.7 5.8 %reshape.503 = bf16[32,1,12288]{2,1,0:T(2,128)(2,1)} reshape(bf16[32,2,6144]{2,1,0:T(2,128)(2,1)} %copy-done.15) | data formatting | bytes 1572864
  378.4 3.8 convolution_convert_fusion.1
  382.2 8.2 %all-to-all-start.3 = ((bf16[32,16,1024]{2,1,0:T(8,128)(2,1)}), bf16[32,16,1024]{2,1,0:T(8,128)(2,1)}, u32[]{:S(2)}, u32[]{:S(2)}) async-start(bf16[32,16,1024]{2,1,0:T(8,128)(2,1)} %bitcast.121), calls=%async_computation.3 | async-start | bytes 2097152 | tf_op jit(solution)/shard_map/all_to_all | solution.py:175
  390.4 7.2 %convert_reduce_fusion = f32[32,12288]{1,0:T(8,128)} fusion(bf16[32,1,12288]{2,1,0:T(2,128)(2,1)} %reshape.503), kind=kLoop, calls=%fused_computation.28 | loop fusion | flops 786432 | bytes 2359296 | tf_op jit(solution)/shard_map/convert_element_type | solution.py:51
  397.6 2.6 reshape.337
  400.2 5.8 %reshape.505 = bf16[32,1,12288]{2,1,0:T(2,128)(2,1)} reshape(bf16[32,2,6144]{2,1,0:T(2,128)(2,1)} %copy-done.14) | data formatting | bytes 1572864
  406.0 7.1 %convert_reduce_fusion.1 = f32[32,12288]{1,0:T(8,128)} fusion(bf16[32,1,12288]{2,1,0:T(2,128)(2,1)} %reshape.505), kind=kLoop, calls=%fused_computation.29 | loop fusion | flops 786432 | bytes 2359296 | tf_op jit(solution)/shard_map/convert_element_type | solution.py:50
  413.2 2.7 reshape.336
  415.9 2.6 reshape.335
  420.7 2.8 gather_fusion.9
  423.5 2.7 gather_fusion.5
  426.2 2.8 broadcast_select_fusion.4
  430.4 2.7 gather_fusion.7
  433.1 4.8 %gather_fusion.3 = bf16[384,1024]{1,0:T(8,128)(2,1)} fusion(bf16[512,1024]{1,0:T(8,128)(2,1)} %bitcast.8, s32[1024]{0:T(1024)S(1)} %pad_clamp_fusion.4), kind=kCustom, calls=%fused_computation.1.clone | custom fusion | bytes 1574400 | tf_op jit(solution)/shard_map/jit(_take)/gather | solution.py:182
  438.0 2.8 broadcast_select_fusion.5
  440.7 2.7 reshape.331
  451.3 4.9 %fusion.4 = (f32[1,256,1536]{2,1,0:T(8,128)}, bf16[1,256,1536]{2,1,0:T(8,128)(2,1)}, f32[1,256,1536]{2,1,0:T(8,128)}) fusion(f32[256,1536]{1,0:T(8,128)S(1)} %copy-done.2, bf16[1024,1536]{1,0:T(8,128)(2,1)} %get-tuple-element.20, s32[]{:T(128)S(6)} %select_n.74, f32[256,1536]{1,0:T(8,128)} %reshape.335, f32[256,1536]{1,0:T(8,128)S(1)} %copy-done.3), kind=kLoop, calls=%fused_computation.58 | loop fusion | flops 5898240 | bytes 9437188 | tf_op jit(solution)/shard_map/add | solution.py:51
  456.2 2.8 fusion.11
  (243 shorter events, 98.4 us)
Async XLA Ops:
  13.8 9.7 %copy-start.30 = (f32[1,192,1024]{2,1,0:T(8,128)S(1)}, f32[1,192,1024]{2,1,0:T(8,128)}, u32[]{:S(2)}) copy-start(f32[1,192,1024]{2,1,0:T(8,128)} %param.31) | copy-start | bytes 2359300
  13.8 28.3 %all-to-all-start.1 = ((bf16[32,2,9216]{2,1,0:T(2,128)(2,1)}), bf16[32,2,9216]{2,1,0:T(2,128)(2,1)S(1)}, u32[]{:S(2)}, u32[]{:S(2)}) async-start(bf16[32,2,9216]{2,1,0:T(2,128)(2,1)} %reshape.496), calls=%async_computation.1 | async-start | bytes 2359296 | tf_op jit(solution)/shard_map/all_to_all | solution.py:22
  23.6 3.5 copy-start.18
  27.1 1.6 copy-start.19
  39.6 8.6 %copy-start.47 = (s32[32]{0:T(128)S(1)}, s32[32]{0:T(128)}, u32[]{:S(2)}) copy-start(s32[32]{0:T(128)} %param.25) | copy-start | bytes 388
  43.0 36.5 %all-to-all-start.10 = ((bf16[32,2,18432]{2,1,0:T(2,128)(2,1)}), bf16[32,2,18432]{2,1,0:T(2,128)(2,1)S(1)}, u32[]{:S(2)}, u32[]{:S(2)}) async-start(bf16[32,2,18432]{2,1,0:T(2,128)(2,1)} %reshape.500), calls=%async_computation.10 | async-start | bytes 4718592 | tf_op jit(solution)/shard_map/all_to_all | solution.py:22
  48.0 151.5 %all-gather.3.cloned.1.call-start = ((), (), s32[]{:S(2)}) async-start(), calls=%async_computation.15 | async-start | bytes 5898240 | tf_op jit(solution)/shard_map/all_gather | solution.py:41
  95.3 1.2 copy-start.7
  128.2 1.2 copy-start.45
  129.3 1.4 copy-start.37
  130.1 2.2 copy-start.38
  130.8 1.5 copy-start.40
  135.5 4.5 copy-start.36
  135.5 21.7 %all-to-all-start.4 = ((bf16[32,16,1024]{2,1,0:T(8,128)(2,1)}), bf16[32,16,1024]{2,1,0:T(8,128)(2,1)S(1)}, u32[]{:S(2)}, u32[]{:S(2)}) async-start(bf16[32,16,1024]{2,1,0:T(8,128)(2,1)} %bitcast.13), calls=%async_computation.4 | async-start | bytes 2097152 | tf_op jit(solution)/shard_map/all_to_all | solution.py:167
  140.4 1.4 copy-start.46
  148.1 13.2 %copy-start.31 = (bf16[64,1024]{1,0:T(8,128)(2,1)S(1)}, bf16[64,1024]{1,0:T(8,128)(2,1)}, u32[]{:S(2)}) copy-start(bf16[64,1024]{1,0:T(8,128)(2,1)} %get-tuple-element.48) | copy-start | bytes 393220
  148.1 13.2 %copy-start.42 = (s32[512]{0:T(512)S(1)}, s32[512]{0:T(512)}, u32[]{:S(2)}) copy-start(s32[512]{0:T(512)} %get-tuple-element.17) | copy-start | bytes 6148
  157.2 7.5 %copy-start.27 = (bf16[32,16,1024]{2,1,0:T(8,128)(2,1)}, bf16[32,16,1024]{2,1,0:T(8,128)(2,1)S(1)}, u32[]{:S(2)}) copy-start(bf16[32,16,1024]{2,1,0:T(8,128)(2,1)S(1)} %all-to-all-done.4) | copy-start | bytes 3145732
  157.2 21.1 %all-to-all-start.8 = ((bf16[32,16,1024]{2,1,0:T(8,128)(2,1)}), bf16[32,16,1024]{2,1,0:T(8,128)(2,1)S(1)}, u32[]{:S(2)}, u32[]{:S(2)}) async-start(bf16[32,16,1024]{2,1,0:T(8,128)(2,1)} %bitcast.25), calls=%async_computation.8 | async-start | bytes 2097152 | tf_op jit(solution)/shard_map/all_to_all | solution.py:193
  178.4 4.7 %copy-start.5 = (bf16[32,16,1024]{2,1,0:T(8,128)(2,1)}, bf16[32,16,1024]{2,1,0:T(8,128)(2,1)S(1)}, u32[]{:S(2)}) copy-start(bf16[32,16,1024]{2,1,0:T(8,128)(2,1)S(1)} %all-to-all-done.8) | copy-start | bytes 3145732
  178.4 40.7 %all-to-all-start = ((bf16[32,16,1024]{2,1,0:T(8,128)(2,1)}), bf16[32,16,1024]{2,1,0:T(8,128)(2,1)}, u32[]{:S(2)}, u32[]{:S(2)}) async-start(bf16[32,16,1024]{2,1,0:T(8,128)(2,1)} %bitcast.3), calls=%async_computation | async-start | bytes 2097152 | tf_op jit(solution)/shard_map/all_to_all | solution.py:167
  183.3 1.4 copy-start.44
  185.4 1.8 copy-start.43
  187.2 2.1 copy-start.49
  189.3 1.2 copy-start.9
  190.5 2.7 copy-start.8
  193.2 2.7 copy-start.23
  194.4 3.3 copy-start.22
  205.8 2.3 copy-start
  208.1 2.5 slice-start
  219.1 7.9 %copy-start.28 = (bf16[32,16,1024]{2,1,0:T(8,128)(2,1)S(1)}, bf16[32,16,1024]{2,1,0:T(8,128)(2,1)}, u32[]{:S(2)}) copy-start(bf16[32,16,1024]{2,1,0:T(8,128)(2,1)} %copy-done.27) | copy-start | bytes 3145732
  219.1 24.9 %all-to-all-start.6 = ((bf16[32,16,1024]{2,1,0:T(8,128)(2,1)}), bf16[32,16,1024]{2,1,0:T(8,128)(2,1)S(1)}, u32[]{:S(2)}, u32[]{:S(2)}) async-start(bf16[32,16,1024]{2,1,0:T(8,128)(2,1)} %bitcast.19), calls=%async_computation.6 | async-start | bytes 2097152 | tf_op jit(solution)/shard_map/all_to_all | solution.py:193
  227.0 3.9 copy-start.6
  227.0 3.9 copy-start.20
  243.9 14.2 %all-to-all-start.14 = ((bf16[32,2,3072]{2,1,0:T(2,128)(2,1)}), bf16[32,2,3072]{2,1,0:T(2,128)(2,1)S(1)}, u32[]{:S(2)}, u32[]{:S(2)}) async-start(bf16[32,2,3072]{2,1,0:T(2,128)(2,1)} %reshape.506), calls=%async_computation.14 | async-start | bytes 786432 | tf_op jit(solution)/shard_map/all_to_all | solution.py:100
  258.1 14.1 %all-to-all-start.13 = ((bf16[32,2,3072]{2,1,0:T(2,128)(2,1)}), bf16[32,2,3072]{2,1,0:T(2,128)(2,1)S(1)}, u32[]{:S(2)}, u32[]{:S(2)}) async-start(bf16[32,2,3072]{2,1,0:T(2,128)(2,1)} %reshape.508), calls=%async_computation.13 | async-start | bytes 786432 | tf_op jit(solution)/shard_map/all_to_all | solution.py:99
  272.9 18.2 %all-to-all-start.12 = ((bf16[32,2,6144]{2,1,0:T(2,128)(2,1)}), bf16[32,2,6144]{2,1,0:T(2,128)(2,1)S(1)}, u32[]{:S(2)}, u32[]{:S(2)}) async-start(bf16[32,2,6144]{2,1,0:T(2,128)(2,1)} %reshape.502), calls=%async_computation.12 | async-start | bytes 1572864 | tf_op jit(solution)/shard_map/all_to_all | solution.py:98
  276.8 6.3 %copy-start.13 = (bf16[1024,1536]{1,0:T(8,128)(2,1)S(1)}, bf16[1024,1536]{1,0:T(8,128)(2,1)}, u32[]{:S(2)}) copy-start(bf16[1024,1536]{1,0:T(8,128)(2,1)} %reshape_reshape.6) | copy-start | bytes 9437188
  276.8 6.3 %copy-start.50 = (bf16[512,768]{1,0:T(8,128)(2,1)S(1)}, bf16[512,768]{1,0:T(8,128)(2,1)}, u32[]{:S(2)}) copy-start(bf16[512,768]{1,0:T(8,128)(2,1)} %get-tuple-element.31) | copy-start | bytes 2359300
  276.8 6.3 %copy-start.52 = (bf16[512,768]{1,0:T(8,128)(2,1)S(1)}, bf16[512,768]{1,0:T(8,128)(2,1)}, u32[]{:S(2)}) copy-start(bf16[512,768]{1,0:T(8,128)(2,1)} %get-tuple-element.32) | copy-start | bytes 2359300
  292.0 18.7 %all-to-all-start.11 = ((bf16[32,2,6144]{2,1,0:T(2,128)(2,1)}), bf16[32,2,6144]{2,1,0:T(2,128)(2,1)S(1)}, u32[]{:S(2)}, u32[]{:S(2)}) async-start(bf16[32,2,6144]{2,1,0:T(2,128)(2,1)} %reshape.504), calls=%async_computation.11 | async-start | bytes 1572864 | tf_op jit(solution)/shard_map/all_to_all | solution.py:97
  296.4 4.0 copy-start.29
  296.5 4.0 copy-start.51
  296.5 4.0 copy-start.53
  310.7 8.5 %copy-start.14 = (bf16[32,2,6144]{2,1,0:T(2,128)(2,1)}, bf16[32,2,6144]{2,1,0:T(2,128)(2,1)S(1)}, u32[]{:S(2)}) copy-start(bf16[32,2,6144]{2,1,0:T(2,128)(2,1)S(1)} %all-to-all-done.11) | copy-start | bytes 2359300
  310.7 21.2 %all-to-all-start.9 = ((bf16[32,16,1024]{2,1,0:T(8,128)(2,1)}), bf16[32,16,1024]{2,1,0:T(8,128)(2,1)S(1)}, u32[]{:S(2)}, u32[]{:S(2)}) async-start(bf16[32,16,1024]{2,1,0:T(8,128)(2,1)} %bitcast.120), calls=%async_computation.9 | async-start | bytes 2097152 | tf_op jit(solution)/shard_map/all_to_all | solution.py:219
  314.8 136.5 %all-reduce.7.cloned.1.call-start = ((), (), s32[]{:S(2)}) async-start(), calls=%async_computation.16 | async-start | bytes 9437184 | tf_op jit(solution)/shard_map/psum | solution.py:233
  319.2 1.4 copy-start.21
  323.7 12.2 %copy-start.39 = (s32[384]{0:T(512)S(1)}, s32[384]{0:T(512)}, u32[]{:S(2)}) copy-start(s32[384]{0:T(512)} %copy-done.38) | copy-start | bytes 4612
  331.9 21.1 %all-to-all-start.5 = ((bf16[32,16,1024]{2,1,0:T(8,128)(2,1)}), bf16[32,16,1024]{2,1,0:T(8,128)(2,1)S(1)}, u32[]{:S(2)}, u32[]{:S(2)}) async-start(bf16[32,16,1024]{2,1,0:T(8,128)(2,1)} %bitcast.123), calls=%async_computation.5 | async-start | bytes 2097152 | tf_op jit(solution)/shard_map/all_to_all | solution.py:175
  353.1 29.2 %all-to-all-start.7 = ((bf16[32,16,1024]{2,1,0:T(8,128)(2,1)}), bf16[32,16,1024]{2,1,0:T(8,128)(2,1)S(1)}, u32[]{:S(2)}, u32[]{:S(2)}) async-start(bf16[32,16,1024]{2,1,0:T(8,128)(2,1)} %bitcast.122), calls=%async_computation.7 | async-start | bytes 2097152 | tf_op jit(solution)/shard_map/all_to_all | solution.py:219
  358.5 6.6 %copy-start.25 = (bf16[32,2,3072]{2,1,0:T(2,128)(2,1)S(1)}, bf16[32,2,3072]{2,1,0:T(2,128)(2,1)}, u32[]{:S(2)}) copy-start(bf16[32,2,3072]{2,1,0:T(2,128)(2,1)} %copy-done.24) | copy-start | bytes 1179652
  382.2 50.9 %all-to-all-start.3 = ((bf16[32,16,1024]{2,1,0:T(8,128)(2,1)}), bf16[32,16,1024]{2,1,0:T(8,128)(2,1)}, u32[]{:S(2)}, u32[]{:S(2)}) async-start(bf16[32,16,1024]{2,1,0:T(8,128)(2,1)} %bitcast.121), calls=%async_computation.3 | async-start | bytes 2097152 | tf_op jit(solution)/shard_map/all_to_all | solution.py:175
  423.5 2.7 copy-start.17
  423.5 2.7 copy-start.48
  433.1 4.8 %copy-start.16 = (bf16[384,1024]{1,0:T(8,128)(2,1)S(1)}, bf16[384,1024]{1,0:T(8,128)(2,1)}, u32[]{:S(2)}) copy-start(bf16[384,1024]{1,0:T(8,128)(2,1)} %gather_fusion.7) | copy-start | bytes 2359300
  445.4 2.1 copy-start.33
  446.8 1.5 copy-start.35
  447.5 1.6 copy-start.1
  449.1 2.2 copy-start.2
  449.1 2.2 copy-start.3
  451.3 4.9 %copy-start.10 = (f32[192,1024]{1,0:T(8,128)S(1)}, f32[192,1024]{1,0:T(8,128)}, u32[]{:S(2)}) copy-start(f32[192,1024]{1,0:T(8,128)} %reshape.340) | copy-start | bytes 2359300
  451.3 4.9 %copy-start.11 = (f32[192,1024]{1,0:T(8,128)S(1)}, f32[192,1024]{1,0:T(8,128)}, u32[]{:S(2)}) copy-start(f32[192,1024]{1,0:T(8,128)} %reshape.339) | copy-start | bytes 2359300
  451.3 4.9 %copy-start.12 = (f32[192,1024]{1,0:T(8,128)S(1)}, f32[192,1024]{1,0:T(8,128)}, u32[]{:S(2)}) copy-start(f32[192,1024]{1,0:T(8,128)} %reshape.338) | copy-start | bytes 2359300
  (7 other events, 5.6 us)
Sparse Core Ops, SparseCore 0:
  129.5 49.8 all-gather.2
  319.3 102.1 all-reduce.6
where the time goes:
time: 475 us; the launch traced here: 466 us
  local copies, waits for them, and re-layouts  138 us (29%)
  waiting for transfers between devices  91.3 us (19%)
  starting transfers between devices  72.6 us (15%)
  other arithmetic  71.5 us (15%)
  matrix products  53.6 us (11%)
  blocking collectives  23.5 us (5%)
  between operations  15.3 us (3%)
    unnamed x127, local copies, waits for them, and re-layouts  56.8 us
    all_to_all x1, blocking collectives, side_by_side(): lax.all_to_all(both, axis, split_axis=split_dim, concat_axis=concat_dim,...  23.5 us
    all_to_all x2, waiting for transfers between devices, side_by_side(): lax.all_to_all(both, axis, split_axis=split_dim, concat_axis=concat_dim,...  21.9 us
    all_to_all x2, waiting for transfers between devices, on_device(): lax.all_to_all(outgoing_grad.reshape(count, capacity, width), 'expert', s...  21.9 us
    all_to_all x2, starting transfers between devices, side_by_side(): lax.all_to_all(both, axis, split_axis=split_dim, concat_axis=concat_dim,...  14.7 us
    dot_general x2, matrix products, on_device(): lax.dot_general(arrived, pre_grad, (((0,), (0,)), ((), ())), preferred_el...  12.7 us
    all_to_all x2, starting transfers between devices, on_device(): lax.all_to_all(output.reshape(count, capacity, width), 'expert', split_ax...  12.2 us
    all_to_all x2, starting transfers between devices, on_device(): lax.all_to_all(outgoing_grad.reshape(count, capacity, width), 'expert', s...  11.9 us
  transfers between devices with their start and end apart: 16, of which 11 were waited for; matrix products, arithmetic and copies ran while one was open for 46% of the time, Pallas kernels for 0%

commit v1 on v0

v1 whole, which is shorter than its diff:
```python
import functools

import jax
import jax.numpy as jnp
from jax import lax
from jax.experimental import pallas as pl
from jax.experimental.pallas import tpu as pltpu
from jax.sharding import PartitionSpec as P

beta_one = 0.9
beta_two = 0.95
learn_rate = 0.00042
decay_rate = 0.1
epsilon = 1e-08
steps_done = 10

SIDE = 768
RI = 256
RO = 192
RT = 64
REP = 4
COUNT = 32
CAP = 16
ROWS = 2 * CAP

f32 = jnp.float32
bf16 = jnp.bfloat16
VMEM = pl.BlockSpec(memory_space=pltpu.VMEM)
SMEM = pl.BlockSpec(memory_space=pltpu.SMEM)
ANY = pl.BlockSpec(memory_space=pl.ANY)


def exchange(x):
    return lax.all_to_all(x, "expert", split_axis=0, concat_axis=0, tiled=True)


def shifted(x, by):
    return lax.ppermute(x, "dp", [(i, (i + by) % REP) for i in range(REP)])


def pack_body(w_in, w_out, f_in, f_out, s_in, s_out, out):
    for j, (a, b) in enumerate(((w_in, w_out), (f_in, f_out), (s_in, s_out))):
        lanes = slice(j * SIDE, (j + 1) * SIDE)
        out[0:RI, lanes] = a[:, :SIDE].astype(bf16)
        out[RI : 2 * RI, lanes] = a[:, SIDE:].astype(bf16)
        out[2 * RI : 2 * RI + RO, lanes] = b[:, :SIDE].astype(bf16)
        for i in range(3):
            at = j * SIDE + 256 * i
            out[2 * RI + RO :, at : at + 256] = b[RT * i : RT * i + RT, SIDE:].astype(bf16)


def pack(w_in, w_out, f_in, f_out, s_in, s_out):
    return pl.pallas_call(
        pack_body,
        out_shape=jax.ShapeDtypeStruct((SIDE, 3 * SIDE), bf16),
        in_specs=[VMEM] * 6,
        out_specs=VMEM,
        name="pack",
    )(w_in, w_out, f_in, f_out, s_in, s_out)


def pick_body(lo, size, plan, src, out, sem):
    copies = [
        pltpu.make_async_copy(src.at[plan[d], :, lo : lo + size], out.at[d], sem.at[d]) for d in range(COUNT)
    ]
    for c in copies:
        c.start()
    for c in copies:
        c.wait()


def pick(plan, src, lo, size):
    return pl.pallas_call(
        functools.partial(pick_body, lo, size),
        out_shape=jax.ShapeDtypeStruct((COUNT, SIDE // COUNT, size), bf16),
        in_specs=[SMEM, ANY],
        out_specs=ANY,
        scratch_shapes=[pltpu.SemaphoreType.DMA((COUNT,))],
        name="pick",
    )(plan, src)


def dispatch_body(routes, gates, plan, tokens, cotangent, out, place, gated):
    n = tokens.shape[1]
    top = routes.shape[0]
    holder = plan[...]
    earlier = (
        lax.broadcasted_iota(jnp.int32, (n, n), 0) < lax.broadcasted_iota(jnp.int32, (n, n), 1)
    ).astype(bf16)
    slot = lax.broadcasted_iota(jnp.int32, (COUNT, CAP, n), 1).astype(f32)
    for m in range(2):
        hit = jnp.zeros((COUNT, n), f32)
        gate = jnp.zeros((COUNT, n), f32)
        for k in range(top):
            one = routes[k, m : m + 1, :] == holder
            hit = hit + jnp.where(one, 1.0, 0.0)
            gate = gate + jnp.where(one, gates[k, m : m + 1, :], 0.0)
        rank = jnp.dot(hit.astype(bf16), earlier, preferred_element_type=f32)
        rank = jnp.where(hit > 0.0, rank, -1.0)
        wide = jnp.broadcast_to(rank[:, None, :], (COUNT, CAP, n))
        chosen = jnp.where(wide == slot, 1.0, 0.0)
        weighted = chosen * jnp.broadcast_to(gate[:, None, :], (COUNT, CAP, n))
        chosen = chosen.reshape(COUNT * CAP, n)
        weighted = weighted.reshape(COUNT * CAP, n)
        column = jnp.sum(weighted, axis=1, keepdims=True)
        chosen = chosen.astype(bf16)
        high = weighted.astype(bf16)
        low = (weighted - high.astype(f32)).astype(bf16)
        place[m] = chosen
        gated[m, :, :n] = high
        gated[m, :, n:] = low
        sent = jnp.dot(chosen, tokens[m], preferred_element_type=f32).astype(bf16)
        out[:, CAP * m : CAP * m + CAP, :] = sent.reshape(COUNT, CAP, -1)
        grads = jnp.dot(chosen, cotangent[m], preferred_element_type=f32) * column
        out[:, ROWS + CAP * m : ROWS + CAP * m + CAP, :] = grads.astype(bf16).reshape(COUNT, CAP, -1)


def dispatch(routes, gates, plan, tokens, cotangent):
    n, width = tokens.shape[1:]
    return pl.pallas_call(
        dispatch_body,
        out_shape=(
            jax.ShapeDtypeStruct((COUNT, 2 * ROWS, width), bf16),
            jax.ShapeDtypeStruct((2, COUNT * CAP, n), bf16),
            jax.ShapeDtypeStruct((2, COUNT * CAP, 2 * n), bf16),
        ),
        in_specs=[VMEM] * 5,
        out_specs=(VMEM, VMEM, VMEM),
        name="dispatch",
    )(routes, gates, plan, tokens, cotangent)


ROW_T = (((0,), (0,)), ((), ()))
COL_T = (((1,), (1,)), ((), ()))


def combine_body(back, place, gated, layer, token):
    n = layer.shape[1]
    for m in range(2):
        rows = back[:, CAP * m : CAP * m + CAP, :].reshape(COUNT * CAP, -1)
        both = lax.dot_general(gated[m], rows, ROW_T, preferred_element_type=f32)
        layer[m] = (both[:n] + both[n:]).astype(bf16)
        rows = back[:, ROWS + CAP * m : ROWS + CAP * m + CAP, :].reshape(COUNT * CAP, -1)
        token[m] = lax.dot_general(place[m], rows, ROW_T, preferred_element_type=f32).astype(bf16)


def combine(back, place, gated):
    n = place.shape[2]
    width = back.shape[2]
    shape = jax.ShapeDtypeStruct((2, n, width), bf16)
    return pl.pallas_call(
        combine_body,
        out_shape=(shape, shape),
        in_specs=[VMEM] * 3,
        out_specs=(VMEM, VMEM),
        name="combine",
    )(back, place, gated)


def expert_body(mine, rows, w0, w1, w2, w3, back, g0, g1, g2, g3, win, wout, hid, pgrad, gout, gpack, sem, gsem):
    r = mine[0]
    copies = []
    for s, w in enumerate((w0, w1, w2, w3)):
        q = (r - s + REP) % REP
        at = pl.multiple_of(q * RI, RI)
        to = pl.multiple_of(q * RO, RT)
        pieces = [
            (w.at[0:RI], win.at[pl.ds(at, RI), 0:SIDE]),
            (w.at[RI : 2 * RI], win.at[pl.ds(at, RI), SIDE : 2 * SIDE]),
            (w.at[2 * RI : 2 * RI + RO], wout.at[pl.ds(to, RO), 0:SIDE]),
        ]
        for i in range(3):
            pieces.append(
                (
                    w.at[2 * RI + RO : SIDE, 256 * i : 256 * i + 256],
                    wout.at[pl.ds(to + RT * i, RT), SIDE : SIDE + 256],
                )
            )
        for a, b in pieces:
            copies.append(pltpu.make_async_copy(a, b, sem.at[len(copies)]))
    for c in copies:
        c.start()
    for c in copies:
        c.wait()

    group = 8
    size = group * ROWS

    def step(i, carry):
        own = pl.ds(pl.multiple_of(i * group, group), group)
        at = pl.ds(pl.multiple_of(i * size, size), size)
        x = rows[own, 0:ROWS, :].reshape(size, -1)
        pre = jnp.dot(x, win[...], preferred_element_type=f32)
        gate = pre[:, :SIDE]
        up = pre[:, SIDE:]
        sigma = jax.nn.sigmoid(gate)
        swish = gate * sigma
        hidden = (swish * up).astype(bf16)
        hid[at, :] = hidden
        out = jnp.dot(hidden, wout[...], preferred_element_type=f32).astype(bf16)
        back[own, 0:ROWS, :] = out.reshape(group, ROWS, -1)
        g = rows[own, ROWS : 2 * ROWS, :].reshape(size, -1)
        hgrad = lax.dot_general(g, wout[...], COL_T, preferred_element_type=f32)
        pgrad[at, 0:SIDE] = (hgrad * up * sigma * (1.0 + gate * (1.0 - sigma))).astype(bf16)
        pgrad[at, SIDE:] = (hgrad * swish).astype(bf16)
        part = lax.dot_general(pgrad[at, :], win[...], COL_T, preferred_element_type=f32).astype(bf16)
        back[own, ROWS : 2 * ROWS, :] = part.reshape(group, ROWS, -1)
        return carry

    lax.fori_loop(0, COUNT // group, step, 0)
    for q in range(REP):
        x = rows[:, 0:ROWS, RI * q : RI * q + RI].reshape(COUNT * ROWS, RI)
        grad = lax.dot_general(x, pgrad[...], ROW_T, preferred_element_type=f32).astype(bf16)
        gpack[q, 0:RI, :] = grad[:, :SIDE]
        gpack[q, RI : 2 * RI, :] = grad[:, SIDE:]
    g = rows[:, ROWS : 2 * ROWS, :].reshape(COUNT * ROWS, -1)
    for j in range(3):
        gout[256 * j : 256 * j + 256, :] = lax.dot_general(
            hid[:, 256 * j : 256 * j + 256], g, ROW_T, preferred_element_type=f32
        ).astype(bf16)
    for q in range(REP):
        gpack[q, 2 * RI : 2 * RI + RO, :] = gout[RO * q : RO * q + RO, :SIDE]
        for i in range(3):
            gpack[q, 2 * RI + RO :, 256 * i : 256 * i + 256] = gout[RO * q + RT * i : RO * q + RT * i + RT, SIDE:]
    copies = [
        pltpu.make_async_copy(gpack.at[(r + s) % REP], out, gsem.at[s]) for s, out in enumerate((g0, g1, g2, g3))
    ]
    for c in copies:
        c.start()
    for c in copies:
        c.wait()


def expert(mine, rows, parts):
    width = rows.shape[2]
    piece = jax.ShapeDtypeStruct((SIDE, SIDE), bf16)
    total = COUNT * ROWS
    return pl.pallas_call(
        expert_body,
        out_shape=(jax.ShapeDtypeStruct(rows.shape, bf16), piece, piece, piece, piece),
        in_specs=[SMEM, VMEM, ANY, ANY, ANY, ANY],
        out_specs=(VMEM, ANY, ANY, ANY, ANY),
        scratch_shapes=[
            pltpu.VMEM((REP * RI, 2 * SIDE), bf16),
            pltpu.VMEM((REP * RO, width), bf16),
            pltpu.VMEM((total, SIDE), bf16),
            pltpu.VMEM((total, 2 * SIDE), bf16),
            pltpu.VMEM((SIDE, width), bf16),
            pltpu.VMEM((REP, SIDE, SIDE), bf16),
            pltpu.SemaphoreType.DMA((24,)),
            pltpu.SemaphoreType.DMA((REP,)),
        ],
        cost_estimate=pl.CostEstimate(flops=14_500_000_000, bytes_accessed=18_000_000, transcendentals=800_000),
        name="expert",
    )(mine, rows, *parts)


def adam(weight, gradient, first, second):
    first_new = beta_one * first + (1.0 - beta_one) * gradient
    second_new = beta_two * second + (1.0 - beta_two) * gradient * gradient
    ratio = (
        first_new
        / (1.0 - beta_one**steps_done)
        / (jnp.sqrt(second_new / (1.0 - beta_two**steps_done)) + epsilon)
    )
    master = weight.astype(f32)
    return (
        (master - learn_rate * (ratio + decay_rate * master)).astype(bf16),
        first_new,
        second_new,
    )


def update_body(w, moments, g0, g1, g2, g3, w_in, w_out, f_in, s_in, f_out, s_out):
    def one(rows, lanes, outs, at, to):
        grad = g0[rows, lanes].astype(f32)
        for g in (g1, g2, g3):
            grad = grad + g[rows, lanes].astype(f32)
        second = slice(lanes.start + SIDE, lanes.stop + SIDE)
        new = adam(w[rows, lanes], grad, moments[rows, lanes].astype(f32), moments[rows, second].astype(f32))
        for o, v in zip(outs, new):
            o[at, to] = v

    ins = (w_in, f_in, s_in)
    outs = (w_out, f_out, s_out)
    whole = slice(0, SIDE)
    for i in range(RI // RT):
        here = slice(RT * i, RT * i + RT)
        one(here, whole, ins, here, whole)
        one(slice(RI + RT * i, RI + RT * i + RT), whole, ins, here, slice(SIDE, 2 * SIDE))
    for i in range(3):
        here = slice(RT * i, RT * i + RT)
        one(slice(2 * RI + RT * i, 2 * RI + RT * i + RT), whole, outs, here, whole)
        one(slice(2 * RI + RO, SIDE), slice(256 * i, 256 * i + 256), outs, here, slice(SIDE, SIDE + 256))


def update(w, moments, grads):
    return pl.pallas_call(
        update_body,
        out_shape=(
            jax.ShapeDtypeStruct((RI, 2 * SIDE), bf16),
            jax.ShapeDtypeStruct((RO, 1024), bf16),
            jax.ShapeDtypeStruct((RI, 2 * SIDE), f32),
            jax.ShapeDtypeStruct((RI, 2 * SIDE), f32),
            jax.ShapeDtypeStruct((RO, 1024), f32),
            jax.ShapeDtypeStruct((RO, 1024), f32),
        ),
        in_specs=[VMEM] * 6,
        out_specs=(VMEM,) * 6,
        name="update",
    )(w, moments, *grads)


def on_device(
    tokens,
    routes,
    gate_weights,
    cotangent,
    expert_plan,
    weight_in,
    weight_out,
    first_in,
    second_in,
    first_out,
    second_out,
):
    mine = lax.axis_index("dp").astype(jnp.int32).reshape(1)
    packed = pack(weight_in[0], weight_out[0], first_in[0], first_out[0], second_in[0], second_out[0])
    spread = exchange(packed.reshape(COUNT, SIDE // COUNT, 3 * SIDE))
    own = exchange(pick(expert_plan, spread, 0, SIDE)).reshape(SIDE, SIDE)
    outgoing, place, gated = dispatch(
        routes.transpose(2, 0, 1), gate_weights.transpose(2, 0, 1), expert_plan.reshape(-1, 1), tokens, cotangent
    )
    outgoing, own = lax.optimization_barrier((outgoing, own))
    parts = (own, shifted(own, 1), shifted(own, 2), shifted(own, 3))
    arrived = exchange(outgoing)
    moved = pick(expert_plan, spread, SIDE, 2 * SIDE)
    arrived, moved = lax.optimization_barrier((arrived, moved))
    moments = exchange(moved).reshape(SIDE, 2 * SIDE)
    back, g0, g1, g2, g3 = expert(mine, arrived, parts)
    back, moments = lax.optimization_barrier((back, moments))
    grads = (g0, shifted(g1, 1), shifted(g2, 2), shifted(g3, 3))
    returned = exchange(back)
    new_in, new_out, first_in_new, second_in_new, first_out_new, second_out_new = update(own, moments, grads)
    layer, token = combine(returned, place, gated)
    return (
        layer,
        token,
        new_in[None],
        new_out[None],
        first_in_new[None],
        second_in_new[None],
        first_out_new[None],
        second_out_new[None],
    )


def solution(mesh):
    rows = P(None, ("expert", "dp"), None)
    held = P("expert", "dp", None)
    return jax.shard_map(
        on_device,
        mesh=mesh,
        in_specs=(rows,) * 4 + (P(),) + (held,) * 6,
        out_specs=(rows,) * 2 + (held,) * 6,
        check_vma=False,
    )
```

time: 475 us -> 317 us (0.67); the launches traced: 466 us -> 317 us
  Pallas kernels: 0 us -> 158 us
  local copies, waits for them, and re-layouts: 138 us -> 3.53 us
  other arithmetic: 71.5 us -> 0 us
  matrix products: 53.6 us -> 0 us
  starting transfers between devices: 72.6 us -> 31.3 us
  blocking collectives: 23.5 us -> 53.5 us
  waiting for transfers between devices: 91.3 us -> 69.3 us
  between operations: 15.3 us -> 0.76 us
    pallas_call x0 -> x7, Pallas kernels: none -> 158 us  [the longest x2 111 us: pick(): pl.pallas_call(functools.partial(pick_body, lo, size), out_shape=jax.Shap...]
    all_to_all x14 -> x4, waiting for transfers between devices: 91.3 us -> 18.9 us  [exchange(): return lax.all_to_all(x, 'expert', split_axis=0, concat_axis=0, tiled=True)]
    unnamed x127 -> x12, local copies, waits for them, and re-layouts: 56.8 us -> 2.84 us
    dot_general x12 -> x0, matrix products: 53.6 us -> none  [the longest x2 12.7 us: on_device(): lax.dot_general(arrived, pre_grad, (((0,), (0,)), ((), ())), preferred_el...]
    ppermute x0 -> x6, waiting for transfers between devices: none -> 50.4 us  [shifted(): return lax.ppermute(x, 'dp', [(i, (i + by) % REP) for i in range(REP)])]
    all_to_all x14 -> x4, starting transfers between devices: 72.3 us -> 23.6 us  [exchange(): return lax.all_to_all(x, 'expert', split_axis=0, concat_axis=0, tiled=True)]
    all_to_all x1, blocking collectives: 23.5 us -> 53.5 us  [exchange(): return lax.all_to_all(x, 'expert', split_axis=0, concat_axis=0, tiled=True)]
    convert_element_type x13 -> x0, other arithmetic: 29.8 us -> none  [the longest x2 11.5 us: adam_update(): second_new = beta_two * second + (1.0 - beta_two) * gradient * gradient]
  transfers between devices with their start and end apart: 16 -> 10, of which waited for: 11 -> 4; matrix products, arithmetic and copies ran while one was open for 46% -> 0% of each run, Pallas kernels for 0% -> 35%
where the time goes in v1:
time: 317 us
  Pallas kernels  158 us (50%)
  waiting for transfers between devices  69.3 us (22%)
  blocking collectives  53.5 us (17%)
  starting transfers between devices  31.3 us (10%)
  local copies, waits for them, and re-layouts  3.53 us (1%)
    pallas_call x2, Pallas kernels, pick(): pl.pallas_call(functools.partial(pick_body, lo, size), out_shape=jax.Shap...  111 us
    all_to_all x1, blocking collectives, exchange(): return lax.all_to_all(x, 'expert', split_axis=0, concat_axis=0, tiled=True)  53.5 us
    ppermute x6, waiting for transfers between devices, shifted(): return lax.ppermute(x, 'dp', [(i, (i + by) % REP) for i in range(REP)])  50.4 us
    pallas_call x1, Pallas kernels, expert(): pl.pallas_call(expert_body, out_shape=(jax.ShapeDtypeStruct(rows.shape, b...  25.6 us
    all_to_all x4, starting transfers between devices, exchange(): return lax.all_to_all(x, 'expert', split_axis=0, concat_axis=0, tiled=True)  23.6 us
    all_to_all x4, waiting for transfers between devices, exchange(): return lax.all_to_all(x, 'expert', split_axis=0, concat_axis=0, tiled=True)  18.9 us
    ppermute x6, starting transfers between devices, shifted(): return lax.ppermute(x, 'dp', [(i, (i + by) % REP) for i in range(REP)])  7.75 us
    pallas_call x1, Pallas kernels, update(): pl.pallas_call(update_body, out_shape=(jax.ShapeDtypeStruct((RI, 2 * SIDE...  7.65 us
  transfers between devices with their start and end apart: 10, of which 4 were waited for; matrix products, arithmetic and copies ran while one was open for 0% of the time, Pallas kernels for 35%

profile of v1, /device:TPU:1, one launch (start us, length us, event | category | flops | bytes accessed | tf_op | source)
XLA Modules:
  0.0 316.6 jit_solution(47170052752439377)
XLA Ops:
  0.6 4.8 %pack.1 = bf16[768,2304]{1,0:T(8,128)(2,1)} custom-call(bf16[256,1536]{1,0:T(8,128)(2,1)} %bitcast.28, bf16[192,1024]{1,0:T(8,128)(2,1)} %bitcast.31, f32[256,1536]{1,0:T(8,128)} %bitcast.26, f32[192,1024]{1,0:T(8,128)} %bitcast.29, f32[256,1536]{1,0:T(8,128)} %bitcast.27, f32[192,1024]{1,0:T(8,128)} %bitcast.30), custom_call_target="tpu_custom_call" | custom-call | tf_op jit(solution)/shard_map/pack/pallas_call | solution.py:53
  5.5 53.5 %all_to_all.25.src = bf16[32,24,2304]{2,1,0:T(8,128)(2,1)} all-to-all(bf16[32,24,2304]{2,1,0:T(8,128)(2,1)} %bitcast.19), channel_id=1, replica_groups=mesh['expert'=32,'dp'=4] {'expert'}, dimensions={0} | all-to-all | bytes 7077888 | tf_op jit(solution)/shard_map/all_to_all | solution.py:34
  59.0 37.8 %pick.2 = bf16[32,24,768]{2,1,0:T(8,128)(2,1)} custom-call(s32[32]{0:T(128)} %plan.3, bf16[32,24,2304]{2,1,0:T(8,128)(2,1)} %all_to_all.25.src), custom_call_target="tpu_custom_call" | custom-call | tf_op jit(solution)/shard_map/pick/pallas_call | solution.py:73
  96.8 0.0 copy-start.5
  96.8 3.9 %all-to-all-start.1 = ((bf16[32,24,768]{2,1,0:T(8,128)(2,1)}), bf16[32,24,768]{2,1,0:T(8,128)(2,1)S(1)}, u32[]{:S(2)}, u32[]{:S(2)}) async-start(bf16[32,24,768]{2,1,0:T(8,128)(2,1)} %pick.2), calls=%async_computation.1 | async-start | bytes 2359296 | tf_op jit(solution)/shard_map/all_to_all | solution.py:34
  100.7 0.0 copy-done.5
  100.7 0.7 copy.19.plan
  101.4 4.9 %dispatch.1 = (bf16[32,64,1024]{2,1,0:T(8,128)(2,1)}, bf16[2,512,64]{2,1,0:T(8,128)(2,1)}, bf16[2,512,128]{2,1,0:T(8,128)(2,1)}) custom-call(s32[6,2,64]{2,1,0:T(2,128)} %bitcast.32, f32[6,2,64]{2,1,0:T(2,128)} %bitcast.33, s32[32,1]{1,0:T(8,128)} %copy.19.plan, bf16[2,64,1024]{2,1,0:T(8,128)(2,1)} %tokens.1, bf16[2,64,1024]{2,1,0:T(8,128)(2,1)} %cotangent.1), custom_call_target="tpu_custom_call" | custom-call | tf_op jit(solution)/shard_map/dispatch/pallas_call | solution.py:120
  106.3 13.1 %all-to-all-done.1 = bf16[32,24,768]{2,1,0:T(8,128)(2,1)S(1)} async-done(((bf16[32,24,768]{2,1,0:T(8,128)(2,1)}), bf16[32,24,768]{2,1,0:T(8,128)(2,1)S(1)}, u32[]{:S(2)}, u32[]{:S(2)}) %all-to-all-start.1) | async-done | bytes 1179680 | tf_op jit(solution)/shard_map/all_to_all | solution.py:34
  119.4 0.0 copy-start.1
  119.4 4.8 %all-to-all-start.2 = ((bf16[32,64,1024]{2,1,0:T(8,128)(2,1)}), bf16[32,64,1024]{2,1,0:T(8,128)(2,1)}, u32[]{:S(2)}, u32[]{:S(2)}) async-start(bf16[32,64,1024]{2,1,0:T(8,128)(2,1)} %get-tuple-element.31), calls=%async_computation.2 | async-start | bytes 8388608 | tf_op jit(solution)/shard_map/all_to_all | solution.py:34
  124.2 2.5 collective-permute-start.2
  126.8 0.5 collective-permute-start.1
  127.3 0.0 copy-done.1
  127.3 0.6 collective-permute-start
  127.9 73.5 %pick.3 = bf16[32,24,1536]{2,1,0:T(8,128)(2,1)} custom-call(s32[32]{0:T(128)} %plan.3, bf16[32,24,2304]{2,1,0:T(8,128)(2,1)} %all_to_all.25.src), custom_call_target="tpu_custom_call" | custom-call | tf_op jit(solution)/shard_map/pick/pallas_call | solution.py:73
  201.4 0.0 all-to-all-done.2.rows
  201.4 8.3 %all-to-all-start.3 = ((bf16[32,24,1536]{2,1,0:T(8,128)(2,1)}), bf16[32,24,1536]{2,1,0:T(8,128)(2,1)S(1)}, u32[]{:S(2)}, u32[]{:S(2)}) async-start(bf16[32,24,1536]{2,1,0:T(8,128)(2,1)} %pick.3), calls=%async_computation.3 | async-start | bytes 4718592 | tf_op jit(solution)/shard_map/all_to_all | solution.py:34
  209.8 0.0 collective-permute-done.2.w3
  209.8 0.0 collective-permute-done.1.w2
  209.8 0.0 collective-permute-done.w1
  209.8 25.6 %expert.1 = (bf16[32,64,1024]{2,1,0:T(8,128)(2,1)}, bf16[768,768]{1,0:T(8,128)(2,1)}, bf16[768,768]{1,0:T(8,128)(2,1)}, bf16[768,768]{1,0:T(8,128)(2,1)}, bf16[768,768]{1,0:T(8,128)(2,1)}) custom-call(s32[1]{0:T(128)} %bitcast.mine, bf16[32,64,1024]{2,1,0:T(8,128)(2,1)} %all-to-all-done.2.rows, bf16[768,768]{1,0:T(8,128)(2,1)} %bitcast.24, ...), custom_call_target="tpu_custom_call" | custom-call | flops 14499999744 | bytes 18000000 | tf_op jit(solution)/shard_map/expert/pallas_call | solution.py:238
  235.4 5.9 %all-to-all-done.3 = bf16[32,24,1536]{2,1,0:T(8,128)(2,1)S(1)} async-done(((bf16[32,24,1536]{2,1,0:T(8,128)(2,1)}), bf16[32,24,1536]{2,1,0:T(8,128)(2,1)S(1)}, u32[]{:S(2)}, u32[]{:S(2)}) %all-to-all-start.3) | async-done | bytes 2359328 | tf_op jit(solution)/shard_map/all_to_all | solution.py:34
  241.3 0.0 copy-start
  241.3 1.4 copy-done
  242.7 6.5 %all-to-all-start.4 = ((bf16[32,64,1024]{2,1,0:T(8,128)(2,1)}), bf16[32,64,1024]{2,1,0:T(8,128)(2,1)}, u32[]{:S(2)}, u32[]{:S(2)}) async-start(bf16[32,64,1024]{2,1,0:T(8,128)(2,1)} %get-tuple-element.36), calls=%async_computation.4 | async-start | bytes 8388608 | tf_op jit(solution)/shard_map/all_to_all | solution.py:34
  249.2 1.6 collective-permute-start.3
  250.8 1.7 collective-permute-start.4
  252.5 0.8 collective-permute-start.5
  253.3 24.6 %collective-permute-done.3.g1 = bf16[768,768]{1,0:T(8,128)(2,1)S(1)} collective-permute-done((bf16[768,768]{1,0:T(8,128)(2,1)}, bf16[768,768]{1,0:T(8,128)(2,1)S(1)}, u32[]{:S(2)}, u32[]{:S(2)}) %collective-permute-start.3) | collective-permute-done | bytes 1179680 | tf_op jit(solution)/shard_map/ppermute | solution.py:38
  277.9 0.0 copy-start.2
  277.9 25.7 %collective-permute-done.4.g2 = bf16[768,768]{1,0:T(8,128)(2,1)S(1)} collective-permute-done((bf16[768,768]{1,0:T(8,128)(2,1)}, bf16[768,768]{1,0:T(8,128)(2,1)S(1)}, u32[]{:S(2)}, u32[]{:S(2)}) %collective-permute-start.4) | collective-permute-done | bytes 1179680 | tf_op jit(solution)/shard_map/ppermute | solution.py:38
  303.7 0.0 copy-start.3
  303.7 0.0 collective-permute-done.5.g3
  303.7 0.0 copy-start.4
  303.7 0.0 copy-done.2
  303.7 1.0 copy-done.3
  304.7 0.4 copy-done.4
  305.1 7.7 %update.1 = (bf16[256,1536]{1,0:T(8,128)(2,1)}, bf16[192,1024]{1,0:T(8,128)(2,1)}, f32[256,1536]{1,0:T(8,128)}, f32[256,1536]{1,0:T(8,128)}, f32[192,1024]{1,0:T(8,128)}, /*index=5*/f32[192,1024]{1,0:T(8,128)}) custom-call(bf16[768,768]{1,0:T(8,128)(2,1)} %bitcast.25, bf16[768,1536]{1,0:T(8,128)(2,1)} %bitcast.20, bf16[768,768]{1,0:T(8,128)(2,1)} %get-tuple-element.42.g0, ...), custom_call_target="tpu_custom_call" | custom-call | tf_op jit(solution)/shard_map/update/pallas_call | solution.py:298
  312.8 0.0 all-to-all-done.4.back
  312.8 3.8 %combine.1 = (bf16[2,64,1024]{2,1,0:T(8,128)(2,1)}, bf16[2,64,1024]{2,1,0:T(8,128)(2,1)}) custom-call(bf16[32,64,1024]{2,1,0:T(8,128)(2,1)} %all-to-all-done.4.back, bf16[2,512,64]{2,1,0:T(8,128)(2,1)} %get-tuple-element.37.place, bf16[2,512,128]{2,1,0:T(8,128)(2,1)} %get-tuple-element.38.gated), custom_call_target="tpu_custom_call" | custom-call | tf_op jit(solution)/shard_map/combine/pallas_call | solution.py:151
Async XLA Ops:
  96.8 3.9 %copy-start.5 = (s32[32]{0:T(128)S(1)}, s32[32]{0:T(128)}, u32[]{:S(2)}) copy-start(s32[32]{0:T(128)} %plan.3) | copy-start | bytes 388
  96.8 22.5 %all-to-all-start.1 = ((bf16[32,24,768]{2,1,0:T(8,128)(2,1)}), bf16[32,24,768]{2,1,0:T(8,128)(2,1)S(1)}, u32[]{:S(2)}, u32[]{:S(2)}) async-start(bf16[32,24,768]{2,1,0:T(8,128)(2,1)} %pick.2), calls=%async_computation.1 | async-start | bytes 2359296 | tf_op jit(solution)/shard_map/all_to_all | solution.py:34
  119.4 7.9 %copy-start.1 = (bf16[32,24,768]{2,1,0:T(8,128)(2,1)}, bf16[32,24,768]{2,1,0:T(8,128)(2,1)S(1)}, u32[]{:S(2)}) copy-start(bf16[32,24,768]{2,1,0:T(8,128)(2,1)S(1)} %all-to-all-done.1) | copy-start | bytes 3538948
  119.4 82.1 %all-to-all-start.2 = ((bf16[32,64,1024]{2,1,0:T(8,128)(2,1)}), bf16[32,64,1024]{2,1,0:T(8,128)(2,1)}, u32[]{:S(2)}, u32[]{:S(2)}) async-start(bf16[32,64,1024]{2,1,0:T(8,128)(2,1)} %get-tuple-element.31), calls=%async_computation.2 | async-start | bytes 8388608 | tf_op jit(solution)/shard_map/all_to_all | solution.py:34
  124.2 85.6 %collective-permute-start.2 = (bf16[768,768]{1,0:T(8,128)(2,1)S(1)}, bf16[768,768]{1,0:T(8,128)(2,1)}, u32[]{:S(2)}, u32[]{:S(2)}) collective-permute-start(bf16[768,768]{1,0:T(8,128)(2,1)S(1)} %bitcast.21), channel_id=1, source_target_pairs={{0,3},{1,0},{2,1},{3,2},{4,7},{5,4},{6,5},{7,6},{8,11},{9,8},{10,9... | collective-permute-start | bytes 3538952 | tf_op jit(solution)/shard_map/ppermute | solution.py:38
  126.8 83.1 %collective-permute-start.1 = (bf16[768,768]{1,0:T(8,128)(2,1)S(1)}, bf16[768,768]{1,0:T(8,128)(2,1)}, u32[]{:S(2)}, u32[]{:S(2)}) collective-permute-start(bf16[768,768]{1,0:T(8,128)(2,1)S(1)} %bitcast.22), channel_id=1, source_target_pairs={{0,2},{1,3},{2,0},{3,1},{4,6},{5,7},{6,4},{7,5},{8,10},{9,11},{10,... | collective-permute-start | bytes 3538952 | tf_op jit(solution)/shard_map/ppermute | solution.py:38
  127.3 82.5 %collective-permute-start = (bf16[768,768]{1,0:T(8,128)(2,1)S(1)}, bf16[768,768]{1,0:T(8,128)(2,1)}, u32[]{:S(2)}, u32[]{:S(2)}) collective-permute-start(bf16[768,768]{1,0:T(8,128)(2,1)S(1)} %bitcast.23), channel_id=1, source_target_pairs={{0,1},{1,2},{2,3},{3,0},{4,5},{5,6},{6,7},{7,4},{8,9},{9,10},{10,1... | collective-permute-start | bytes 3538952 | tf_op jit(solution)/shard_map/ppermute | solution.py:38
  201.4 39.9 %all-to-all-start.3 = ((bf16[32,24,1536]{2,1,0:T(8,128)(2,1)}), bf16[32,24,1536]{2,1,0:T(8,128)(2,1)S(1)}, u32[]{:S(2)}, u32[]{:S(2)}) async-start(bf16[32,24,1536]{2,1,0:T(8,128)(2,1)} %pick.3), calls=%async_computation.3 | async-start | bytes 4718592 | tf_op jit(solution)/shard_map/all_to_all | solution.py:34
  241.3 1.4 copy-start
  242.7 70.1 %all-to-all-start.4 = ((bf16[32,64,1024]{2,1,0:T(8,128)(2,1)}), bf16[32,64,1024]{2,1,0:T(8,128)(2,1)}, u32[]{:S(2)}, u32[]{:S(2)}) async-start(bf16[32,64,1024]{2,1,0:T(8,128)(2,1)} %get-tuple-element.36), calls=%async_computation.4 | async-start | bytes 8388608 | tf_op jit(solution)/shard_map/all_to_all | solution.py:34
  249.2 28.7 %collective-permute-start.3 = (bf16[768,768]{1,0:T(8,128)(2,1)}, bf16[768,768]{1,0:T(8,128)(2,1)S(1)}, u32[]{:S(2)}, u32[]{:S(2)}) collective-permute-start(bf16[768,768]{1,0:T(8,128)(2,1)} %get-tuple-element.43), channel_id=1, source_target_pairs={{0,1},{1,2},{2,3},{3,0},{4,5},{5,6},{6,7},{7,4},{8,9},{9,10},{10,1... | collective-permute-start | bytes 3538952 | tf_op jit(solution)/shard_map/ppermute | solution.py:38
  250.8 52.9 %collective-permute-start.4 = (bf16[768,768]{1,0:T(8,128)(2,1)}, bf16[768,768]{1,0:T(8,128)(2,1)S(1)}, u32[]{:S(2)}, u32[]{:S(2)}) collective-permute-start(bf16[768,768]{1,0:T(8,128)(2,1)} %get-tuple-element.44), channel_id=1, source_target_pairs={{0,2},{1,3},{2,0},{3,1},{4,6},{5,7},{6,4},{7,5},{8,10},{9,11},{10,... | collective-permute-start | bytes 3538952 | tf_op jit(solution)/shard_map/ppermute | solution.py:38
  252.5 51.1 %collective-permute-start.5 = (bf16[768,768]{1,0:T(8,128)(2,1)}, bf16[768,768]{1,0:T(8,128)(2,1)S(1)}, u32[]{:S(2)}, u32[]{:S(2)}) collective-permute-start(bf16[768,768]{1,0:T(8,128)(2,1)} %get-tuple-element.45), channel_id=1, source_target_pairs={{0,3},{1,0},{2,1},{3,2},{4,7},{5,4},{6,5},{7,6},{8,11},{9,8},{10,9... | collective-permute-start | bytes 3538952 | tf_op jit(solution)/shard_map/ppermute | solution.py:38
  277.9 25.8 %copy-start.2 = (bf16[768,768]{1,0:T(8,128)(2,1)}, bf16[768,768]{1,0:T(8,128)(2,1)S(1)}, u32[]{:S(2)}) copy-start(bf16[768,768]{1,0:T(8,128)(2,1)S(1)} %collective-permute-done.3.g1) | copy-start | bytes 3538948
  303.7 1.0 copy-start.3
  303.7 1.4 copy-start.4

commit v2 on v1

--- a/solution.py
+++ b/solution.py
@@ -1,11 +1,10 @@
-import functools
-
 import jax
 import jax.numpy as jnp
 from jax import lax
 from jax.experimental import pallas as pl
 from jax.experimental.pallas import tpu as pltpu
 from jax.sharding import PartitionSpec as P
+
 
 beta_one = 0.9
 beta_two = 0.95
@@ -22,6 +21,8 @@
 COUNT = 32
 CAP = 16
 ROWS = 2 * CAP
+HALF = SIDE // 2
+CHUNKS = 2
 
 f32 = jnp.float32
 bf16 = jnp.bfloat16
@@ -30,6 +31,10 @@
 ANY = pl.BlockSpec(memory_space=pl.ANY)
 
 
+ROW_T = (((0,), (0,)), ((), ()))
+COL_T = (((1,), (1,)), ((), ()))
+
+
 def exchange(x):
     return lax.all_to_all(x, "expert", split_axis=0, concat_axis=0, tiled=True)
 
@@ -38,8 +43,12 @@
     return lax.ppermute(x, "dp", [(i, (i + by) % REP) for i in range(REP)])
 
 
+def both(a, b):
+    return (a.astype(f32) + b.astype(f32)).astype(bf16)
+
+
 def pack_body(w_in, w_out, f_in, f_out, s_in, s_out, out):
-    for j, (a, b) in enumerate(((w_in, w_out), (f_in, f_out), (s_in, s_out))):
+    for j, (a, b) in enumerate(((f_in, f_out), (s_in, s_out), (w_in, w_out))):
         lanes = slice(j * SIDE, (j + 1) * SIDE)
         out[0:RI, lanes] = a[:, :SIDE].astype(bf16)
         out[RI : 2 * RI, lanes] = a[:, SIDE:].astype(bf16)
@@ -59,23 +68,22 @@
     )(w_in, w_out, f_in, f_out, s_in, s_out)
 
 
-def pick_body(lo, size, plan, src, out, sem):
-    copies = [
-        pltpu.make_async_copy(src.at[plan[d], :, lo : lo + size], out.at[d], sem.at[d]) for d in range(COUNT)
-    ]
-    for c in copies:
-        c.start()
-    for c in copies:
-        c.wait()
+def pick_body(plan, src, out):
+    def step(d, carry):
+        out[d] = src[plan[d]]
+        return carry
+
+    lax.fori_loop(0, COUNT, step, 0, unroll=True)
 
 
 def pick(plan, src, lo, size):
-    return pl.pallas_call(
-        functools.partial(pick_body, lo, size),
-        out_shape=jax.ShapeDtypeStruct((COUNT, SIDE // COUNT, size), bf16),
-        in_specs=[SMEM, ANY],
-        out_specs=ANY,
-        scratch_shapes=[pltpu.SemaphoreType.DMA((COUNT,))],
+    shape = (COUNT, SIDE // COUNT, size)
+    return pl.pallas_call(
+        pick_body,
+        grid=(1,),
+        out_shape=jax.ShapeDtypeStruct(shape, bf16),
+        in_specs=[SMEM, pl.BlockSpec(shape, lambda i: (0, 0, lo // size))],
+        out_specs=pl.BlockSpec(shape, lambda i: (0, 0, 0)),
         name="pick",
     )(plan, src)
 
@@ -86,6 +94,9 @@
     holder = plan[...]
     earlier = (
         lax.broadcasted_iota(jnp.int32, (n, n), 0) < lax.broadcasted_iota(jnp.int32, (n, n), 1)
+    ).astype(bf16)
+    same = (
+        lax.broadcasted_iota(jnp.int32, (n, n), 0) == lax.broadcasted_iota(jnp.int32, (n, n), 1)
     ).astype(bf16)
     slot = lax.broadcasted_iota(jnp.int32, (COUNT, CAP, n), 1).astype(f32)
     for m in range(2):
@@ -106,9 +117,9 @@
         chosen = chosen.astype(bf16)
         high = weighted.astype(bf16)
         low = (weighted - high.astype(f32)).astype(bf16)
-        place[m] = chosen
-        gated[m, :, :n] = high
-        gated[m, :, n:] = low
+        place[m] = lax.dot_general(same, chosen, COL_T, preferred_element_type=f32).astype(bf16)
+        gated[m, :n] = lax.dot_general(same, high, COL_T, preferred_element_type=f32).astype(bf16)
+        gated[m, n:] = lax.dot_general(same, low, COL_T, preferred_element_type=f32).astype(bf16)
         sent = jnp.dot(chosen, tokens[m], preferred_element_type=f32).astype(bf16)
         out[:, CAP * m : CAP * m + CAP, :] = sent.reshape(COUNT, CAP, -1)
         grads = jnp.dot(chosen, cotangent[m], preferred_element_type=f32) * column
@@ -121,8 +132,8 @@
         dispatch_body,
         out_shape=(
             jax.ShapeDtypeStruct((COUNT, 2 * ROWS, width), bf16),
-            jax.ShapeDtypeStruct((2, COUNT * CAP, n), bf16),
-            jax.ShapeDtypeStruct((2, COUNT * CAP, 2 * n), bf16),
+            jax.ShapeDtypeStruct((2, n, COUNT * CAP), bf16),
+            jax.ShapeDtypeStruct((2, 2 * n, COUNT * CAP), bf16),
         ),
         in_specs=[VMEM] * 5,
         out_specs=(VMEM, VMEM, VMEM),
@@ -130,54 +141,78 @@
     )(routes, gates, plan, tokens, cotangent)
 
 
-ROW_T = (((0,), (0,)), ((), ()))
-COL_T = (((1,), (1,)), ((), ()))
-
-
-def combine_body(back, place, gated, layer, token):
+def combine_body(back, place, gated, layer, token, buf, sem):
     n = layer.shape[1]
+    size = COUNT // CHUNKS
+    copies = [
+        pltpu.make_async_copy(back.at[i * size : (i + 1) * size], buf.at[i], sem.at[i]) for i in range(CHUNKS)
+    ]
+    for c in copies:
+        c.start()
+    sums = [None] * 4
+    for i, c in enumerate(copies):
+        c.wait()
+        slots = slice(i * size * CAP, (i + 1) * size * CAP)
+        for m in range(2):
+            for j, (table, at) in enumerate(((gated, 0), (place, ROWS))):
+                rows = buf[i, :, at + CAP * m : at + CAP * m + CAP, :].reshape(size * CAP, -1)
+                part = jnp.dot(table[m, :, slots], rows, preferred_element_type=f32)
+                sums[2 * j + m] = part if i == 0 else sums[2 * j + m] + part
     for m in range(2):
-        rows = back[:, CAP * m : CAP * m + CAP, :].reshape(COUNT * CAP, -1)
-        both = lax.dot_general(gated[m], rows, ROW_T, preferred_element_type=f32)
-        layer[m] = (both[:n] + both[n:]).astype(bf16)
-        rows = back[:, ROWS + CAP * m : ROWS + CAP * m + CAP, :].reshape(COUNT * CAP, -1)
-        token[m] = lax.dot_general(place[m], rows, ROW_T, preferred_element_type=f32).astype(bf16)
+        layer[m] = (sums[m][:n] + sums[m][n:]).astype(bf16)
+        token[m] = sums[2 + m].astype(bf16)
 
 
 def combine(back, place, gated):
-    n = place.shape[2]
+    n = place.shape[1]
     width = back.shape[2]
     shape = jax.ShapeDtypeStruct((2, n, width), bf16)
     return pl.pallas_call(
         combine_body,
         out_shape=(shape, shape),
-        in_specs=[VMEM] * 3,
+        in_specs=[ANY, VMEM, VMEM],
         out_specs=(VMEM, VMEM),
+        scratch_shapes=[
+            pltpu.VMEM((CHUNKS, COUNT // CHUNKS, 2 * ROWS, width), bf16),
+            pltpu.SemaphoreType.DMA((CHUNKS,)),
+        ],
         name="combine",
     )(back, place, gated)
 
 
-def expert_body(mine, rows, w0, w1, w2, w3, back, g0, g1, g2, g3, win, wout, hid, pgrad, gout, gpack, sem, gsem):
+def expert_body(mine, rows, w0, w1, w2a, w2b, w3, back, g0, g1t, g1b, g2t, g2b, g3t, g3b, win, wout, hid, pgrad, gout, gpack, sem, gsem):
     r = mine[0]
     copies = []
-    for s, w in enumerate((w0, w1, w2, w3)):
+
+    def fetch(s, w, lo, hi, src):
         q = (r - s + REP) % REP
         at = pl.multiple_of(q * RI, RI)
         to = pl.multiple_of(q * RO, RT)
-        pieces = [
-            (w.at[0:RI], win.at[pl.ds(at, RI), 0:SIDE]),
-            (w.at[RI : 2 * RI], win.at[pl.ds(at, RI), SIDE : 2 * SIDE]),
-            (w.at[2 * RI : 2 * RI + RO], wout.at[pl.ds(to, RO), 0:SIDE]),
-        ]
-        for i in range(3):
-            pieces.append(
-                (
-                    w.at[2 * RI + RO : SIDE, 256 * i : 256 * i + 256],
-                    wout.at[pl.ds(to + RT * i, RT), SIDE : SIDE + 256],
+        pieces = []
+        for base, end, ref, first, lanes in (
+            (0, RI, win, at, 0),
+            (RI, 2 * RI, win, at, SIDE),
+            (2 * RI, 2 * RI + RO, wout, to, 0),
+        ):
+            l, h = max(lo, base), min(hi, end)
+            if l < h:
+                start = pl.multiple_of(first + (l - base), RT)
+                pieces.append((w.at[l - lo + src : h - lo + src], ref.at[pl.ds(start, h - l), lanes : lanes + SIDE]))
+        if hi == SIDE:
+            for i in range(3):
+                l = 2 * RI + RO - lo + src
+                start = pl.multiple_of(to + RT * i, RT)
+                pieces.append(
+                    (w.at[l : l + RT, 256 * i : 256 * i + 256], wout.at[pl.ds(start, RT), SIDE : SIDE + 256])
                 )
-            )
-        for a, b in pieces:
-            copies.append(pltpu.make_async_copy(a, b, sem.at[len(copies)]))
+        for x, y in pieces:
+            copies.append(pltpu.make_async_copy(x, y, sem.at[len(copies)]))
+
+    fetch(0, w0, 0, SIDE, 0)
+    fetch(1, w1, 0, SIDE, 0)
+    fetch(2, w2a, 0, HALF, 0)
+    fetch(2, w2b, HALF, SIDE, 0)
+    fetch(3, w3, 0, SIDE, 0)
     for c in copies:
         c.start()
     for c in copies:
@@ -222,9 +257,11 @@
         gpack[q, 2 * RI : 2 * RI + RO, :] = gout[RO * q : RO * q + RO, :SIDE]
         for i in range(3):
             gpack[q, 2 * RI + RO :, 256 * i : 256 * i + 256] = gout[RO * q + RT * i : RO * q + RT * i + RT, SIDE:]
-    copies = [
-        pltpu.make_async_copy(gpack.at[(r + s) % REP], out, gsem.at[s]) for s, out in enumerate((g0, g1, g2, g3))
-    ]
+    copies = [pltpu.make_async_copy(gpack.at[r], g0, gsem.at[0])]
+    for s, t, b in ((2, g2t, g2b), (1, g1t, g1b), (3, g3t, g3b)):
+        q = (r + s) % REP
+        for out, at in ((t, 0), (b, HALF)):
+            copies.append(pltpu.make_async_copy(gpack.at[q, at : at + HALF], out, gsem.at[len(copies)]))
     for c in copies:
         c.start()
     for c in copies:
@@ -234,12 +271,13 @@
 def expert(mine, rows, parts):
     width = rows.shape[2]
     piece = jax.ShapeDtypeStruct((SIDE, SIDE), bf16)
+    half = jax.ShapeDtypeStruct((HALF, SIDE), bf16)
     total = COUNT * ROWS
     return pl.pallas_call(
         expert_body,
-        out_shape=(jax.ShapeDtypeStruct(rows.shape, bf16), piece, piece, piece, piece),
-        in_specs=[SMEM, VMEM, ANY, ANY, ANY, ANY],
-        out_specs=(VMEM, ANY, ANY, ANY, ANY),
+        out_shape=(jax.ShapeDtypeStruct(rows.shape, bf16), piece) + (half,) * 6,
+        in_specs=[SMEM, VMEM] + [ANY] * 5,
+        out_specs=(VMEM,) + (ANY,) * 7,
         scratch_shapes=[
             pltpu.VMEM((REP * RI, 2 * SIDE), bf16),
             pltpu.VMEM((REP * RO, width), bf16),
@@ -247,8 +285,8 @@
             pltpu.VMEM((total, 2 * SIDE), bf16),
             pltpu.VMEM((SIDE, width), bf16),
             pltpu.VMEM((REP, SIDE, SIDE), bf16),
-            pltpu.SemaphoreType.DMA((24,)),
-            pltpu.SemaphoreType.DMA((REP,)),
+            pltpu.SemaphoreType.DMA((25,)),
+            pltpu.SemaphoreType.DMA((2 * REP - 1,)),
         ],
         cost_estimate=pl.CostEstimate(flops=14_500_000_000, bytes_accessed=18_000_000, transcendentals=800_000),
         name="expert",
@@ -271,11 +309,13 @@
     )
 
 
-def update_body(w, moments, g0, g1, g2, g3, w_in, w_out, f_in, s_in, f_out, s_out):
+def update_body(w, moments, g0, g1t, g1b, g3t, g3b, w_in, w_out, f_in, s_in, f_out, s_out):
     def one(rows, lanes, outs, at, to):
+        base = rows.start // HALF * HALF
+        here = slice(rows.start - base, rows.stop - base)
         grad = g0[rows, lanes].astype(f32)
-        for g in (g1, g2, g3):
-            grad = grad + g[rows, lanes].astype(f32)
+        for g in (g1b, g3b) if base else (g1t, g3t):
+            grad = grad + g[here, lanes].astype(f32)
         second = slice(lanes.start + SIDE, lanes.stop + SIDE)
         new = adam(w[rows, lanes], grad, moments[rows, lanes].astype(f32), moments[rows, second].astype(f32))
         for o, v in zip(outs, new):
@@ -305,7 +345,7 @@
             jax.ShapeDtypeStruct((RO, 1024), f32),
             jax.ShapeDtypeStruct((RO, 1024), f32),
         ),
-        in_specs=[VMEM] * 6,
+        in_specs=[VMEM] * 7,
         out_specs=(VMEM,) * 6,
         name="update",
     )(w, moments, *grads)
@@ -327,19 +367,28 @@
     mine = lax.axis_index("dp").astype(jnp.int32).reshape(1)
     packed = pack(weight_in[0], weight_out[0], first_in[0], first_out[0], second_in[0], second_out[0])
     spread = exchange(packed.reshape(COUNT, SIDE // COUNT, 3 * SIDE))
-    own = exchange(pick(expert_plan, spread, 0, SIDE)).reshape(SIDE, SIDE)
+    own = exchange(pick(expert_plan, spread, 2 * SIDE, SIDE)).reshape(SIDE, SIDE)
     outgoing, place, gated = dispatch(
         routes.transpose(2, 0, 1), gate_weights.transpose(2, 0, 1), expert_plan.reshape(-1, 1), tokens, cotangent
     )
     outgoing, own = lax.optimization_barrier((outgoing, own))
-    parts = (own, shifted(own, 1), shifted(own, 2), shifted(own, 3))
+    before = shifted(own, 1)
+    after = shifted(own, 3)
+    top = shifted(before[:HALF], 1)
+    bottom = shifted(after[HALF:], 3)
+    parts = (own, before, top, bottom, after)
     arrived = exchange(outgoing)
-    moved = pick(expert_plan, spread, SIDE, 2 * SIDE)
+    moved = pick(expert_plan, spread, 0, 2 * SIDE)
     arrived, moved = lax.optimization_barrier((arrived, moved))
     moments = exchange(moved).reshape(SIDE, 2 * SIDE)
-    back, g0, g1, g2, g3 = expert(mine, arrived, parts)
-    back, moments = lax.optimization_barrier((back, moments))
-    grads = (g0, shifted(g1, 1), shifted(g2, 2), shifted(g3, 3))
+    back, g0, g1t, g1b, g2t, g2b, g3t, g3b = expert(mine, arrived, parts)
+    from_before = shifted(g2t, 1)
+    from_after = shifted(g2b, 3)
+    h1b = shifted(g1b, 1)
+    h3t = shifted(g3t, 3)
+    h1t = shifted(both(g1t, from_before), 1)
+    h3b = shifted(both(g3b, from_after), 3)
+    grads = (g0, h1t, h1b, h3t, h3b)
     returned = exchange(back)
     new_in, new_out, first_in_new, second_in_new, first_out_new, second_out_new = update(own, moments, grads)
     layer, token = combine(returned, place, gated)

time: 317 us -> 263 us (0.83)
  Pallas kernels: 158 us -> 52.7 us
  waiting for transfers between devices: 69.3 us -> 106 us
  starting transfers between devices: 31.3 us -> 38.6 us
  local copies, waits for them, and re-layouts: 3.53 us -> 7 us
    pallas_call x3, Pallas kernels: 115 us -> 10.4 us  [the longest x2 5.64 us: pick(): pl.pallas_call(pick_body, grid=(1,), out_shape=jax.ShapeDtypeStruct(shape...]
    all_to_all x4, waiting for transfers between devices: 18.9 us -> 59 us  [exchange(): return lax.all_to_all(x, 'expert', split_axis=0, concat_axis=0, tiled=True)]
    ppermute x6 -> x10, starting transfers between devices: 7.75 us -> 13.7 us  [shifted(): return lax.ppermute(x, 'dp', [(i, (i + by) % REP) for i in range(REP)])]
    ppermute x6 -> x10, waiting for transfers between devices: 50.4 us -> 47.1 us  [shifted(): return lax.ppermute(x, 'dp', [(i, (i + by) % REP) for i in range(REP)])]
  transfers between devices with their start and end apart: 10 -> 14, of which waited for: 4 -> 8; matrix products, arithmetic and copies ran while one was open for 0% -> 2% of each run, Pallas kernels for 35% -> 16%
where the time goes in v2:
time: 263 us; the launch traced here: 260 us
  waiting for transfers between devices  106 us (40%)
  blocking collectives  53.5 us (20%)
  Pallas kernels  52.7 us (20%)
  starting transfers between devices  38.6 us (15%)
  local copies, waits for them, and re-layouts  7 us (3%)
    all_to_all x4, waiting for transfers between devices, exchange(): return lax.all_to_all(x, 'expert', split_axis=0, concat_axis=0, tiled=True)  59 us
    all_to_all x1, blocking collectives, exchange(): return lax.all_to_all(x, 'expert', split_axis=0, concat_axis=0, tiled=True)  53.5 us
    ppermute x10, waiting for transfers between devices, shifted(): return lax.ppermute(x, 'dp', [(i, (i + by) % REP) for i in range(REP)])  47.1 us
    pallas_call x1, Pallas kernels, expert(): pl.pallas_call(expert_body, out_shape=(jax.ShapeDtypeStruct(rows.shape, b...  25.5 us
    all_to_all x4, starting transfers between devices, exchange(): return lax.all_to_all(x, 'expert', split_axis=0, concat_axis=0, tiled=True)  24.9 us
    ppermute x10, starting transfers between devices, shifted(): return lax.ppermute(x, 'dp', [(i, (i + by) % REP) for i in range(REP)])  13.7 us
    pallas_call x1, Pallas kernels, update(): pl.pallas_call(update_body, out_shape=(jax.ShapeDtypeStruct((RI, 2 * SIDE...  7.1 us
    pallas_call x2, Pallas kernels, pick(): pl.pallas_call(pick_body, grid=(1,), out_shape=jax.ShapeDtypeStruct(shape...  5.64 us
  transfers between devices with their start and end apart: 14, of which 8 were waited for; matrix products, arithmetic and copies ran while one was open for 2% of the time, Pallas kernels for 16%

profile of v2, /device:TPU:1, one launch (start us, length us, event | category | flops | bytes accessed | tf_op | source)
XLA Modules:
  0.0 260.2 jit_solution(12021137040267433964)
XLA Ops:
  0.6 4.7 %pack.1 = bf16[768,2304]{1,0:T(8,128)(2,1)} custom-call(bf16[256,1536]{1,0:T(8,128)(2,1)} %bitcast.27, bf16[192,1024]{1,0:T(8,128)(2,1)} %bitcast.30, f32[256,1536]{1,0:T(8,128)} %bitcast.25, f32[192,1024]{1,0:T(8,128)} %bitcast.28, f32[256,1536]{1,0:T(8,128)} %bitcast.26, f32[192,1024]{1,0:T(8,128)} %bitcast.29), custom_call_target="tpu_custom_call" | custom-call | tf_op jit(solution)/shard_map/pack/pallas_call | solution.py:62
  5.4 53.5 %all_to_all.25.src = bf16[32,24,2304]{2,1,0:T(8,128)(2,1)} all-to-all(bf16[32,24,2304]{2,1,0:T(8,128)(2,1)} %bitcast.19), channel_id=1, replica_groups=mesh['expert'=32,'dp'=4] {'expert'}, dimensions={0} | all-to-all | bytes 7077888 | tf_op jit(solution)/shard_map/all_to_all | solution.py:39
  58.9 2.4 pick.2
  61.3 0.0 copy-start.7
  61.3 4.0 %all-to-all-start.1 = ((bf16[32,24,768]{2,1,0:T(8,128)(2,1)}), bf16[32,24,768]{2,1,0:T(8,128)(2,1)S(1)}, u32[]{:S(2)}, u32[]{:S(2)}) async-start(bf16[32,24,768]{2,1,0:T(8,128)(2,1)} %pick.2), calls=%async_computation.1 | async-start | bytes 2359296 | tf_op jit(solution)/shard_map/all_to_all | solution.py:39
  65.3 0.0 copy-done.7
  65.3 0.7 copy.19.plan
  66.0 4.9 %dispatch.1 = (bf16[32,64,1024]{2,1,0:T(8,128)(2,1)}, bf16[2,64,512]{2,1,0:T(8,128)(2,1)}, bf16[2,128,512]{2,1,0:T(8,128)(2,1)}) custom-call(s32[6,2,64]{2,1,0:T(2,128)} %bitcast.31, f32[6,2,64]{2,1,0:T(2,128)} %bitcast.32, s32[32,1]{1,0:T(8,128)} %copy.19.plan, bf16[2,64,1024]{2,1,0:T(8,128)(2,1)} %tokens.1, bf16[2,64,1024]{2,1,0:T(8,128)(2,1)} %cotangent.1), custom_call_target="tpu_custom_call" | custom-call | tf_op jit(solution)/shard_map/dispatch/pallas_call | solution.py:131
  71.0 13.0 %all-to-all-done.1 = bf16[32,24,768]{2,1,0:T(8,128)(2,1)S(1)} async-done(((bf16[32,24,768]{2,1,0:T(8,128)(2,1)}), bf16[32,24,768]{2,1,0:T(8,128)(2,1)S(1)}, u32[]{:S(2)}, u32[]{:S(2)}) %all-to-all-start.1) | async-done | bytes 1179680 | tf_op jit(solution)/shard_map/all_to_all | solution.py:39
  84.0 0.0 copy-start.1
  84.0 4.8 %all-to-all-start.2 = ((bf16[32,64,1024]{2,1,0:T(8,128)(2,1)}), bf16[32,64,1024]{2,1,0:T(8,128)(2,1)}, u32[]{:S(2)}, u32[]{:S(2)}) async-start(bf16[32,64,1024]{2,1,0:T(8,128)(2,1)} %get-tuple-element.32), calls=%async_computation.2 | async-start | bytes 8388608 | tf_op jit(solution)/shard_map/all_to_all | solution.py:39
  88.8 2.5 collective-permute-start.2
  91.4 0.0 copy-done.1
  91.4 0.0 collective-permute-start
  91.4 3.3 %pick.3 = bf16[32,24,1536]{2,1,0:T(8,128)(2,1)} custom-call(s32[32]{0:T(128)} %plan.3, bf16[32,24,2304]{2,1,0:T(8,128)(2,1)} %all_to_all.25.src), custom_call_target="tpu_custom_call" | custom-call | tf_op jit(solution)/shard_map/pick/pallas_call | solution.py:81
  94.6 44.9 %all-to-all-done.2.rows = bf16[32,64,1024]{2,1,0:T(8,128)(2,1)} async-done(((bf16[32,64,1024]{2,1,0:T(8,128)(2,1)}), bf16[32,64,1024]{2,1,0:T(8,128)(2,1)}, u32[]{:S(2)}, u32[]{:S(2)}) %all-to-all-start.2) | async-done | bytes 4194336 | tf_op jit(solution)/shard_map/all_to_all | solution.py:39
  139.5 7.4 %all-to-all-start.4 = ((bf16[32,24,1536]{2,1,0:T(8,128)(2,1)}), bf16[32,24,1536]{2,1,0:T(8,128)(2,1)S(1)}, u32[]{:S(2)}, u32[]{:S(2)}) async-start(bf16[32,24,1536]{2,1,0:T(8,128)(2,1)} %pick.3), calls=%async_computation.4 | async-start | bytes 4718592 | tf_op jit(solution)/shard_map/all_to_all | solution.py:39
  146.9 0.0 collective-permute-done.2.w3
  146.9 1.9 slice.9
  148.8 2.5 collective-permute-start.3
  151.3 0.0 collective-permute-done.w1
  151.3 1.1 slice.8
  152.4 0.3 collective-permute-start.1
  152.7 11.3 %collective-permute-done.3.w2b = bf16[384,768]{1,0:T(8,128)(2,1)} collective-permute-done((bf16[384,768]{1,0:T(8,128)(2,1)}, bf16[384,768]{1,0:T(8,128)(2,1)}, u32[]{:S(2)}, u32[]{:S(2)}) %collective-permute-start.3) | collective-permute-done | bytes 589856 | tf_op jit(solution)/shard_map/ppermute | solution.py:43
  164.0 4.2 %collective-permute-done.1.w2a = bf16[384,768]{1,0:T(8,128)(2,1)S(1)} collective-permute-done((bf16[384,768]{1,0:T(8,128)(2,1)S(1)}, bf16[384,768]{1,0:T(8,128)(2,1)S(1)}, u32[]{:S(2)}, u32[]{:S(2)}) %collective-permute-start.1) | collective-permute-done | bytes 589856 | tf_op jit(solution)/shard_map/ppermute | solution.py:43
  168.1 0.0 copy-start.8
  168.1 0.8 copy-done.8
  169.0 25.5 %expert.1 = (bf16[32,64,1024]{2,1,0:T(8,128)(2,1)}, bf16[768,768]{1,0:T(8,128)(2,1)}, bf16[384,768]{1,0:T(8,128)(2,1)}, bf16[384,768]{1,0:T(8,128)(2,1)}, bf16[3...) custom-call(s32[1]{0:T(128)} %bitcast.mine, ...), custom_call_target="tpu_custom_call" | custom-call | flops 14499999744 | bytes 18000000 | tf_op jit(solution)/shard_map/expert/pallas_call | solution.py:276
  194.5 0.0 all-to-all-done.4
  194.5 0.0 copy-start
  194.5 1.4 copy-done
  196.0 8.7 %all-to-all-start.3 = ((bf16[32,64,1024]{2,1,0:T(8,128)(2,1)}), bf16[32,64,1024]{2,1,0:T(8,128)(2,1)}, u32[]{:S(2)}, u32[]{:S(2)}) async-start(bf16[32,64,1024]{2,1,0:T(8,128)(2,1)} %get-tuple-element.35), calls=%async_computation.3 | async-start | bytes 8388608 | tf_op jit(solution)/shard_map/all_to_all | solution.py:39
  204.6 0.0 copy-start.6
  204.6 0.1 collective-permute-start.4
  204.7 2.7 %collective-permute-start.8 = (bf16[384,768]{1,0:T(8,128)(2,1)}, bf16[384,768]{1,0:T(8,128)(2,1)S(1)}, u32[]{:S(2)}, u32[]{:S(2)}) collective-permute-start(bf16[384,768]{1,0:T(8,128)(2,1)} %get-tuple-element.47), channel_id=1, source_target_pairs={{0,3},{1,0},{2,1},{3,2},{4,7},{5,4},{6,5},{7,6},{8,11},{9,8},{10,9... | collective-permute-start | bytes 1769480 | tf_op jit(solution)/shard_map/ppermute | solution.py:43
  207.4 0.0 collective-permute-start.6
  207.4 2.7 %collective-permute-start.7 = (bf16[384,768]{1,0:T(8,128)(2,1)}, bf16[384,768]{1,0:T(8,128)(2,1)S(1)}, u32[]{:S(2)}, u32[]{:S(2)}) collective-permute-start(bf16[384,768]{1,0:T(8,128)(2,1)} %get-tuple-element.45), channel_id=1, source_target_pairs={{0,3},{1,0},{2,1},{3,2},{4,7},{5,4},{6,5},{7,6},{8,11},{9,8},{10,9... | collective-permute-start | bytes 1769480 | tf_op jit(solution)/shard_map/ppermute | solution.py:43
  210.0 10.7 %collective-permute-done.4 = bf16[384,768]{1,0:T(8,128)(2,1)S(1)} collective-permute-done((bf16[384,768]{1,0:T(8,128)(2,1)}, bf16[384,768]{1,0:T(8,128)(2,1)S(1)}, u32[]{:S(2)}, u32[]{:S(2)}) %collective-permute-start.4) | collective-permute-done | bytes 589856 | tf_op jit(solution)/shard_map/ppermute | solution.py:43
  220.8 1.2 add_convert_fusion.1
  222.0 0.1 collective-permute-start.5
  222.1 0.0 collective-permute-done.8
  222.1 0.0 copy-done.6
  222.1 0.1 add_convert_fusion
  222.2 2.9 %collective-permute-start.9 = (bf16[384,768]{1,0:T(8,128)(2,1)S(1)}, bf16[384,768]{1,0:T(8,128)(2,1)S(1)}, u32[]{:S(2)}, u32[]{:S(2)}) collective-permute-start(bf16[384,768]{1,0:T(8,128)(2,1)S(1)} %add_convert_fusion), channel_id=1, source_target_pairs={{0,3},{1,0},{2,1},{3,2},{4,7},{5,4},{6,5},{7,6},{8,11},{9,8},{10,9... | collective-permute-start | bytes 1769480 | tf_op jit(solution)/shard_map/ppermute | solution.py:43
  225.2 8.3 %collective-permute-done.6.g1b = bf16[384,768]{1,0:T(8,128)(2,1)S(1)} collective-permute-done((bf16[384,768]{1,0:T(8,128)(2,1)}, bf16[384,768]{1,0:T(8,128)(2,1)S(1)}, u32[]{:S(2)}, u32[]{:S(2)}) %collective-permute-start.6) | collective-permute-done | bytes 589856 | tf_op jit(solution)/shard_map/ppermute | solution.py:43
  233.4 0.0 copy-start.2
  233.4 0.0 collective-permute-done.7.g3t
  233.4 0.0 copy-start.3
  233.4 12.6 %collective-permute-done.5.g1t = bf16[384,768]{1,0:T(8,128)(2,1)S(1)} collective-permute-done((bf16[384,768]{1,0:T(8,128)(2,1)S(1)}, bf16[384,768]{1,0:T(8,128)(2,1)S(1)}, u32[]{:S(2)}, u32[]{:S(2)}) %collective-permute-start.5) | collective-permute-done | bytes 589856 | tf_op jit(solution)/shard_map/ppermute | solution.py:43
  246.1 0.0 copy-start.4
  246.1 0.0 collective-permute-done.9.g3b
  246.1 0.0 copy-start.5
  246.1 0.0 copy-done.2
  246.1 0.0 copy-done.3
  246.1 0.9 copy-done.4
  247.0 0.1 copy-done.5
  247.1 7.1 %update.1 = (bf16[256,1536]{1,0:T(8,128)(2,1)}, bf16[192,1024]{1,0:T(8,128)(2,1)}, f32[256,1536]{1,0:T(8,128)}, f32[256,1536]{1,0:T(8,128)}, f32[192,1024]{1,0:T(8,128)}, /*index=5*/f32[192,1024]{1,0:T(8,128)}) custom-call(bf16[768,768]{1,0:T(8,128)(2,1)} %bitcast.24, bf16[768,1536]{1,0:T(8,128)(2,1)} %bitcast.20, bf16[768,768]{1,0:T(8,128)(2,1)} %get-tuple-element.41.g0, ...), custom_call_target="tpu_custom_call" | custom-call | tf_op jit(solution)/shard_map/update/pallas_call | solution.py:338
  254.2 1.1 all-to-all-done.3.back
  255.3 4.8 %combine.1 = (bf16[2,64,1024]{2,1,0:T(8,128)(2,1)}, bf16[2,64,1024]{2,1,0:T(8,128)(2,1)}) custom-call(bf16[32,64,1024]{2,1,0:T(8,128)(2,1)} %all-to-all-done.3.back, bf16[2,64,512]{2,1,0:T(8,128)(2,1)} %get-tuple-element.36.place, bf16[2,128,512]{2,1,0:T(8,128)(2,1)} %get-tuple-element.37.gated), custom_call_target="tpu_custom_call" | custom-call | tf_op jit(solution)/shard_map/combine/pallas_call | solution.py:170
Async XLA Ops:
  61.3 4.0 %copy-start.7 = (s32[32]{0:T(128)S(1)}, s32[32]{0:T(128)}, u32[]{:S(2)}) copy-start(s32[32]{0:T(128)} %plan.3) | copy-start | bytes 388
  61.3 22.7 %all-to-all-start.1 = ((bf16[32,24,768]{2,1,0:T(8,128)(2,1)}), bf16[32,24,768]{2,1,0:T(8,128)(2,1)S(1)}, u32[]{:S(2)}, u32[]{:S(2)}) async-start(bf16[32,24,768]{2,1,0:T(8,128)(2,1)} %pick.2), calls=%async_computation.1 | async-start | bytes 2359296 | tf_op jit(solution)/shard_map/all_to_all | solution.py:39
  84.0 7.4 %copy-start.1 = (bf16[32,24,768]{2,1,0:T(8,128)(2,1)}, bf16[32,24,768]{2,1,0:T(8,128)(2,1)S(1)}, u32[]{:S(2)}) copy-start(bf16[32,24,768]{2,1,0:T(8,128)(2,1)S(1)} %all-to-all-done.1) | copy-start | bytes 3538948
  84.0 55.5 %all-to-all-start.2 = ((bf16[32,64,1024]{2,1,0:T(8,128)(2,1)}), bf16[32,64,1024]{2,1,0:T(8,128)(2,1)}, u32[]{:S(2)}, u32[]{:S(2)}) async-start(bf16[32,64,1024]{2,1,0:T(8,128)(2,1)} %get-tuple-element.32), calls=%async_computation.2 | async-start | bytes 8388608 | tf_op jit(solution)/shard_map/all_to_all | solution.py:39
  88.8 58.1 %collective-permute-start.2 = (bf16[768,768]{1,0:T(8,128)(2,1)S(1)}, bf16[768,768]{1,0:T(8,128)(2,1)}, u32[]{:S(2)}, u32[]{:S(2)}) collective-permute-start(bf16[768,768]{1,0:T(8,128)(2,1)S(1)} %bitcast.21), channel_id=1, source_target_pairs={{0,3},{1,0},{2,1},{3,2},{4,7},{5,4},{6,5},{7,6},{8,11},{9,8},{10,9... | collective-permute-start | bytes 3538952 | tf_op jit(solution)/shard_map/ppermute | solution.py:43
  91.4 60.0 %collective-permute-start = (bf16[768,768]{1,0:T(8,128)(2,1)S(1)}, bf16[768,768]{1,0:T(8,128)(2,1)}, u32[]{:S(2)}, u32[]{:S(2)}) collective-permute-start(bf16[768,768]{1,0:T(8,128)(2,1)S(1)} %bitcast.22), channel_id=1, source_target_pairs={{0,1},{1,2},{2,3},{3,0},{4,5},{5,6},{6,7},{7,4},{8,9},{9,10},{10,1... | collective-permute-start | bytes 3538952 | tf_op jit(solution)/shard_map/ppermute | solution.py:43
  139.5 55.0 %all-to-all-start.4 = ((bf16[32,24,1536]{2,1,0:T(8,128)(2,1)}), bf16[32,24,1536]{2,1,0:T(8,128)(2,1)S(1)}, u32[]{:S(2)}, u32[]{:S(2)}) async-start(bf16[32,24,1536]{2,1,0:T(8,128)(2,1)} %pick.3), calls=%async_computation.4 | async-start | bytes 4718592 | tf_op jit(solution)/shard_map/all_to_all | solution.py:39
  148.8 15.1 %collective-permute-start.3 = (bf16[384,768]{1,0:T(8,128)(2,1)}, bf16[384,768]{1,0:T(8,128)(2,1)}, u32[]{:S(2)}, u32[]{:S(2)}) collective-permute-start(bf16[384,768]{1,0:T(8,128)(2,1)} %slice.9), channel_id=1, source_target_pairs={{0,3},{1,0},{2,1},{3,2},{4,7},{5,4},{6,5},{7,6},{8,11},{9,8},{10,9... | collective-permute-start | bytes 1769480 | tf_op jit(solution)/shard_map/ppermute | solution.py:43
  152.4 15.7 %collective-permute-start.1 = (bf16[384,768]{1,0:T(8,128)(2,1)S(1)}, bf16[384,768]{1,0:T(8,128)(2,1)S(1)}, u32[]{:S(2)}, u32[]{:S(2)}) collective-permute-start(bf16[384,768]{1,0:T(8,128)(2,1)S(1)} %slice.8), channel_id=1, source_target_pairs={{0,1},{1,2},{2,3},{3,0},{4,5},{5,6},{6,7},{7,4},{8,9},{9,10},{10,1... | collective-permute-start | bytes 1769480 | tf_op jit(solution)/shard_map/ppermute | solution.py:43
  168.1 0.8 copy-start.8
  194.5 1.5 copy-start
  196.0 59.3 %all-to-all-start.3 = ((bf16[32,64,1024]{2,1,0:T(8,128)(2,1)}), bf16[32,64,1024]{2,1,0:T(8,128)(2,1)}, u32[]{:S(2)}, u32[]{:S(2)}) async-start(bf16[32,64,1024]{2,1,0:T(8,128)(2,1)} %get-tuple-element.35), calls=%async_computation.3 | async-start | bytes 8388608 | tf_op jit(solution)/shard_map/all_to_all | solution.py:39
  204.6 17.5 %copy-start.6 = (bf16[384,768]{1,0:T(8,128)(2,1)S(1)}, bf16[384,768]{1,0:T(8,128)(2,1)}, u32[]{:S(2)}) copy-start(bf16[384,768]{1,0:T(8,128)(2,1)} %get-tuple-element.46) | copy-start | bytes 1769476
  204.6 16.2 %collective-permute-start.4 = (bf16[384,768]{1,0:T(8,128)(2,1)}, bf16[384,768]{1,0:T(8,128)(2,1)S(1)}, u32[]{:S(2)}, u32[]{:S(2)}) collective-permute-start(bf16[384,768]{1,0:T(8,128)(2,1)} %get-tuple-element.43), channel_id=1, source_target_pairs={{0,1},{1,2},{2,3},{3,0},{4,5},{5,6},{6,7},{7,4},{8,9},{9,10},{10,1... | collective-permute-start | bytes 1769480 | tf_op jit(solution)/shard_map/ppermute | solution.py:43
  204.7 17.4 %collective-permute-start.8 = (bf16[384,768]{1,0:T(8,128)(2,1)}, bf16[384,768]{1,0:T(8,128)(2,1)S(1)}, u32[]{:S(2)}, u32[]{:S(2)}) collective-permute-start(bf16[384,768]{1,0:T(8,128)(2,1)} %get-tuple-element.47), channel_id=1, source_target_pairs={{0,3},{1,0},{2,1},{3,2},{4,7},{5,4},{6,5},{7,6},{8,11},{9,8},{10,9... | collective-permute-start | bytes 1769480 | tf_op jit(solution)/shard_map/ppermute | solution.py:43
  207.4 26.1 %collective-permute-start.6 = (bf16[384,768]{1,0:T(8,128)(2,1)}, bf16[384,768]{1,0:T(8,128)(2,1)S(1)}, u32[]{:S(2)}, u32[]{:S(2)}) collective-permute-start(bf16[384,768]{1,0:T(8,128)(2,1)} %get-tuple-element.44), channel_id=1, source_target_pairs={{0,1},{1,2},{2,3},{3,0},{4,5},{5,6},{6,7},{7,4},{8,9},{9,10},{10,1... | collective-permute-start | bytes 1769480 | tf_op jit(solution)/shard_map/ppermute | solution.py:43
  207.4 26.1 %collective-permute-start.7 = (bf16[384,768]{1,0:T(8,128)(2,1)}, bf16[384,768]{1,0:T(8,128)(2,1)S(1)}, u32[]{:S(2)}, u32[]{:S(2)}) collective-permute-start(bf16[384,768]{1,0:T(8,128)(2,1)} %get-tuple-element.45), channel_id=1, source_target_pairs={{0,3},{1,0},{2,1},{3,2},{4,7},{5,4},{6,5},{7,6},{8,11},{9,8},{10,9... | collective-permute-start | bytes 1769480 | tf_op jit(solution)/shard_map/ppermute | solution.py:43
  222.0 24.1 %collective-permute-start.5 = (bf16[384,768]{1,0:T(8,128)(2,1)S(1)}, bf16[384,768]{1,0:T(8,128)(2,1)S(1)}, u32[]{:S(2)}, u32[]{:S(2)}) collective-permute-start(bf16[384,768]{1,0:T(8,128)(2,1)S(1)} %add_convert_fusion.1), channel_id=1, source_target_pairs={{0,1},{1,2},{2,3},{3,0},{4,5},{5,6},{6,7},{7,4},{8,9},{9,10},{10,1... | collective-permute-start | bytes 1769480 | tf_op jit(solution)/shard_map/ppermute | solution.py:43
  222.2 23.8 %collective-permute-start.9 = (bf16[384,768]{1,0:T(8,128)(2,1)S(1)}, bf16[384,768]{1,0:T(8,128)(2,1)S(1)}, u32[]{:S(2)}, u32[]{:S(2)}) collective-permute-start(bf16[384,768]{1,0:T(8,128)(2,1)S(1)} %add_convert_fusion), channel_id=1, source_target_pairs={{0,3},{1,0},{2,1},{3,2},{4,7},{5,4},{6,5},{7,6},{8,11},{9,8},{10,9... | collective-permute-start | bytes 1769480 | tf_op jit(solution)/shard_map/ppermute | solution.py:43
  233.4 12.6 %copy-start.2 = (bf16[384,768]{1,0:T(8,128)(2,1)}, bf16[384,768]{1,0:T(8,128)(2,1)S(1)}, u32[]{:S(2)}) copy-start(bf16[384,768]{1,0:T(8,128)(2,1)S(1)} %collective-permute-done.6.g1b) | copy-start | bytes 1769476
  233.4 12.7 %copy-start.3 = (bf16[384,768]{1,0:T(8,128)(2,1)}, bf16[384,768]{1,0:T(8,128)(2,1)S(1)}, u32[]{:S(2)}) copy-start(bf16[384,768]{1,0:T(8,128)(2,1)S(1)} %collective-permute-done.7.g3t) | copy-start | bytes 1769476
  246.1 0.9 copy-start.4
  246.1 1.0 copy-start.5

commit v3 on v2

--- a/solution.py
+++ b/solution.py
@@ -22,7 +22,6 @@
 CAP = 16
 ROWS = 2 * CAP
 HALF = SIDE // 2
-CHUNKS = 2
 
 f32 = jnp.float32
 bf16 = jnp.bfloat16
@@ -47,8 +46,10 @@
     return (a.astype(f32) + b.astype(f32)).astype(bf16)
 
 
-def pack_body(w_in, w_out, f_in, f_out, s_in, s_out, out):
-    for j, (a, b) in enumerate(((f_in, f_out), (s_in, s_out), (w_in, w_out))):
+def pack_body(*refs):
+    out = refs[-1]
+    for j in range(len(refs) // 2):
+        a, b = refs[2 * j : 2 * j + 2]
         lanes = slice(j * SIDE, (j + 1) * SIDE)
         out[0:RI, lanes] = a[:, :SIDE].astype(bf16)
         out[RI : 2 * RI, lanes] = a[:, SIDE:].astype(bf16)
@@ -58,34 +59,57 @@
             out[2 * RI + RO :, at : at + 256] = b[RT * i : RT * i + RT, SIDE:].astype(bf16)
 
 
-def pack(w_in, w_out, f_in, f_out, s_in, s_out):
+def pack(pairs, width):
+    flat = [a for pair in pairs for a in pair]
+    size = len(pairs) * SIDE
     return pl.pallas_call(
         pack_body,
-        out_shape=jax.ShapeDtypeStruct((SIDE, 3 * SIDE), bf16),
-        in_specs=[VMEM] * 6,
+        grid=(1,),
+        out_shape=jax.ShapeDtypeStruct((SIDE, width), bf16),
+        in_specs=[VMEM] * len(flat),
+        out_specs=pl.BlockSpec((SIDE, size), lambda i: (0, 0)),
+        name="pack",
+    )(*flat)
+
+
+def copy_picked(plan, src, out, lanes):
+    def step(d, carry):
+        out[d] = src[plan[d], :, lanes]
+        return carry
+
+    lax.fori_loop(0, COUNT, step, 0, unroll=True)
+
+
+def pick_body(plan, src, out):
+    copy_picked(plan, src, out, slice(0, out.shape[2]))
+
+
+def pick(plan, src, size):
+    return pl.pallas_call(
+        pick_body,
+        out_shape=jax.ShapeDtypeStruct(src.shape[:2] + (size,), bf16),
+        in_specs=[SMEM, VMEM],
         out_specs=VMEM,
-        name="pack",
-    )(w_in, w_out, f_in, f_out, s_in, s_out)
-
-
-def pick_body(plan, src, out):
-    def step(d, carry):
-        out[d] = src[plan[d]]
-        return carry
-
-    lax.fori_loop(0, COUNT, step, 0, unroll=True)
-
-
-def pick(plan, src, lo, size):
-    shape = (COUNT, SIDE // COUNT, size)
-    return pl.pallas_call(
-        pick_body,
-        grid=(1,),
-        out_shape=jax.ShapeDtypeStruct(shape, bf16),
-        in_specs=[SMEM, pl.BlockSpec(shape, lambda i: (0, 0, lo // size))],
-        out_specs=pl.BlockSpec(shape, lambda i: (0, 0, 0)),
+        compiler_params=pltpu.CompilerParams(vmem_limit_bytes=12 << 20),
         name="pick",
     )(plan, src)
+
+
+def place_body(plan, src, held, out):
+    copy_picked(plan, src, out, slice(0, SIDE))
+
+
+def place_picked(plan, src, held):
+    return pl.pallas_call(
+        place_body,
+        grid=(1,),
+        out_shape=jax.ShapeDtypeStruct(held.shape, bf16),
+        in_specs=[SMEM, VMEM, pl.BlockSpec(memory_space=pltpu.HBM)],
+        out_specs=pl.BlockSpec(src.shape, lambda i: (0, 0, 2)),
+        input_output_aliases={2: 0},
+        compiler_params=pltpu.CompilerParams(vmem_limit_bytes=50 << 20),
+        name="place",
+    )(plan, src, held)
 
 
 def dispatch_body(routes, gates, plan, tokens, cotangent, out, place, gated):
@@ -141,26 +165,14 @@
     )(routes, gates, plan, tokens, cotangent)
 
 
-def combine_body(back, place, gated, layer, token, buf, sem):
+def combine_body(back, place, gated, layer, token):
     n = layer.shape[1]
-    size = COUNT // CHUNKS
-    copies = [
-        pltpu.make_async_copy(back.at[i * size : (i + 1) * size], buf.at[i], sem.at[i]) for i in range(CHUNKS)
-    ]
-    for c in copies:
-        c.start()
-    sums = [None] * 4
-    for i, c in enumerate(copies):
-        c.wait()
-        slots = slice(i * size * CAP, (i + 1) * size * CAP)
-        for m in range(2):
-            for j, (table, at) in enumerate(((gated, 0), (place, ROWS))):
-                rows = buf[i, :, at + CAP * m : at + CAP * m + CAP, :].reshape(size * CAP, -1)
-                part = jnp.dot(table[m, :, slots], rows, preferred_element_type=f32)
-                sums[2 * j + m] = part if i == 0 else sums[2 * j + m] + part
     for m in range(2):
-        layer[m] = (sums[m][:n] + sums[m][n:]).astype(bf16)
-        token[m] = sums[2 + m].astype(bf16)
+        rows = back[:, CAP * m : CAP * m + CAP, :].reshape(COUNT * CAP, -1)
+        sums = jnp.dot(gated[m], rows, preferred_element_type=f32)
+        layer[m] = (sums[:n] + sums[n:]).astype(bf16)
+        rows = back[:, ROWS + CAP * m : ROWS + CAP * m + CAP, :].reshape(COUNT * CAP, -1)
+        token[m] = jnp.dot(place[m], rows, preferred_element_type=f32).astype(bf16)
 
 
 def combine(back, place, gated):
@@ -170,12 +182,8 @@
     return pl.pallas_call(
         combine_body,
         out_shape=(shape, shape),
-        in_specs=[ANY, VMEM, VMEM],
+        in_specs=[VMEM] * 3,
         out_specs=(VMEM, VMEM),
-        scratch_shapes=[
-            pltpu.VMEM((CHUNKS, COUNT // CHUNKS, 2 * ROWS, width), bf16),
-            pltpu.SemaphoreType.DMA((CHUNKS,)),
-        ],
         name="combine",
     )(back, place, gated)
 
@@ -347,6 +355,7 @@
         ),
         in_specs=[VMEM] * 7,
         out_specs=(VMEM,) * 6,
+        compiler_params=pltpu.CompilerParams(vmem_limit_bytes=32 << 20),
         name="update",
     )(w, moments, *grads)
 
@@ -365,21 +374,23 @@
     second_out,
 ):
     mine = lax.axis_index("dp").astype(jnp.int32).reshape(1)
-    packed = pack(weight_in[0], weight_out[0], first_in[0], first_out[0], second_in[0], second_out[0])
-    spread = exchange(packed.reshape(COUNT, SIDE // COUNT, 3 * SIDE))
-    own = exchange(pick(expert_plan, spread, 2 * SIDE, SIDE)).reshape(SIDE, SIDE)
+    slim = (COUNT, SIDE // COUNT, SIDE)
+    wide = (COUNT, SIDE // COUNT, 3 * SIDE)
+    weights = exchange(pack(((weight_in[0], weight_out[0]),), SIDE).reshape(slim))
+    held = pack(((first_in[0], first_out[0]), (second_in[0], second_out[0])), 3 * SIDE)
+    filled = place_picked(expert_plan, weights, held.reshape(wide))
+    spread = exchange(filled)
+    own = spread[:, :, 2 * SIDE :].reshape(SIDE, SIDE)
     outgoing, place, gated = dispatch(
         routes.transpose(2, 0, 1), gate_weights.transpose(2, 0, 1), expert_plan.reshape(-1, 1), tokens, cotangent
     )
-    outgoing, own = lax.optimization_barrier((outgoing, own))
     before = shifted(own, 1)
     after = shifted(own, 3)
     top = shifted(before[:HALF], 1)
     bottom = shifted(after[HALF:], 3)
     parts = (own, before, top, bottom, after)
     arrived = exchange(outgoing)
-    moved = pick(expert_plan, spread, 0, 2 * SIDE)
-    arrived, moved = lax.optimization_barrier((arrived, moved))
+    moved = pick(expert_plan, spread, 2 * SIDE)
     moments = exchange(moved).reshape(SIDE, 2 * SIDE)
     back, g0, g1t, g1b, g2t, g2b, g3t, g3b = expert(mine, arrived, parts)
     from_before = shifted(g2t, 1)

time: 263 us -> 259 us (0.985)
  blocking collectives: 53.5 us -> 0 us
  waiting for transfers between devices: 106 us -> 149 us
  starting transfers between devices: 38.6 us -> 51.1 us
  Pallas kernels: 52.7 us -> 48.8 us
    all_to_all x1 -> x0, blocking collectives: 53.5 us -> none  [exchange(): return lax.all_to_all(x, 'expert', split_axis=0, concat_axis=0, tiled=True)]
    all_to_all x4 -> x5, waiting for transfers between devices: 59 us -> 101 us  [exchange(): return lax.all_to_all(x, 'expert', split_axis=0, concat_axis=0, tiled=True)]
    all_to_all x4 -> x5, starting transfers between devices: 24.9 us -> 37.4 us  [exchange(): return lax.all_to_all(x, 'expert', split_axis=0, concat_axis=0, tiled=True)]
    pallas_call x4 -> x5, Pallas kernels: 15.1 us -> 12.5 us  [the longest x2 6.35 us: pack(): pl.pallas_call(pack_body, grid=(1,), out_shape=jax.ShapeDtypeStruct((SIDE...]
  transfers between devices with their start and end apart: 14 -> 15, of which waited for: 8 -> 9; matrix products, arithmetic and copies ran while one was open for 2% -> 2% of each run, Pallas kernels for 16% -> 16%
where the time goes in v3:
time: 259 us; the launch traced here: 256 us
  waiting for transfers between devices  149 us (58%)
  starting transfers between devices  51.1 us (20%)
  Pallas kernels  48.8 us (19%)
  local copies, waits for them, and re-layouts  5.46 us (2%)
    all_to_all x5, waiting for transfers between devices, exchange(): return lax.all_to_all(x, 'expert', split_axis=0, concat_axis=0, tiled=True)  101 us
    ppermute x10, waiting for transfers between devices, shifted(): return lax.ppermute(x, 'dp', [(i, (i + by) % REP) for i in range(REP)])  48.3 us
    all_to_all x5, starting transfers between devices, exchange(): return lax.all_to_all(x, 'expert', split_axis=0, concat_axis=0, tiled=True)  37.4 us
    pallas_call x1, Pallas kernels, expert(): pl.pallas_call(expert_body, out_shape=(jax.ShapeDtypeStruct(rows.shape, b...  25.6 us
    ppermute x10, starting transfers between devices, shifted(): return lax.ppermute(x, 'dp', [(i, (i + by) % REP) for i in range(REP)])  13.7 us
    pallas_call x2, Pallas kernels, pack(): pl.pallas_call(pack_body, grid=(1,), out_shape=jax.ShapeDtypeStruct((SIDE...  6.35 us
    pallas_call x1, Pallas kernels, update(): pl.pallas_call(update_body, out_shape=(jax.ShapeDtypeStruct((RI, 2 * SIDE...  5.69 us
  transfers between devices with their start and end apart: 15, of which 9 were waited for; matrix products, arithmetic and copies ran while one was open for 2% of the time, Pallas kernels for 16%

profile of v3, /device:TPU:1, one launch (start us, length us, event | category | flops | bytes accessed | tf_op | source)
XLA Modules:
  0.0 255.8 jit_solution(10629553456674385515)
XLA Ops:
  0.6 2.3 pack.2
  3.0 9.6 %all-to-all-start.1 = ((bf16[32,24,768]{2,1,0:T(8,128)(2,1)}), bf16[32,24,768]{2,1,0:T(8,128)(2,1)S(1)}, u32[]{:S(2)}, u32[]{:S(2)}) async-start(bf16[32,24,768]{2,1,0:T(8,128)(2,1)} %bitcast.23), calls=%async_computation.1 | async-start | bytes 2359296 | tf_op jit(solution)/shard_map/all_to_all | solution.py:38
  12.6 0.0 copy-start.2
  12.6 4.0 %pack.3 = bf16[768,2304]{1,0:T(8,128)(2,1)} custom-call(f32[256,1536]{1,0:T(8,128)} %bitcast.24, f32[192,1024]{1,0:T(8,128)} %bitcast.27, f32[256,1536]{1,0:T(8,128)} %bitcast.25, f32[192,1024]{1,0:T(8,128)} %bitcast.28), custom_call_target="tpu_custom_call" | custom-call | tf_op jit(solution)/shard_map/pack/pallas_call | solution.py:65
  16.6 14.5 %all-to-all-done.1.src = bf16[32,24,768]{2,1,0:T(8,128)(2,1)S(1)} async-done(((bf16[32,24,768]{2,1,0:T(8,128)(2,1)}), bf16[32,24,768]{2,1,0:T(8,128)(2,1)S(1)}, u32[]{:S(2)}, u32[]{:S(2)}) %all-to-all-start.1) | async-done | bytes 1179680 | tf_op jit(solution)/shard_map/all_to_all | solution.py:38
  31.1 0.0 copy-done.2
  31.1 1.7 place.1
  32.8 4.1 %all-to-all-start.2 = ((bf16[32,24,2304]{2,1,0:T(8,128)(2,1)}), bf16[32,24,2304]{2,1,0:T(8,128)(2,1)S(1)}, u32[]{:S(2)}, u32[]{:S(2)}) async-start(bf16[32,24,2304]{2,1,0:T(8,128)(2,1)} %place.1), calls=%async_computation.2 | async-start | bytes 7077888 | tf_op jit(solution)/shard_map/all_to_all | solution.py:38
  36.9 0.7 copy.20.plan
  37.6 5.0 %dispatch.1 = (bf16[32,64,1024]{2,1,0:T(8,128)(2,1)}, bf16[2,64,512]{2,1,0:T(8,128)(2,1)}, bf16[2,128,512]{2,1,0:T(8,128)(2,1)}) custom-call(s32[6,2,64]{2,1,0:T(2,128)} %bitcast.30, f32[6,2,64]{2,1,0:T(2,128)} %bitcast.31, s32[32,1]{1,0:T(8,128)} %copy.20.plan, bf16[2,64,1024]{2,1,0:T(8,128)(2,1)} %tokens.1, bf16[2,64,1024]{2,1,0:T(8,128)(2,1)} %cotangent.1), custom_call_target="tpu_custom_call" | custom-call | tf_op jit(solution)/shard_map/dispatch/pallas_call | solution.py:155
  42.6 38.0 %all-to-all-done.2.src = bf16[32,24,2304]{2,1,0:T(8,128)(2,1)S(1)} async-done(((bf16[32,24,2304]{2,1,0:T(8,128)(2,1)}), bf16[32,24,2304]{2,1,0:T(8,128)(2,1)S(1)}, u32[]{:S(2)}, u32[]{:S(2)}) %all-to-all-start.2) | async-done | bytes 3538976 | tf_op jit(solution)/shard_map/all_to_all | solution.py:38
  80.6 7.5 %all-to-all-start = ((bf16[32,64,1024]{2,1,0:T(8,128)(2,1)}), bf16[32,64,1024]{2,1,0:T(8,128)(2,1)}, u32[]{:S(2)}, u32[]{:S(2)}) async-start(bf16[32,64,1024]{2,1,0:T(8,128)(2,1)} %get-tuple-element.27), calls=%async_computation | async-start | bytes 8388608 | tf_op jit(solution)/shard_map/all_to_all | solution.py:38
  88.1 1.1 slice.12
  89.2 2.5 collective-permute-start.2
  91.7 0.0 collective-permute-start
  91.7 0.7 pick.1
  92.4 0.0 copy-start
  92.4 1.5 copy-done
  93.9 45.0 %all-to-all-done.rows = bf16[32,64,1024]{2,1,0:T(8,128)(2,1)} async-done(((bf16[32,64,1024]{2,1,0:T(8,128)(2,1)}), bf16[32,64,1024]{2,1,0:T(8,128)(2,1)}, u32[]{:S(2)}, u32[]{:S(2)}) %all-to-all-start) | async-done | bytes 4194336 | tf_op jit(solution)/shard_map/all_to_all | solution.py:38
  138.8 7.4 %all-to-all-start.4 = ((bf16[32,24,1536]{2,1,0:T(8,128)(2,1)}), bf16[32,24,1536]{2,1,0:T(8,128)(2,1)S(1)}, u32[]{:S(2)}, u32[]{:S(2)}) async-start(bf16[32,24,1536]{2,1,0:T(8,128)(2,1)} %copy-done), calls=%async_computation.4 | async-start | bytes 4718592 | tf_op jit(solution)/shard_map/all_to_all | solution.py:38
  146.2 0.0 collective-permute-done.2.w3
  146.3 1.1 slice.14
  147.4 2.5 collective-permute-start.3
  149.9 0.0 collective-permute-done.w1
  149.9 1.1 slice.13
  151.0 0.3 collective-permute-start.1
  151.3 11.0 %collective-permute-done.3.w2b = bf16[384,768]{1,0:T(8,128)(2,1)} collective-permute-done((bf16[384,768]{1,0:T(8,128)(2,1)S(1)}, bf16[384,768]{1,0:T(8,128)(2,1)}, u32[]{:S(2)}, u32[]{:S(2)}) %collective-permute-start.3) | collective-permute-done | bytes 589856 | tf_op jit(solution)/shard_map/ppermute | solution.py:42
  162.2 4.6 %collective-permute-done.1.w2a = bf16[384,768]{1,0:T(8,128)(2,1)} collective-permute-done((bf16[384,768]{1,0:T(8,128)(2,1)S(1)}, bf16[384,768]{1,0:T(8,128)(2,1)}, u32[]{:S(2)}, u32[]{:S(2)}) %collective-permute-start.1) | collective-permute-done | bytes 589856 | tf_op jit(solution)/shard_map/ppermute | solution.py:42
  166.8 25.6 %expert.1 = (bf16[32,64,1024]{2,1,0:T(8,128)(2,1)}, bf16[768,768]{1,0:T(8,128)(2,1)}, bf16[384,768]{1,0:T(8,128)(2,1)}, bf16[384,768]{1,0:T(8,128)(2,1)}, bf16[3...) custom-call(s32[1]{0:T(128)} %bitcast.mine, ...), custom_call_target="tpu_custom_call" | custom-call | flops 14499999744 | bytes 18000000 | tf_op jit(solution)/shard_map/expert/pallas_call | solution.py:284
  192.5 0.0 all-to-all-done.4
  192.5 0.0 copy-start.5
  192.5 0.0 copy-start.4
  192.5 8.8 %all-to-all-start.3 = ((bf16[32,64,1024]{2,1,0:T(8,128)(2,1)}), bf16[32,64,1024]{2,1,0:T(8,128)(2,1)}, u32[]{:S(2)}, u32[]{:S(2)}) async-start(bf16[32,64,1024]{2,1,0:T(8,128)(2,1)} %get-tuple-element.28), calls=%async_computation.3 | async-start | bytes 8388608 | tf_op jit(solution)/shard_map/all_to_all | solution.py:38
  201.3 0.0 copy-start.3
  201.3 0.1 collective-permute-start.4
  201.4 2.7 %collective-permute-start.8 = (bf16[384,768]{1,0:T(8,128)(2,1)}, bf16[384,768]{1,0:T(8,128)(2,1)S(1)}, u32[]{:S(2)}, u32[]{:S(2)}) collective-permute-start(bf16[384,768]{1,0:T(8,128)(2,1)} %get-tuple-element.39), channel_id=1, source_target_pairs={{0,3},{1,0},{2,1},{3,2},{4,7},{5,4},{6,5},{7,6},{8,11},{9,8},{10,9... | collective-permute-start | bytes 1769480 | tf_op jit(solution)/shard_map/ppermute | solution.py:42
  204.1 0.0 collective-permute-start.6
  204.1 0.0 copy-done.5
  204.1 2.7 %collective-permute-start.7 = (bf16[384,768]{1,0:T(8,128)(2,1)S(1)}, bf16[384,768]{1,0:T(8,128)(2,1)S(1)}, u32[]{:S(2)}, u32[]{:S(2)}) collective-permute-start(bf16[384,768]{1,0:T(8,128)(2,1)S(1)} %copy-done.5), channel_id=1, source_target_pairs={{0,3},{1,0},{2,1},{3,2},{4,7},{5,4},{6,5},{7,6},{8,11},{9,8},{10,9... | collective-permute-start | bytes 1769480 | tf_op jit(solution)/shard_map/ppermute | solution.py:42
  206.7 10.7 %collective-permute-done.4 = bf16[384,768]{1,0:T(8,128)(2,1)S(1)} collective-permute-done((bf16[384,768]{1,0:T(8,128)(2,1)}, bf16[384,768]{1,0:T(8,128)(2,1)S(1)}, u32[]{:S(2)}, u32[]{:S(2)}) %collective-permute-start.4) | collective-permute-done | bytes 589856 | tf_op jit(solution)/shard_map/ppermute | solution.py:42
  217.5 0.0 copy-done.4
  217.5 0.0 copy-start.1
  217.5 0.1 add_convert_fusion.1
  217.6 0.1 collective-permute-start.5
  217.7 0.0 collective-permute-done.8
  217.7 0.0 copy-done.3
  217.7 0.1 add_convert_fusion
  217.9 2.9 %collective-permute-start.9 = (bf16[384,768]{1,0:T(8,128)(2,1)S(1)}, bf16[384,768]{1,0:T(8,128)(2,1)S(1)}, u32[]{:S(2)}, u32[]{:S(2)}) collective-permute-start(bf16[384,768]{1,0:T(8,128)(2,1)S(1)} %add_convert_fusion), channel_id=1, source_target_pairs={{0,3},{1,0},{2,1},{3,2},{4,7},{5,4},{6,5},{7,6},{8,11},{9,8},{10,9... | collective-permute-start | bytes 1769480 | tf_op jit(solution)/shard_map/ppermute | solution.py:42
  220.8 9.3 %collective-permute-done.6.g1b = bf16[384,768]{1,0:T(8,128)(2,1)S(1)} collective-permute-done((bf16[384,768]{1,0:T(8,128)(2,1)}, bf16[384,768]{1,0:T(8,128)(2,1)S(1)}, u32[]{:S(2)}, u32[]{:S(2)}) %collective-permute-start.6) | collective-permute-done | bytes 589856 | tf_op jit(solution)/shard_map/ppermute | solution.py:42
  230.1 0.0 collective-permute-done.7.g3t
  230.1 12.6 %collective-permute-done.5.g1t = bf16[384,768]{1,0:T(8,128)(2,1)S(1)} collective-permute-done((bf16[384,768]{1,0:T(8,128)(2,1)S(1)}, bf16[384,768]{1,0:T(8,128)(2,1)S(1)}, u32[]{:S(2)}, u32[]{:S(2)}) %collective-permute-start.5) | collective-permute-done | bytes 589856 | tf_op jit(solution)/shard_map/ppermute | solution.py:42
  242.8 0.0 collective-permute-done.9.g3b
  242.8 0.0 copy-done.1
  242.8 5.7 %update.1 = (bf16[256,1536]{1,0:T(8,128)(2,1)}, bf16[192,1024]{1,0:T(8,128)(2,1)}, f32[256,1536]{1,0:T(8,128)}, f32[256,1536]{1,0:T(8,128)}, f32[192,1024]{1,0:T(8,128)}, /*index=5*/f32[192,1024]{1,0:T(8,128)}) custom-call(bf16[768,768]{1,0:T(8,128)(2,1)} %bitcast.12.w0.w, bf16[768,1536]{1,0:T(8,128)(2,1)S(1)} %bitcast.20, bf16[768,768]{1,0:T(8,128)(2,1)S(1)} %copy-done.1, ...), custom_call_target="tpu_custom_call" | custom-call | tf_op jit(solution)/shard_map/update/pallas_call | solution.py:346
  248.5 3.5 %all-to-all-done.3.back = bf16[32,64,1024]{2,1,0:T(8,128)(2,1)} async-done(((bf16[32,64,1024]{2,1,0:T(8,128)(2,1)}), bf16[32,64,1024]{2,1,0:T(8,128)(2,1)}, u32[]{:S(2)}, u32[]{:S(2)}) %all-to-all-start.3) | async-done | bytes 4194336 | tf_op jit(solution)/shard_map/all_to_all | solution.py:38
  252.0 3.8 %combine.1 = (bf16[2,64,1024]{2,1,0:T(8,128)(2,1)}, bf16[2,64,1024]{2,1,0:T(8,128)(2,1)}) custom-call(bf16[32,64,1024]{2,1,0:T(8,128)(2,1)} %all-to-all-done.3.back, bf16[2,64,512]{2,1,0:T(8,128)(2,1)} %get-tuple-element.29.place, bf16[2,128,512]{2,1,0:T(8,128)(2,1)} %get-tuple-element.30.gated), custom_call_target="tpu_custom_call" | custom-call | tf_op jit(solution)/shard_map/combine/pallas_call | solution.py:182
Async XLA Ops:
  3.0 28.1 %all-to-all-start.1 = ((bf16[32,24,768]{2,1,0:T(8,128)(2,1)}), bf16[32,24,768]{2,1,0:T(8,128)(2,1)S(1)}, u32[]{:S(2)}, u32[]{:S(2)}) async-start(bf16[32,24,768]{2,1,0:T(8,128)(2,1)} %bitcast.23), calls=%async_computation.1 | async-start | bytes 2359296 | tf_op jit(solution)/shard_map/all_to_all | solution.py:38
  12.6 18.5 %copy-start.2 = (s32[32]{0:T(128)S(1)}, s32[32]{0:T(128)}, u32[]{:S(2)}) copy-start(s32[32]{0:T(128)} %plan.3) | copy-start | bytes 388
  32.8 47.8 %all-to-all-start.2 = ((bf16[32,24,2304]{2,1,0:T(8,128)(2,1)}), bf16[32,24,2304]{2,1,0:T(8,128)(2,1)S(1)}, u32[]{:S(2)}, u32[]{:S(2)}) async-start(bf16[32,24,2304]{2,1,0:T(8,128)(2,1)} %place.1), calls=%async_computation.2 | async-start | bytes 7077888 | tf_op jit(solution)/shard_map/all_to_all | solution.py:38
  80.6 58.2 %all-to-all-start = ((bf16[32,64,1024]{2,1,0:T(8,128)(2,1)}), bf16[32,64,1024]{2,1,0:T(8,128)(2,1)}, u32[]{:S(2)}, u32[]{:S(2)}) async-start(bf16[32,64,1024]{2,1,0:T(8,128)(2,1)} %get-tuple-element.27), calls=%async_computation | async-start | bytes 8388608 | tf_op jit(solution)/shard_map/all_to_all | solution.py:38
  89.2 57.0 %collective-permute-start.2 = (bf16[768,768]{1,0:T(8,128)(2,1)}, bf16[768,768]{1,0:T(8,128)(2,1)}, u32[]{:S(2)}, u32[]{:S(2)}) collective-permute-start(bf16[768,768]{1,0:T(8,128)(2,1)} %bitcast.12.w0.w), channel_id=1, source_target_pairs={{0,3},{1,0},{2,1},{3,2},{4,7},{5,4},{6,5},{7,6},{8,11},{9,8},{10,9... | collective-permute-start | bytes 3538952 | tf_op jit(solution)/shard_map/ppermute | solution.py:42
  91.7 58.2 %collective-permute-start = (bf16[768,768]{1,0:T(8,128)(2,1)}, bf16[768,768]{1,0:T(8,128)(2,1)}, u32[]{:S(2)}, u32[]{:S(2)}) collective-permute-start(bf16[768,768]{1,0:T(8,128)(2,1)} %bitcast.12.w0.w), channel_id=1, source_target_pairs={{0,1},{1,2},{2,3},{3,0},{4,5},{5,6},{6,7},{7,4},{8,9},{9,10},{10,1... | collective-permute-start | bytes 3538952 | tf_op jit(solution)/shard_map/ppermute | solution.py:42
  92.4 1.5 copy-start
  138.8 53.6 %all-to-all-start.4 = ((bf16[32,24,1536]{2,1,0:T(8,128)(2,1)}), bf16[32,24,1536]{2,1,0:T(8,128)(2,1)S(1)}, u32[]{:S(2)}, u32[]{:S(2)}) async-start(bf16[32,24,1536]{2,1,0:T(8,128)(2,1)} %copy-done), calls=%async_computation.4 | async-start | bytes 4718592 | tf_op jit(solution)/shard_map/all_to_all | solution.py:38
  147.4 14.9 %collective-permute-start.3 = (bf16[384,768]{1,0:T(8,128)(2,1)S(1)}, bf16[384,768]{1,0:T(8,128)(2,1)}, u32[]{:S(2)}, u32[]{:S(2)}) collective-permute-start(bf16[384,768]{1,0:T(8,128)(2,1)S(1)} %slice.14), channel_id=1, source_target_pairs={{0,3},{1,0},{2,1},{3,2},{4,7},{5,4},{6,5},{7,6},{8,11},{9,8},{10,9... | collective-permute-start | bytes 1769480 | tf_op jit(solution)/shard_map/ppermute | solution.py:42
  151.0 15.8 %collective-permute-start.1 = (bf16[384,768]{1,0:T(8,128)(2,1)S(1)}, bf16[384,768]{1,0:T(8,128)(2,1)}, u32[]{:S(2)}, u32[]{:S(2)}) collective-permute-start(bf16[384,768]{1,0:T(8,128)(2,1)S(1)} %slice.13), channel_id=1, source_target_pairs={{0,1},{1,2},{2,3},{3,0},{4,5},{5,6},{6,7},{7,4},{8,9},{9,10},{10,1... | collective-permute-start | bytes 1769480 | tf_op jit(solution)/shard_map/ppermute | solution.py:42
  192.5 11.6 %copy-start.5 = (bf16[384,768]{1,0:T(8,128)(2,1)S(1)}, bf16[384,768]{1,0:T(8,128)(2,1)}, u32[]{:S(2)}) copy-start(bf16[384,768]{1,0:T(8,128)(2,1)} %get-tuple-element.37) | copy-start | bytes 1769476
  192.5 25.0 %copy-start.4 = (bf16[384,768]{1,0:T(8,128)(2,1)S(1)}, bf16[384,768]{1,0:T(8,128)(2,1)}, u32[]{:S(2)}) copy-start(bf16[384,768]{1,0:T(8,128)(2,1)} %get-tuple-element.34) | copy-start | bytes 1769476
  192.5 59.5 %all-to-all-start.3 = ((bf16[32,64,1024]{2,1,0:T(8,128)(2,1)}), bf16[32,64,1024]{2,1,0:T(8,128)(2,1)}, u32[]{:S(2)}, u32[]{:S(2)}) async-start(bf16[32,64,1024]{2,1,0:T(8,128)(2,1)} %get-tuple-element.28), calls=%async_computation.3 | async-start | bytes 8388608 | tf_op jit(solution)/shard_map/all_to_all | solution.py:38
  201.3 16.4 %copy-start.3 = (bf16[384,768]{1,0:T(8,128)(2,1)S(1)}, bf16[384,768]{1,0:T(8,128)(2,1)}, u32[]{:S(2)}) copy-start(bf16[384,768]{1,0:T(8,128)(2,1)} %get-tuple-element.38) | copy-start | bytes 1769476
  201.3 16.2 %collective-permute-start.4 = (bf16[384,768]{1,0:T(8,128)(2,1)}, bf16[384,768]{1,0:T(8,128)(2,1)S(1)}, u32[]{:S(2)}, u32[]{:S(2)}) collective-permute-start(bf16[384,768]{1,0:T(8,128)(2,1)} %get-tuple-element.35), channel_id=1, source_target_pairs={{0,1},{1,2},{2,3},{3,0},{4,5},{5,6},{6,7},{7,4},{8,9},{9,10},{10,1... | collective-permute-start | bytes 1769480 | tf_op jit(solution)/shard_map/ppermute | solution.py:42
  201.4 16.3 %collective-permute-start.8 = (bf16[384,768]{1,0:T(8,128)(2,1)}, bf16[384,768]{1,0:T(8,128)(2,1)S(1)}, u32[]{:S(2)}, u32[]{:S(2)}) collective-permute-start(bf16[384,768]{1,0:T(8,128)(2,1)} %get-tuple-element.39), channel_id=1, source_target_pairs={{0,3},{1,0},{2,1},{3,2},{4,7},{5,4},{6,5},{7,6},{8,11},{9,8},{10,9... | collective-permute-start | bytes 1769480 | tf_op jit(solution)/shard_map/ppermute | solution.py:42
  204.1 26.1 %collective-permute-start.6 = (bf16[384,768]{1,0:T(8,128)(2,1)}, bf16[384,768]{1,0:T(8,128)(2,1)S(1)}, u32[]{:S(2)}, u32[]{:S(2)}) collective-permute-start(bf16[384,768]{1,0:T(8,128)(2,1)} %get-tuple-element.36), channel_id=1, source_target_pairs={{0,1},{1,2},{2,3},{3,0},{4,5},{5,6},{6,7},{7,4},{8,9},{9,10},{10,1... | collective-permute-start | bytes 1769480 | tf_op jit(solution)/shard_map/ppermute | solution.py:42
  204.1 26.1 %collective-permute-start.7 = (bf16[384,768]{1,0:T(8,128)(2,1)S(1)}, bf16[384,768]{1,0:T(8,128)(2,1)S(1)}, u32[]{:S(2)}, u32[]{:S(2)}) collective-permute-start(bf16[384,768]{1,0:T(8,128)(2,1)S(1)} %copy-done.5), channel_id=1, source_target_pairs={{0,3},{1,0},{2,1},{3,2},{4,7},{5,4},{6,5},{7,6},{8,11},{9,8},{10,9... | collective-permute-start | bytes 1769480 | tf_op jit(solution)/shard_map/ppermute | solution.py:42
  217.5 25.3 %copy-start.1 = (bf16[768,768]{1,0:T(8,128)(2,1)S(1)}, bf16[768,768]{1,0:T(8,128)(2,1)}, u32[]{:S(2)}) copy-start(bf16[768,768]{1,0:T(8,128)(2,1)} %get-tuple-element.33.g0) | copy-start | bytes 3538948
  217.6 25.1 %collective-permute-start.5 = (bf16[384,768]{1,0:T(8,128)(2,1)S(1)}, bf16[384,768]{1,0:T(8,128)(2,1)S(1)}, u32[]{:S(2)}, u32[]{:S(2)}) collective-permute-start(bf16[384,768]{1,0:T(8,128)(2,1)S(1)} %add_convert_fusion.1), channel_id=1, source_target_pairs={{0,1},{1,2},{2,3},{3,0},{4,5},{5,6},{6,7},{7,4},{8,9},{9,10},{10,1... | collective-permute-start | bytes 1769480 | tf_op jit(solution)/shard_map/ppermute | solution.py:42
  217.9 24.9 %collective-permute-start.9 = (bf16[384,768]{1,0:T(8,128)(2,1)S(1)}, bf16[384,768]{1,0:T(8,128)(2,1)S(1)}, u32[]{:S(2)}, u32[]{:S(2)}) collective-permute-start(bf16[384,768]{1,0:T(8,128)(2,1)S(1)} %add_convert_fusion), channel_id=1, source_target_pairs={{0,3},{1,0},{2,1},{3,2},{4,7},{5,4},{6,5},{7,6},{8,11},{9,8},{10,9... | collective-permute-start | bytes 1769480 | tf_op jit(solution)/shard_map/ppermute | solution.py:42

commit v4 on v3

--- a/solution.py
+++ b/solution.py
@@ -40,6 +40,32 @@
 
 def shifted(x, by):
     return lax.ppermute(x, "dp", [(i, (i + by) % REP) for i in range(REP)])
+
+
+def along_first(x, s):
+    return lax.ppermute(x, "expert", [(i, (i + 8 * s) % COUNT) for i in range(COUNT)])
+
+
+def along_second(x, t):
+    return lax.ppermute(x, "expert", [(i, i // 8 * 8 + (i + 2 * t) % 8) for i in range(COUNT)])
+
+
+def along_third(x):
+    return lax.ppermute(x, "expert", [(i, i ^ 1) for i in range(COUNT)])
+
+
+def spread_offsets(x):
+    first = x[..., :SIDE]
+    second = x[..., SIDE:]
+    a = [first[0]] + [along_first(first[s], s) for s in range(1, 4)]
+    b = [second[:, 0]] + [along_second(second[:, t], t) for t in range(1, 4)]
+    a = [jnp.stack([g[t] for g in a]) for t in range(4)]
+    b = [jnp.stack([g[s] for g in b]) for s in range(4)]
+    a = jnp.stack([a[0]] + [along_second(a[t], t) for t in range(1, 4)])
+    b = jnp.stack([b[0]] + [along_first(b[s], s) for s in range(1, 4)], axis=1)
+    done = jnp.concatenate([a, b], axis=-1)
+    other = along_third(done[:, :, 1])
+    return jnp.concatenate([done[:, :, 0], other], axis=0).reshape(COUNT, *x.shape[3:])
 
 
 def both(a, b):
@@ -93,23 +119,6 @@
         compiler_params=pltpu.CompilerParams(vmem_limit_bytes=12 << 20),
         name="pick",
     )(plan, src)
-
-
-def place_body(plan, src, held, out):
-    copy_picked(plan, src, out, slice(0, SIDE))
-
-
-def place_picked(plan, src, held):
-    return pl.pallas_call(
-        place_body,
-        grid=(1,),
-        out_shape=jax.ShapeDtypeStruct(held.shape, bf16),
-        in_specs=[SMEM, VMEM, pl.BlockSpec(memory_space=pltpu.HBM)],
-        out_specs=pl.BlockSpec(src.shape, lambda i: (0, 0, 2)),
-        input_output_aliases={2: 0},
-        compiler_params=pltpu.CompilerParams(vmem_limit_bytes=50 << 20),
-        name="place",
-    )(plan, src, held)
 
 
 def dispatch_body(routes, gates, plan, tokens, cotangent, out, place, gated):
@@ -188,7 +197,7 @@
     )(back, place, gated)
 
 
-def expert_body(mine, rows, w0, w1, w2a, w2b, w3, back, g0, g1t, g1b, g2t, g2b, g3t, g3b, win, wout, hid, pgrad, gout, gpack, sem, gsem):
+def expert_body(mine, sent, w0, w1, w2, w3, given, g0, g1t, g1b, g2t, g2b, g3t, g3b, win, wout, hid, pgrad, gout, gpack, rows, back, sem, gsem, rsem, bsem):
     r = mine[0]
     copies = []
 
@@ -218,18 +227,30 @@
 
     fetch(0, w0, 0, SIDE, 0)
     fetch(1, w1, 0, SIDE, 0)
-    fetch(2, w2a, 0, HALF, 0)
-    fetch(2, w2b, HALF, SIDE, 0)
+    fetch(2, w2, 0, SIDE, 0)
     fetch(3, w3, 0, SIDE, 0)
+    group = 8
+    size = group * ROWS
+
+    def incoming(i):
+        own = pl.ds(i * group, group)
+        return pltpu.make_async_copy(sent.at[own], rows.at[own], rsem.at[i])
+
+    def outgoing(i):
+        own = pl.ds(i * group, group)
+        return pltpu.make_async_copy(back.at[own], given.at[own], bsem.at[i])
+
+    blocks = COUNT // group
+    incoming(0).start()
     for c in copies:
         c.start()
+    for i in range(1, blocks):
+        incoming(i).start()
     for c in copies:
         c.wait()
 
-    group = 8
-    size = group * ROWS
-
     def step(i, carry):
+        incoming(i).wait()
         own = pl.ds(pl.multiple_of(i * group, group), group)
         at = pl.ds(pl.multiple_of(i * size, size), size)
         x = rows[own, 0:ROWS, :].reshape(size, -1)
@@ -248,9 +269,10 @@
         pgrad[at, SIDE:] = (hgrad * swish).astype(bf16)
         part = lax.dot_general(pgrad[at, :], win[...], COL_T, preferred_element_type=f32).astype(bf16)
         back[own, ROWS : 2 * ROWS, :] = part.reshape(group, ROWS, -1)
+        outgoing(i).start()
         return carry
 
-    lax.fori_loop(0, COUNT // group, step, 0)
+    lax.fori_loop(0, blocks, step, 0)
     for q in range(REP):
         x = rows[:, 0:ROWS, RI * q : RI * q + RI].reshape(COUNT * ROWS, RI)
         grad = lax.dot_general(x, pgrad[...], ROW_T, preferred_element_type=f32).astype(bf16)
@@ -272,6 +294,8 @@
             copies.append(pltpu.make_async_copy(gpack.at[q, at : at + HALF], out, gsem.at[len(copies)]))
     for c in copies:
         c.start()
+    for i in range(blocks):
+        outgoing(i).wait()
     for c in copies:
         c.wait()
 
@@ -284,8 +308,8 @@
     return pl.pallas_call(
         expert_body,
         out_shape=(jax.ShapeDtypeStruct(rows.shape, bf16), piece) + (half,) * 6,
-        in_specs=[SMEM, VMEM] + [ANY] * 5,
-        out_specs=(VMEM,) + (ANY,) * 7,
+        in_specs=[SMEM] + [ANY] * 5,
+        out_specs=(ANY,) * 8,
         scratch_shapes=[
             pltpu.VMEM((REP * RI, 2 * SIDE), bf16),
             pltpu.VMEM((REP * RO, width), bf16),
@@ -293,8 +317,12 @@
             pltpu.VMEM((total, 2 * SIDE), bf16),
             pltpu.VMEM((SIDE, width), bf16),
             pltpu.VMEM((REP, SIDE, SIDE), bf16),
-            pltpu.SemaphoreType.DMA((25,)),
+            pltpu.VMEM(rows.shape, bf16),
+            pltpu.VMEM(rows.shape, bf16),
+            pltpu.SemaphoreType.DMA((24,)),
             pltpu.SemaphoreType.DMA((2 * REP - 1,)),
+            pltpu.SemaphoreType.DMA((4,)),
+            pltpu.SemaphoreType.DMA((4,)),
         ],
         cost_estimate=pl.CostEstimate(flops=14_500_000_000, bytes_accessed=18_000_000, transcendentals=800_000),
         name="expert",
@@ -375,23 +403,26 @@
 ):
     mine = lax.axis_index("dp").astype(jnp.int32).reshape(1)
     slim = (COUNT, SIDE // COUNT, SIDE)
-    wide = (COUNT, SIDE // COUNT, 3 * SIDE)
     weights = exchange(pack(((weight_in[0], weight_out[0]),), SIDE).reshape(slim))
-    held = pack(((first_in[0], first_out[0]), (second_in[0], second_out[0])), 3 * SIDE)
-    filled = place_picked(expert_plan, weights, held.reshape(wide))
-    spread = exchange(filled)
-    own = spread[:, :, 2 * SIDE :].reshape(SIDE, SIDE)
+    held = pack(((first_in[0], first_out[0]), (second_in[0], second_out[0])), 2 * SIDE)
+    spread = spread_offsets(held.reshape(4, 4, 2, SIDE // COUNT, 2 * SIDE))
+    here = lax.axis_index("expert").astype(jnp.int32)
+    each = jnp.arange(COUNT, dtype=jnp.int32)
+    source = (here + expert_plan) % 2 * 16 + (here // 2 - expert_plan // 2) % 4 * 4 + (here // 8 - expert_plan // 8) % 4
+    held_here = jnp.sum(jnp.where(each == here, expert_plan, 0))
+    holder = (
+        (held_here // 8 + each // 8) % 4 * 8 + (held_here // 2 + each // 2) % 4 * 2 + (held_here + each) % 2
+    )
+    picked = pick(expert_plan, weights, SIDE)
+    own = exchange(picked).reshape(SIDE, SIDE)
     outgoing, place, gated = dispatch(
         routes.transpose(2, 0, 1), gate_weights.transpose(2, 0, 1), expert_plan.reshape(-1, 1), tokens, cotangent
     )
-    before = shifted(own, 1)
-    after = shifted(own, 3)
-    top = shifted(before[:HALF], 1)
-    bottom = shifted(after[HALF:], 3)
-    parts = (own, before, top, bottom, after)
+    parts = (own,) + tuple(shifted(own, r) for r in range(1, REP))
     arrived = exchange(outgoing)
-    moved = pick(expert_plan, spread, 2 * SIDE)
-    moments = exchange(moved).reshape(SIDE, 2 * SIDE)
+    moved = pick(source, spread, 2 * SIDE)
+    landed = exchange(moved)
+    moments = pick(holder, landed, 2 * SIDE).reshape(SIDE, 2 * SIDE)
     back, g0, g1t, g1b, g2t, g2b, g3t, g3b = expert(mine, arrived, parts)
     from_before = shifted(g2t, 1)
     from_after = shifted(g2b, 3)

time: 259 us -> 272 us (1.050)
  starting transfers between devices: 51.1 us -> 63.1 us
  waiting for transfers between devices: 149 us -> 137 us
  local copies, waits for them, and re-layouts: 5.46 us -> 12.7 us
  other arithmetic: 0.27 us -> 6.26 us
  between operations: 0.82 us -> 3.62 us
  Pallas kernels: 48.8 us -> 46 us
    all_to_all x5, waiting for transfers between devices: 101 us -> 17.4 us  [exchange(): return lax.all_to_all(x, 'expert', split_axis=0, concat_axis=0, tiled=True)]
    ppermute x0 -> x13, waiting for transfers between devices: none -> 54 us  [the longest x6 49.4 us: along_first(): lax.ppermute(x, 'expert', [(i, (i + 8 * s) % COUNT) for i in range(COUNT)])]
    ppermute x10 -> x9, waiting for transfers between devices: 48.3 us -> 65.3 us  [shifted(): return lax.ppermute(x, 'dp', [(i, (i + by) % REP) for i in range(REP)])]
    ppermute x0 -> x13, starting transfers between devices: none -> 16.3 us  [the longest x6 7.92 us: along_first(): lax.ppermute(x, 'expert', [(i, (i + 8 * s) % COUNT) for i in range(COUNT)])]
    squeeze x0 -> x6, local copies, waits for them, and re-layouts: none -> 4.64 us  [the longest x4 3.55 us: spread_offsets(): b = [second[:, 0]] + [along_second(second[:, t], t) for t in range(1, 4)]]
    all_to_all x5, starting transfers between devices: 37.4 us -> 33.9 us  [exchange(): return lax.all_to_all(x, 'expert', split_axis=0, concat_axis=0, tiled=True)]
    pallas_call x1, Pallas kernels: 25.6 us -> 22.3 us  [expert(): pl.pallas_call(expert_body, out_shape=(jax.ShapeDtypeStruct(rows.shape, b...]
    slice x3 -> x7, local copies, waits for them, and re-layouts: 3.29 us -> 5.94 us  [the longest x3 3.06 us: spread_offsets(): b = [jnp.stack([g[s] for g in b]) for s in range(4)]]
  transfers between devices with their start and end apart: 15 -> 27, of which waited for: 9 -> 11; matrix products, arithmetic and copies ran while one was open for 2% -> 7% of each run, Pallas kernels for 16% -> 15%
where the time goes in v4:
time: 272 us; the launch traced here: 268 us
  waiting for transfers between devices  137 us (50%)
  starting transfers between devices  63.1 us (23%)
  Pallas kernels  46 us (17%)
  local copies, waits for them, and re-layouts  12.7 us (5%)
  other arithmetic  6.26 us (2%)
  between operations  3.62 us (1%)
    ppermute x9, waiting for transfers between devices, shifted(): return lax.ppermute(x, 'dp', [(i, (i + by) % REP) for i in range(REP)])  65.3 us
    ppermute x6, waiting for transfers between devices, along_first(): lax.ppermute(x, 'expert', [(i, (i + 8 * s) % COUNT) for i in range(COUNT)])  49.4 us
    all_to_all x5, starting transfers between devices, exchange(): return lax.all_to_all(x, 'expert', split_axis=0, concat_axis=0, tiled=True)  33.9 us
    pallas_call x1, Pallas kernels, expert(): pl.pallas_call(expert_body, out_shape=(jax.ShapeDtypeStruct(rows.shape, b...  22.3 us
    all_to_all x5, waiting for transfers between devices, exchange(): return lax.all_to_all(x, 'expert', split_axis=0, concat_axis=0, tiled=True)  17.4 us
    ppermute x9, starting transfers between devices, shifted(): return lax.ppermute(x, 'dp', [(i, (i + by) % REP) for i in range(REP)])  12.9 us
    ppermute x6, starting transfers between devices, along_first(): lax.ppermute(x, 'expert', [(i, (i + 8 * s) % COUNT) for i in range(COUNT)])  7.92 us
    ppermute x6, starting transfers between devices, along_second(): lax.ppermute(x, 'expert', [(i, i // 8 * 8 + (i + 2 * t) % 8) for i in ran...  7.51 us
  transfers between devices with their start and end apart: 27, of which 11 were waited for; matrix products, arithmetic and copies ran while one was open for 7% of the time, Pallas kernels for 15%

profile of v4, /device:TPU:1, one launch (start us, length us, event | category | flops | bytes accessed | tf_op | source)
XLA Modules:
  0.0 268.4 jit_solution(6980528491954749584)
XLA Ops:
  0.6 2.3 pack.2
  3.0 9.6 %all-to-all-start.1 = ((bf16[32,24,768]{2,1,0:T(8,128)(2,1)}), bf16[32,24,768]{2,1,0:T(8,128)(2,1)S(1)}, u32[]{:S(2)}, u32[]{:S(2)}) async-start(bf16[32,24,768]{2,1,0:T(8,128)(2,1)} %bitcast.86), calls=%async_computation.1 | async-start | bytes 2359296 | tf_op jit(solution)/shard_map/all_to_all | solution.py:38
  12.6 3.9 %pack.3 = bf16[768,1536]{1,0:T(8,128)(2,1)} custom-call(f32[256,1536]{1,0:T(8,128)} %bitcast.87, f32[192,1024]{1,0:T(8,128)} %bitcast.89, f32[256,1536]{1,0:T(8,128)} %bitcast.88, f32[192,1024]{1,0:T(8,128)} %bitcast.90), custom_call_target="tpu_custom_call" | custom-call | tf_op jit(solution)/shard_map/pack/pallas_call | solution.py:91
  16.5 1.4 slice_bitcast_fusion.4
  17.9 0.7 copy.22
  18.6 2.6 collective-permute-start.11
  21.2 0.7 copy.21
  21.9 0.6 collective-permute-start.10
  22.5 0.7 copy.20
  23.2 0.6 collective-permute-start.9
  23.8 0.9 slice_bitcast_fusion.7
  24.7 2.5 collective-permute-start.5
  27.2 0.5 collective-permute-start.4
  27.7 9.5 %all-to-all-done.1.src = bf16[32,24,768]{2,1,0:T(8,128)(2,1)S(1)} async-done(((bf16[32,24,768]{2,1,0:T(8,128)(2,1)}), bf16[32,24,768]{2,1,0:T(8,128)(2,1)S(1)}, u32[]{:S(2)}, u32[]{:S(2)}) %all-to-all-start.1) | async-done | bytes 1179680 | tf_op jit(solution)/shard_map/all_to_all | solution.py:38
  37.2 1.6 pick.3
  38.8 3.7 %all-to-all-start.2 = ((bf16[32,24,768]{2,1,0:T(8,128)(2,1)}), bf16[32,24,768]{2,1,0:T(8,128)(2,1)S(1)}, u32[]{:S(2)}, u32[]{:S(2)}) async-start(bf16[32,24,768]{2,1,0:T(8,128)(2,1)} %pick.3), calls=%async_computation.2 | async-start | bytes 2359296 | tf_op jit(solution)/shard_map/all_to_all | solution.py:38
  42.6 0.8 slice_bitcast_fusion.15
  43.4 0.7 copy.19.plan
  44.1 5.0 %dispatch.1 = (bf16[32,64,1024]{2,1,0:T(8,128)(2,1)}, bf16[2,64,512]{2,1,0:T(8,128)(2,1)}, bf16[2,128,512]{2,1,0:T(8,128)(2,1)}) custom-call(s32[6,2,64]{2,1,0:T(2,128)} %bitcast.99, f32[6,2,64]{2,1,0:T(2,128)} %bitcast.100, s32[32,1]{1,0:T(8,128)} %copy.19.plan, bf16[2,64,1024]{2,1,0:T(8,128)(2,1)} %tokens.1, bf16[2,64,1024]{2,1,0:T(8,128)(2,1)} %cotangent.1), custom_call_target="tpu_custom_call" | custom-call | tf_op jit(solution)/shard_map/dispatch/pallas_call | solution.py:164
  49.0 0.3 collective-permute-start.3
  49.4 1.0 fusion.22
  50.4 1.0 fusion.21
  51.4 1.0 fusion.20
  52.5 2.4 collective-permute-start.14
  55.0 0.7 collective-permute-start.13
  55.7 4.4 %all-to-all-done.2 = bf16[32,24,768]{2,1,0:T(8,128)(2,1)S(1)} async-done(((bf16[32,24,768]{2,1,0:T(8,128)(2,1)}), bf16[32,24,768]{2,1,0:T(8,128)(2,1)S(1)}, u32[]{:S(2)}, u32[]{:S(2)}) %all-to-all-start.2) | async-done | bytes 1179680 | tf_op jit(solution)/shard_map/all_to_all | solution.py:38
  60.1 5.0 %all-to-all-start = ((bf16[32,64,1024]{2,1,0:T(8,128)(2,1)}), bf16[32,64,1024]{2,1,0:T(8,128)(2,1)}, u32[]{:S(2)}, u32[]{:S(2)}) async-start(bf16[32,64,1024]{2,1,0:T(8,128)(2,1)} %get-tuple-element.27), calls=%async_computation | async-start | bytes 8388608 | tf_op jit(solution)/shard_map/all_to_all | solution.py:38
  65.2 1.5 collective-permute-start.12
  66.6 1.0 fusion.19
  67.7 1.0 fusion.18
  68.8 2.5 collective-permute-start.8
  71.4 0.6 collective-permute-start.7
  72.1 0.7 collective-permute-start.6
  72.8 49.4 %collective-permute-done.12 = bf16[4,2,24,768]{3,2,0,1:T(8,128)(2,1)S(1)} collective-permute-done((bf16[4,2,24,768]{3,2,0,1:T(8,128)(2,1)S(1)}, bf16[4,2,24,768]{3,2,0,1:T(8,128)(2,1)S(1)}, u32[]{:S(2)}, u32[]{:S(2)}) %collective-permute-start.12) | collective-permute-done | bytes 294944 | tf_op jit(solution)/shard_map/ppermute | solution.py:46
  122.2 0.2 collective-permute-done.7
  122.5 4.4 %collective-permute-done.6 = bf16[4,2,24,768]{3,2,1,0:T(8,128)(2,1)S(1)} collective-permute-done((bf16[4,2,24,768]{3,2,1,0:T(8,128)(2,1)S(1)}, bf16[4,2,24,768]{3,2,1,0:T(8,128)(2,1)S(1)}, u32[]{:S(2)}, u32[]{:S(2)}) %collective-permute-start.6) | collective-permute-done | bytes 294944 | tf_op jit(solution)/shard_map/ppermute | solution.py:50
  126.8 0.2 maximum_maximum_fusion
  127.2 0.9 collective-permute-start.15
  128.0 0.6 fusion.1
  128.7 1.2 collective-permute-start
  129.9 2.5 collective-permute-start.1
  132.3 1.2 collective-permute-start.2
  133.5 1.5 pad_maximum_fusion
  135.0 0.7 pick.4
  135.7 1.4 copy-done
  137.1 7.8 %all-to-all-start.4 = ((bf16[32,24,1536]{2,1,0:T(8,128)(2,1)}), bf16[32,24,1536]{2,1,0:T(8,128)(2,1)S(1)}, u32[]{:S(2)}, u32[]{:S(2)}) async-start(bf16[32,24,1536]{2,1,0:T(8,128)(2,1)} %copy-done), calls=%async_computation.4 | async-start | bytes 4718592 | tf_op jit(solution)/shard_map/all_to_all | solution.py:38
  144.8 12.6 %collective-permute-done.w1 = bf16[768,768]{1,0:T(8,128)(2,1)} collective-permute-done((bf16[768,768]{1,0:T(8,128)(2,1)S(1)}, bf16[768,768]{1,0:T(8,128)(2,1)}, u32[]{:S(2)}, u32[]{:S(2)}) %collective-permute-start) | collective-permute-done | bytes 1179680 | tf_op jit(solution)/shard_map/ppermute | solution.py:42
  157.5 26.3 %collective-permute-done.1.w2 = bf16[768,768]{1,0:T(8,128)(2,1)} collective-permute-done((bf16[768,768]{1,0:T(8,128)(2,1)S(1)}, bf16[768,768]{1,0:T(8,128)(2,1)}, u32[]{:S(2)}, u32[]{:S(2)}) %collective-permute-start.1) | collective-permute-done | bytes 1179680 | tf_op jit(solution)/shard_map/ppermute | solution.py:42
  183.8 22.3 %expert.1 = (bf16[32,64,1024]{2,1,0:T(8,128)(2,1)}, bf16[768,768]{1,0:T(8,128)(2,1)}, bf16[384,768]{1,0:T(8,128)(2,1)}, bf16[384,768]{1,0:T(8,128)(2,1)}, bf16[3...) custom-call(s32[1]{0:T(128)} %bitcast.mine, ...), custom_call_target="tpu_custom_call" | custom-call | flops 14499999744 | bytes 18000000 | tf_op jit(solution)/shard_map/expert/pallas_call | solution.py:308
  206.1 7.8 %all-to-all-start.3 = ((bf16[32,64,1024]{2,1,0:T(8,128)(2,1)}), bf16[32,64,1024]{2,1,0:T(8,128)(2,1)}, u32[]{:S(2)}, u32[]{:S(2)}) async-start(bf16[32,64,1024]{2,1,0:T(8,128)(2,1)} %get-tuple-element.28), calls=%async_computation.3 | async-start | bytes 8388608 | tf_op jit(solution)/shard_map/all_to_all | solution.py:38
  213.9 1.1 collective-permute-start.16
  215.0 1.6 collective-permute-start.20
  216.7 2.7 collective-permute-start.19
  219.3 10.7 %collective-permute-done.16 = bf16[384,768]{1,0:T(8,128)(2,1)S(1)} collective-permute-done((bf16[384,768]{1,0:T(8,128)(2,1)}, bf16[384,768]{1,0:T(8,128)(2,1)S(1)}, u32[]{:S(2)}, u32[]{:S(2)}) %collective-permute-start.16) | collective-permute-done | bytes 589856 | tf_op jit(solution)/shard_map/ppermute | solution.py:42
  230.1 2.0 add_convert_fusion.1
  232.1 1.0 add_convert_fusion
  233.1 2.7 collective-permute-start.21
  238.3 0.7 fusion.plan
  239.0 0.7 pick.5
  239.7 3.0 %collective-permute-done.18.g1b = bf16[384,768]{1,0:T(8,128)(2,1)S(1)} collective-permute-done((bf16[384,768]{1,0:T(8,128)(2,1)}, bf16[384,768]{1,0:T(8,128)(2,1)S(1)}, u32[]{:S(2)}, u32[]{:S(2)}) %collective-permute-start.18) | collective-permute-done | bytes 589856 | tf_op jit(solution)/shard_map/ppermute | solution.py:42
  242.7 12.6 %collective-permute-done.17.g1t = bf16[384,768]{1,0:T(8,128)(2,1)} collective-permute-done((bf16[384,768]{1,0:T(8,128)(2,1)}, bf16[384,768]{1,0:T(8,128)(2,1)}, u32[]{:S(2)}, u32[]{:S(2)}) %collective-permute-start.17) | collective-permute-done | bytes 589856 | tf_op jit(solution)/shard_map/ppermute | solution.py:42
  255.4 5.7 %update.1 = (bf16[256,1536]{1,0:T(8,128)(2,1)}, bf16[192,1024]{1,0:T(8,128)(2,1)}, f32[256,1536]{1,0:T(8,128)}, f32[256,1536]{1,0:T(8,128)}, f32[192,1024]{1,0:T(8,128)}, /*index=5*/f32[192,1024]{1,0:T(8,128)}) custom-call(bf16[768,768]{1,0:T(8,128)(2,1)S(1)} %bitcast.81, bf16[768,1536]{1,0:T(8,128)(2,1)S(1)} %bitcast.75, bf16[768,768]{1,0:T(8,128)(2,1)S(1)} %copy-done.3, ...), custom_call_target="tpu_custom_call" | custom-call | tf_op jit(solution)/shard_map/update/pallas_call | solution.py:374
  261.0 3.5 %all-to-all-done.3.back = bf16[32,64,1024]{2,1,0:T(8,128)(2,1)} async-done(((bf16[32,64,1024]{2,1,0:T(8,128)(2,1)}), bf16[32,64,1024]{2,1,0:T(8,128)(2,1)}, u32[]{:S(2)}, u32[]{:S(2)}) %all-to-all-start.3) | async-done | bytes 4194336 | tf_op jit(solution)/shard_map/all_to_all | solution.py:38
  264.6 3.8 %combine.1 = (bf16[2,64,1024]{2,1,0:T(8,128)(2,1)}, bf16[2,64,1024]{2,1,0:T(8,128)(2,1)}) custom-call(bf16[32,64,1024]{2,1,0:T(8,128)(2,1)} %all-to-all-done.3.back, bf16[2,64,512]{2,1,0:T(8,128)(2,1)} %get-tuple-element.29.place, bf16[2,128,512]{2,1,0:T(8,128)(2,1)} %get-tuple-element.30.gated), custom_call_target="tpu_custom_call" | custom-call | tf_op jit(solution)/shard_map/combine/pallas_call | solution.py:191
  (57 shorter events, 0.6 us)
Async XLA Ops:
  3.0 34.2 %all-to-all-start.1 = ((bf16[32,24,768]{2,1,0:T(8,128)(2,1)}), bf16[32,24,768]{2,1,0:T(8,128)(2,1)S(1)}, u32[]{:S(2)}, u32[]{:S(2)}) async-start(bf16[32,24,768]{2,1,0:T(8,128)(2,1)} %bitcast.86), calls=%async_computation.1 | async-start | bytes 2359296 | tf_op jit(solution)/shard_map/all_to_all | solution.py:38
  16.5 7.3 %copy-start.5 = (bf16[768,1536]{1,0:T(8,128)(2,1)S(1)}, bf16[768,1536]{1,0:T(8,128)(2,1)}, u32[]{:S(2)}) copy-start(bf16[768,1536]{1,0:T(8,128)(2,1)} %pack.3) | copy-start | bytes 7077892
  18.6 18.6 %copy-start.4 = (s32[32]{0:T(128)S(1)}, s32[32]{0:T(128)}, u32[]{:S(2)}) copy-start(s32[32]{0:T(128)} %plan.1) | copy-start | bytes 388
  18.6 30.4 %collective-permute-start.11 = (bf16[4,2,24,768]{3,2,0,1:T(8,128)(2,1)}, bf16[4,2,24,768]{3,2,0,1:T(8,128)(2,1)}, u32[]{:S(2)}, u32[]{:S(2)}) collective-permute-start(bf16[4,2,24,768]{3,2,0,1:T(8,128)(2,1)} %copy.22), channel_id=1, source_target_pairs={{0,24},{4,28},{8,0},{12,4},{16,8},{20,12},{24,16},{28,20},{32,56},... | collective-permute-start | bytes 884744 | tf_op jit(solution)/shard_map/ppermute | solution.py:50
  21.9 28.5 %collective-permute-start.10 = (bf16[4,2,24,768]{3,2,0,1:T(8,128)(2,1)}, bf16[4,2,24,768]{3,2,0,1:T(8,128)(2,1)}, u32[]{:S(2)}, u32[]{:S(2)}) collective-permute-start(bf16[4,2,24,768]{3,2,0,1:T(8,128)(2,1)} %copy.21), channel_id=1, source_target_pairs={{0,16},{4,20},{8,24},{12,28},{16,0},{20,4},{24,8},{28,12},{32,48},... | collective-permute-start | bytes 884744 | tf_op jit(solution)/shard_map/ppermute | solution.py:50
  23.2 28.2 %collective-permute-start.9 = (bf16[4,2,24,768]{3,2,0,1:T(8,128)(2,1)}, bf16[4,2,24,768]{3,2,0,1:T(8,128)(2,1)}, u32[]{:S(2)}, u32[]{:S(2)}) collective-permute-start(bf16[4,2,24,768]{3,2,0,1:T(8,128)(2,1)} %copy.20), channel_id=1, source_target_pairs={{0,8},{4,12},{8,16},{12,20},{16,24},{20,28},{24,0},{28,4},{32,40},... | collective-permute-start | bytes 884744 | tf_op jit(solution)/shard_map/ppermute | solution.py:50
  24.7 40.4 %collective-permute-start.5 = (bf16[4,2,24,768]{3,2,1,0:T(8,128)(2,1)}, bf16[4,2,24,768]{3,2,1,0:T(8,128)(2,1)}, u32[]{:S(2)}, u32[]{:S(2)}) collective-permute-start(bf16[4,2,24,768]{3,2,1,0:T(8,128)(2,1)} %get-tuple-element.57), channel_id=1, source_target_pairs={{0,96},{4,100},{8,104},{12,108},{16,112},{20,116},{24,120},{28,124... | collective-permute-start | bytes 884744 | tf_op jit(solution)/shard_map/ppermute | solution.py:46
  27.2 40.5 %collective-permute-start.4 = (bf16[4,2,24,768]{3,2,1,0:T(8,128)(2,1)}, bf16[4,2,24,768]{3,2,1,0:T(8,128)(2,1)}, u32[]{:S(2)}, u32[]{:S(2)}) collective-permute-start(bf16[4,2,24,768]{3,2,1,0:T(8,128)(2,1)} %get-tuple-element.58), channel_id=1, source_target_pairs={{0,64},{4,68},{8,72},{12,76},{16,80},{20,84},{24,88},{28,92},{32,9... | collective-permute-start | bytes 884744 | tf_op jit(solution)/shard_map/ppermute | solution.py:46
  38.8 21.3 %all-to-all-start.2 = ((bf16[32,24,768]{2,1,0:T(8,128)(2,1)}), bf16[32,24,768]{2,1,0:T(8,128)(2,1)S(1)}, u32[]{:S(2)}, u32[]{:S(2)}) async-start(bf16[32,24,768]{2,1,0:T(8,128)(2,1)} %pick.3), calls=%async_computation.2 | async-start | bytes 2359296 | tf_op jit(solution)/shard_map/all_to_all | solution.py:38
  43.4 9.1 %copy-start.14 = (bf16[1,2,24,768]{3,2,0,1:T(8,128)(2,1)S(1)}, bf16[1,2,24,768]{3,2,0,1:T(8,128)(2,1)}, u32[]{:S(2)}) copy-start(bf16[1,2,24,768]{3,2,0,1:T(8,128)(2,1)} %get-tuple-element.49) | copy-start | bytes 221188
  43.4 11.6 %copy-start.13 = (bf16[1,2,24,768]{3,2,0,1:T(8,128)(2,1)S(1)}, bf16[1,2,24,768]{3,2,0,1:T(8,128)(2,1)}, u32[]{:S(2)}) copy-start(bf16[1,2,24,768]{3,2,0,1:T(8,128)(2,1)} %get-tuple-element.50) | copy-start | bytes 221188
  49.0 19.7 %collective-permute-start.3 = (bf16[4,2,24,768]{3,2,1,0:T(8,128)(2,1)}, bf16[4,2,24,768]{3,2,1,0:T(8,128)(2,1)S(1)}, u32[]{:S(2)}, u32[]{:S(2)}) collective-permute-start(bf16[4,2,24,768]{3,2,1,0:T(8,128)(2,1)} %get-tuple-element.56), channel_id=1, source_target_pairs={{0,32},{4,36},{8,40},{12,44},{16,48},{20,52},{24,56},{28,60},{32,6... | collective-permute-start | bytes 884744 | tf_op jit(solution)/shard_map/ppermute | solution.py:46
  52.5 19.6 %collective-permute-start.14 = (bf16[4,2,24,768]{3,2,0,1:T(8,128)(2,1)S(1)}, bf16[4,2,24,768]{3,2,0,1:T(8,128)(2,1)S(1)}, u32[]{:S(2)}, u32[]{:S(2)}) collective-permute-start(bf16[4,2,24,768]{3,2,0,1:T(8,128)(2,1)S(1)} %pad_maximum_fusion.7), channel_id=1, source_target_pairs={{0,96},{4,100},{8,104},{12,108},{16,112},{20,116},{24,120},{28,124... | collective-permute-start | bytes 884744 | tf_op jit(solution)/shard_map/ppermute | solution.py:46
  55.0 17.9 %collective-permute-start.13 = (bf16[4,2,24,768]{3,2,0,1:T(8,128)(2,1)S(1)}, bf16[4,2,24,768]{3,2,0,1:T(8,128)(2,1)S(1)}, u32[]{:S(2)}, u32[]{:S(2)}) collective-permute-start(bf16[4,2,24,768]{3,2,0,1:T(8,128)(2,1)S(1)} %pad_maximum_fusion.6), channel_id=1, source_target_pairs={{0,64},{4,68},{8,72},{12,76},{16,80},{20,84},{24,88},{28,92},{32,9... | collective-permute-start | bytes 884744 | tf_op jit(solution)/shard_map/ppermute | solution.py:46
  60.1 72.3 %copy-start.1 = (bf16[32,24,768]{2,1,0:T(8,128)(2,1)}, bf16[32,24,768]{2,1,0:T(8,128)(2,1)S(1)}, u32[]{:S(2)}) copy-start(bf16[32,24,768]{2,1,0:T(8,128)(2,1)S(1)} %all-to-all-done.2) | copy-start | bytes 3538948
  60.1 5.0 %copy-start.12 = (bf16[1,2,24,768]{3,2,0,1:T(8,128)(2,1)S(1)}, bf16[1,2,24,768]{3,2,0,1:T(8,128)(2,1)}, u32[]{:S(2)}) copy-start(bf16[1,2,24,768]{3,2,0,1:T(8,128)(2,1)} %get-tuple-element.51) | copy-start | bytes 221188
  60.1 77.0 %all-to-all-start = ((bf16[32,64,1024]{2,1,0:T(8,128)(2,1)}), bf16[32,64,1024]{2,1,0:T(8,128)(2,1)}, u32[]{:S(2)}, u32[]{:S(2)}) async-start(bf16[32,64,1024]{2,1,0:T(8,128)(2,1)} %get-tuple-element.27), calls=%async_computation | async-start | bytes 8388608 | tf_op jit(solution)/shard_map/all_to_all | solution.py:38
  65.1 3.7 %copy-start.11 = (bf16[1,2,24,768]{3,2,1,0:T(8,128)(2,1)S(1)}, bf16[1,2,24,768]{3,2,1,0:T(8,128)(2,1)}, u32[]{:S(2)}) copy-start(bf16[1,2,24,768]{3,2,1,0:T(8,128)(2,1)} %get-tuple-element.53) | copy-start | bytes 221188
  65.1 6.3 %copy-start.10 = (bf16[1,2,24,768]{3,2,1,0:T(8,128)(2,1)S(1)}, bf16[1,2,24,768]{3,2,1,0:T(8,128)(2,1)}, u32[]{:S(2)}) copy-start(bf16[1,2,24,768]{3,2,1,0:T(8,128)(2,1)} %get-tuple-element.54) | copy-start | bytes 221188
  65.1 6.9 %copy-start.9 = (bf16[1,2,24,768]{3,2,1,0:T(8,128)(2,1)S(1)}, bf16[1,2,24,768]{3,2,1,0:T(8,128)(2,1)}, u32[]{:S(2)}) copy-start(bf16[1,2,24,768]{3,2,1,0:T(8,128)(2,1)} %get-tuple-element.55) | copy-start | bytes 221188
  65.2 57.1 %collective-permute-start.12 = (bf16[4,2,24,768]{3,2,0,1:T(8,128)(2,1)S(1)}, bf16[4,2,24,768]{3,2,0,1:T(8,128)(2,1)S(1)}, u32[]{:S(2)}, u32[]{:S(2)}) collective-permute-start(bf16[4,2,24,768]{3,2,0,1:T(8,128)(2,1)S(1)} %pad_maximum_fusion.5), channel_id=1, source_target_pairs={{0,32},{4,36},{8,40},{12,44},{16,48},{20,52},{24,56},{28,60},{32,6... | collective-permute-start | bytes 884744 | tf_op jit(solution)/shard_map/ppermute | solution.py:46
  67.7 5.1 %copy-start.8 = (bf16[1,2,24,768]{3,2,0,1:T(8,128)(2,1)S(1)}, bf16[1,2,24,768]{3,2,0,1:T(8,128)(2,1)}, u32[]{:S(2)}) copy-start(bf16[1,2,24,768]{3,2,0,1:T(8,128)(2,1)} %get-tuple-element.52) | copy-start | bytes 221188
  68.7 4.1 %copy-start.7 = (bf16[1,2,24,768]{3,2,1,0:T(8,128)(2,1)S(1)}, bf16[1,2,24,768]{3,2,1,0:T(8,128)(2,1)}, u32[]{:S(2)}) copy-start(bf16[1,2,24,768]{3,2,1,0:T(8,128)(2,1)} %get-tuple-element.48) | copy-start | bytes 221188
  68.8 53.4 %collective-permute-start.8 = (bf16[4,2,24,768]{3,2,1,0:T(8,128)(2,1)S(1)}, bf16[4,2,24,768]{3,2,1,0:T(8,128)(2,1)S(1)}, u32[]{:S(2)}, u32[]{:S(2)}) collective-permute-start(bf16[4,2,24,768]{3,2,1,0:T(8,128)(2,1)S(1)} %pad_maximum_fusion.4), channel_id=1, source_target_pairs={{0,24},{4,28},{8,0},{12,4},{16,8},{20,12},{24,16},{28,20},{32,56},... | collective-permute-start | bytes 884744 | tf_op jit(solution)/shard_map/ppermute | solution.py:50
  71.4 51.1 %collective-permute-start.7 = (bf16[4,2,24,768]{3,2,1,0:T(8,128)(2,1)S(1)}, bf16[4,2,24,768]{3,2,1,0:T(8,128)(2,1)S(1)}, u32[]{:S(2)}, u32[]{:S(2)}) collective-permute-start(bf16[4,2,24,768]{3,2,1,0:T(8,128)(2,1)S(1)} %pad_maximum_fusion.3), channel_id=1, source_target_pairs={{0,16},{4,20},{8,24},{12,28},{16,0},{20,4},{24,8},{28,12},{32,48},... | collective-permute-start | bytes 884744 | tf_op jit(solution)/shard_map/ppermute | solution.py:50
  72.1 54.7 %collective-permute-start.6 = (bf16[4,2,24,768]{3,2,1,0:T(8,128)(2,1)S(1)}, bf16[4,2,24,768]{3,2,1,0:T(8,128)(2,1)S(1)}, u32[]{:S(2)}, u32[]{:S(2)}) collective-permute-start(bf16[4,2,24,768]{3,2,1,0:T(8,128)(2,1)S(1)} %pad_maximum_fusion.2), channel_id=1, source_target_pairs={{0,8},{4,12},{8,16},{12,20},{16,24},{20,28},{24,0},{28,4},{32,40},... | collective-permute-start | bytes 884744 | tf_op jit(solution)/shard_map/ppermute | solution.py:50
  127.2 6.3 %collective-permute-start.15 = (bf16[4,4,24,1536]{3,2,1,0:T(8,128)(2,1)S(1)}, bf16[4,4,24,1536]{3,2,1,0:T(8,128)(2,1)}, u32[]{:S(2)}, u32[]{:S(2)}) collective-permute-start(bf16[4,4,24,1536]{3,2,1,0:T(8,128)(2,1)S(1)} %get-tuple-element.47), channel_id=1, source_target_pairs={{0,4},{4,0},{8,12},{12,8},{16,20},{20,16},{24,28},{28,24},{32,36},... | collective-permute-start | bytes 3538952 | tf_op jit(solution)/shard_map/ppermute | solution.py:54
  128.7 28.8 %collective-permute-start = (bf16[768,768]{1,0:T(8,128)(2,1)S(1)}, bf16[768,768]{1,0:T(8,128)(2,1)}, u32[]{:S(2)}, u32[]{:S(2)}) collective-permute-start(bf16[768,768]{1,0:T(8,128)(2,1)S(1)} %bitcast.77), channel_id=1, source_target_pairs={{0,1},{1,2},{2,3},{3,0},{4,5},{5,6},{6,7},{7,4},{8,9},{9,10},{10,1... | collective-permute-start | bytes 3538952 | tf_op jit(solution)/shard_map/ppermute | solution.py:42
  129.9 53.9 %collective-permute-start.1 = (bf16[768,768]{1,0:T(8,128)(2,1)S(1)}, bf16[768,768]{1,0:T(8,128)(2,1)}, u32[]{:S(2)}, u32[]{:S(2)}) collective-permute-start(bf16[768,768]{1,0:T(8,128)(2,1)S(1)} %bitcast.78), channel_id=1, source_target_pairs={{0,2},{1,3},{2,0},{3,1},{4,6},{5,7},{6,4},{7,5},{8,10},{9,11},{10,... | collective-permute-start | bytes 3538952 | tf_op jit(solution)/shard_map/ppermute | solution.py:42
  132.3 51.4 %collective-permute-start.2 = (bf16[768,768]{1,0:T(8,128)(2,1)S(1)}, bf16[768,768]{1,0:T(8,128)(2,1)}, u32[]{:S(2)}, u32[]{:S(2)}) collective-permute-start(bf16[768,768]{1,0:T(8,128)(2,1)S(1)} %bitcast.79), channel_id=1, source_target_pairs={{0,3},{1,0},{2,1},{3,2},{4,7},{5,4},{6,5},{7,6},{8,11},{9,8},{10,9... | collective-permute-start | bytes 3538952 | tf_op jit(solution)/shard_map/ppermute | solution.py:42
  135.7 1.4 copy-start
  137.1 69.0 %all-to-all-start.4 = ((bf16[32,24,1536]{2,1,0:T(8,128)(2,1)}), bf16[32,24,1536]{2,1,0:T(8,128)(2,1)S(1)}, u32[]{:S(2)}, u32[]{:S(2)}) async-start(bf16[32,24,1536]{2,1,0:T(8,128)(2,1)} %copy-done), calls=%async_computation.4 | async-start | bytes 4718592 | tf_op jit(solution)/shard_map/all_to_all | solution.py:38
  206.1 58.5 %all-to-all-start.3 = ((bf16[32,64,1024]{2,1,0:T(8,128)(2,1)}), bf16[32,64,1024]{2,1,0:T(8,128)(2,1)}, u32[]{:S(2)}, u32[]{:S(2)}) async-start(bf16[32,64,1024]{2,1,0:T(8,128)(2,1)} %get-tuple-element.28), calls=%async_computation.3 | async-start | bytes 8388608 | tf_op jit(solution)/shard_map/all_to_all | solution.py:38
  213.9 18.2 %copy-start.6 = (bf16[384,768]{1,0:T(8,128)(2,1)S(1)}, bf16[384,768]{1,0:T(8,128)(2,1)}, u32[]{:S(2)}) copy-start(bf16[384,768]{1,0:T(8,128)(2,1)} %get-tuple-element.38) | copy-start | bytes 1769476
  213.9 16.2 %collective-permute-start.16 = (bf16[384,768]{1,0:T(8,128)(2,1)}, bf16[384,768]{1,0:T(8,128)(2,1)S(1)}, u32[]{:S(2)}, u32[]{:S(2)}) collective-permute-start(bf16[384,768]{1,0:T(8,128)(2,1)} %get-tuple-element.35), channel_id=1, source_target_pairs={{0,1},{1,2},{2,3},{3,0},{4,5},{5,6},{6,7},{7,4},{8,9},{9,10},{10,1... | collective-permute-start | bytes 1769480 | tf_op jit(solution)/shard_map/ppermute | solution.py:42
  215.0 17.1 %collective-permute-start.20 = (bf16[384,768]{1,0:T(8,128)(2,1)}, bf16[384,768]{1,0:T(8,128)(2,1)S(1)}, u32[]{:S(2)}, u32[]{:S(2)}) collective-permute-start(bf16[384,768]{1,0:T(8,128)(2,1)} %get-tuple-element.39), channel_id=1, source_target_pairs={{0,3},{1,0},{2,1},{3,2},{4,7},{5,4},{6,5},{7,6},{8,11},{9,8},{10,9... | collective-permute-start | bytes 1769480 | tf_op jit(solution)/shard_map/ppermute | solution.py:42
  216.7 26.1 %collective-permute-start.18 = (bf16[384,768]{1,0:T(8,128)(2,1)}, bf16[384,768]{1,0:T(8,128)(2,1)S(1)}, u32[]{:S(2)}, u32[]{:S(2)}) collective-permute-start(bf16[384,768]{1,0:T(8,128)(2,1)} %get-tuple-element.36), channel_id=1, source_target_pairs={{0,1},{1,2},{2,3},{3,0},{4,5},{5,6},{6,7},{7,4},{8,9},{9,10},{10,1... | collective-permute-start | bytes 1769480 | tf_op jit(solution)/shard_map/ppermute | solution.py:42
  216.7 26.1 %collective-permute-start.19 = (bf16[384,768]{1,0:T(8,128)(2,1)}, bf16[384,768]{1,0:T(8,128)(2,1)S(1)}, u32[]{:S(2)}, u32[]{:S(2)}) collective-permute-start(bf16[384,768]{1,0:T(8,128)(2,1)} %get-tuple-element.37), channel_id=1, source_target_pairs={{0,3},{1,0},{2,1},{3,2},{4,7},{5,4},{6,5},{7,6},{8,11},{9,8},{10,9... | collective-permute-start | bytes 1769480 | tf_op jit(solution)/shard_map/ppermute | solution.py:42
  232.1 23.3 %collective-permute-start.17 = (bf16[384,768]{1,0:T(8,128)(2,1)}, bf16[384,768]{1,0:T(8,128)(2,1)}, u32[]{:S(2)}, u32[]{:S(2)}) collective-permute-start(bf16[384,768]{1,0:T(8,128)(2,1)} %add_convert_fusion.1), channel_id=1, source_target_pairs={{0,1},{1,2},{2,3},{3,0},{4,5},{5,6},{6,7},{7,4},{8,9},{9,10},{10,1... | collective-permute-start | bytes 1769480 | tf_op jit(solution)/shard_map/ppermute | solution.py:42
  233.1 22.3 %collective-permute-start.21 = (bf16[384,768]{1,0:T(8,128)(2,1)}, bf16[384,768]{1,0:T(8,128)(2,1)}, u32[]{:S(2)}, u32[]{:S(2)}) collective-permute-start(bf16[384,768]{1,0:T(8,128)(2,1)} %add_convert_fusion), channel_id=1, source_target_pairs={{0,3},{1,0},{2,1},{3,2},{4,7},{5,4},{6,5},{7,6},{8,11},{9,8},{10,9... | collective-permute-start | bytes 1769480 | tf_op jit(solution)/shard_map/ppermute | solution.py:42
  239.0 16.4 %copy-start.2 = (bf16[32,24,768]{2,1,0:T(8,128)(2,1)S(1)}, bf16[32,24,768]{2,1,0:T(8,128)(2,1)}, u32[]{:S(2)}) copy-start(bf16[32,24,768]{2,1,0:T(8,128)(2,1)} %copy-done.1) | copy-start | bytes 3538948
  239.0 16.3 %copy-start.3 = (bf16[768,768]{1,0:T(8,128)(2,1)S(1)}, bf16[768,768]{1,0:T(8,128)(2,1)}, u32[]{:S(2)}) copy-start(bf16[768,768]{1,0:T(8,128)(2,1)} %get-tuple-element.33.g0) | copy-start | bytes 3538948
